TPU v7x, 128 devices: a whole 4x4x4 slice. The times are simulated.
128 devices in a mesh: stage: 2 (over core), data: 64 (over z, y, x).
Axes of the slice: x: 4, y: 4, z: 4, core: 2. Of those that a mesh axis runs over, the one named last changes fastest.
Arguments:
- x_in: bfloat16 [16, 2048, 768], P(None, 'data')
- targets: bfloat16 [16, 2048, 768], P(None, 'data')
- w1_bf: bfloat16 [2, 2, 1, 768, 3072], P('stage')
- w2_bf: bfloat16 [2, 2, 1, 3072, 768], P('stage')
- w_master: float32 [2, 2, 1, 4718592], P('stage', None, None, 'data')
- m_state: float32 [2, 2, 1, 4718592], P('stage', None, None, 'data')
- v_state: float32 [2, 2, 1, 4718592], P('stage', None, None, 'data')
Outputs:
- output 1: bfloat16 [2, 2, 1, 768, 3072], P('stage')
- output 2: bfloat16 [2, 2, 1, 3072, 768], P('stage')
- output 3: float32 [2, 2, 1, 4718592], P('stage', None, None, 'data')
- output 4: float32 [2, 2, 1, 4718592], P('stage', None, None, 'data')
- output 5: float32 [2, 2, 1, 4718592], P('stage', None, None, 'data')
- output 6: float32 [], replicated
All inputs are finite; a program needn't handle non-finite values.
Results may differ from a plain program's by a relative error of at most 0.001.
Values are sent between devices in bfloat16 or wider.
A program may use at most 1 GiB of HBM per device.

v0:
```python
import math
import jax
import jax.numpy as jnp
from jax import lax
from jax.sharding import PartitionSpec as P

BETA_ONE = 0.9
BETA_TWO = 0.999
ADAM_EPS = 1e-8
WEIGHT_DECAY = 0.1
ADAM_STEP = 1000


def gelu_tanh(pre_act):
    return jax.nn.gelu(pre_act, approximate=True)


def block_forward(h_in, w_one, w_two):
    pre_act = jnp.dot(h_in, w_one, preferred_element_type=jnp.float32)
    act_bf = gelu_tanh(pre_act).astype(jnp.bfloat16)
    out_val = h_in.astype(jnp.float32) + jnp.dot(act_bf, w_two, preferred_element_type=jnp.float32)
    return out_val.astype(jnp.bfloat16)


def block_backward(h_in, grad_out, w_one, w_two):
    pre_act = jnp.dot(h_in, w_one, preferred_element_type=jnp.float32)
    act_val, gelu_pull = jax.vjp(gelu_tanh, pre_act)
    grad_act = jnp.einsum("td,fd->tf", grad_out, w_two, preferred_element_type=jnp.float32)
    grad_pre = gelu_pull(grad_act)[0].astype(jnp.bfloat16)
    back_val = jnp.einsum("tf,df->td", grad_pre, w_one, preferred_element_type=jnp.float32)
    grad_in = (grad_out.astype(jnp.float32) + back_val).astype(jnp.bfloat16)
    grad_one = jnp.einsum("td,tf->df", h_in, grad_pre, preferred_element_type=jnp.float32)
    grad_two = jnp.einsum("tf,td->fd", act_val.astype(jnp.bfloat16), grad_out, preferred_element_type=jnp.float32)
    return grad_in, grad_one, grad_two


def adam_update(w_old, m_old, v_old, grad_val, clip_factor, learn_rate):
    grad_clip = clip_factor * grad_val
    m_new = BETA_ONE * m_old + (1.0 - BETA_ONE) * grad_clip
    v_new = BETA_TWO * v_old + (1.0 - BETA_TWO) * grad_clip * grad_clip
    m_hat = m_new / (1.0 - BETA_ONE ** ADAM_STEP)
    v_hat = v_new / (1.0 - BETA_TWO ** ADAM_STEP)
    w_new = w_old - learn_rate * (m_hat / (jnp.sqrt(v_hat) + ADAM_EPS) + WEIGHT_DECAY * w_old)
    return w_new, m_new, v_new


def item_coords(item_idx, n_stage, backward):
    group_idx = item_idx // (2 * n_stage)
    within = item_idx % (2 * n_stage)
    half_idx = within // n_stage
    if backward:
        half_idx = 1 - half_idx
    return half_idx, group_idx * n_stage + within % n_stage


def run_stack(x_loc, t_loc, w_ones, w_twos, n_stage, n_tokens):
    stage_idx = lax.axis_index("stage")
    n_micro, n_tok, d_model = x_loc.shape
    n_blk, d_ff = w_ones.shape[1], w_ones.shape[3]
    n_items = 2 * n_micro
    n_ticks = n_items + n_stage - 1
    fwd_perm = [(src, (src + 1) % n_stage) for src in range(n_stage)]
    bwd_perm = [(src, (src - 1) % n_stage) for src in range(n_stage)]

    def fwd_tick(tick_idx, state_carry):
        recv_act, saved_in, seed_buf, loss_acc = state_carry
        item_idx = tick_idx - stage_idx
        active = (item_idx >= 0) & (item_idx < n_items)
        half_idx, micro_idx = item_coords(jnp.clip(item_idx, 0, n_items - 1), n_stage, False)
        slot_idx = jnp.where(active, micro_idx, n_micro)
        x_mb = lax.dynamic_index_in_dim(x_loc, micro_idx, 0, keepdims=False)
        h_cur = jnp.where((half_idx == 0) & (stage_idx == 0), x_mb, recv_act)
        half_one = lax.dynamic_index_in_dim(w_ones, half_idx, 0, keepdims=False)
        half_two = lax.dynamic_index_in_dim(w_twos, half_idx, 0, keepdims=False)
        for block_idx in range(n_blk):
            saved_in = lax.dynamic_update_slice(saved_in, h_cur[None, None, None], (half_idx, slot_idx, block_idx, 0, 0))
            h_cur = block_forward(h_cur, half_one[block_idx], half_two[block_idx])
        is_last = active & (half_idx == 1) & (stage_idx == n_stage - 1)
        t_mb = lax.dynamic_index_in_dim(t_loc, micro_idx, 0, keepdims=False)
        residual = h_cur.astype(jnp.float32) - t_mb.astype(jnp.float32)
        loss_acc = loss_acc + jnp.where(is_last, 0.5 * jnp.sum(residual * residual), 0.0)
        seed_slot = jnp.where(is_last, micro_idx, n_micro)
        seed_buf = lax.dynamic_update_slice(seed_buf, (residual / n_tokens).astype(jnp.bfloat16)[None], (seed_slot, 0, 0))
        recv_act = lax.ppermute(h_cur, "stage", fwd_perm)
        return recv_act, saved_in, seed_buf, loss_acc

    fwd_start = (jnp.zeros((n_tok, d_model), jnp.bfloat16), jnp.zeros((2, n_micro + 1, n_blk, n_tok, d_model), jnp.bfloat16), jnp.zeros((n_micro + 1, n_tok, d_model), jnp.bfloat16), jnp.zeros((), jnp.float32))
    fwd_out = lax.fori_loop(0, n_ticks, fwd_tick, fwd_start)
    saved_in, seed_buf, loss_acc = fwd_out[1], fwd_out[2], fwd_out[3]

    def bwd_tick(tick_idx, state_carry):
        recv_grad, acc_one, acc_two = state_carry
        item_idx = tick_idx - (n_stage - 1 - stage_idx)
        active = (item_idx >= 0) & (item_idx < n_items)
        half_idx, micro_idx = item_coords(jnp.clip(item_idx, 0, n_items - 1), n_stage, True)
        seed_mb = lax.dynamic_index_in_dim(seed_buf, micro_idx, 0, keepdims=False)
        is_seed = (half_idx == 1) & (stage_idx == n_stage - 1)
        grad_cur = jnp.where(is_seed, seed_mb, recv_grad)
        grad_cur = jnp.where(active, grad_cur, jnp.zeros_like(grad_cur))
        half_one = lax.dynamic_index_in_dim(w_ones, half_idx, 0, keepdims=False)
        half_two = lax.dynamic_index_in_dim(w_twos, half_idx, 0, keepdims=False)
        saved_mb = lax.dynamic_slice(saved_in, (half_idx, micro_idx, 0, 0, 0), (1, 1, n_blk, n_tok, d_model))[0, 0]
        for block_idx in reversed(range(n_blk)):
            grad_cur, grad_one, grad_two = block_backward(saved_mb[block_idx], grad_cur, half_one[block_idx], half_two[block_idx])
            old_one = lax.dynamic_slice(acc_one, (half_idx, block_idx, 0, 0), (1, 1, d_model, d_ff))
            acc_one = lax.dynamic_update_slice(acc_one, old_one + grad_one[None, None], (half_idx, block_idx, 0, 0))
            old_two = lax.dynamic_slice(acc_two, (half_idx, block_idx, 0, 0), (1, 1, d_ff, d_model))
            acc_two = lax.dynamic_update_slice(acc_two, old_two + grad_two[None, None], (half_idx, block_idx, 0, 0))
        recv_grad = lax.ppermute(grad_cur, "stage", bwd_perm)
        return recv_grad, acc_one, acc_two

    bwd_start = (jnp.zeros((n_tok, d_model), jnp.bfloat16), jnp.zeros((2, n_blk, d_model, d_ff), jnp.float32), jnp.zeros((2, n_blk, d_ff, d_model), jnp.float32))
    bwd_out = lax.fori_loop(0, n_ticks, bwd_tick, bwd_start)
    return bwd_out[1], bwd_out[2], loss_acc


def solution(mesh):
    n_stage = mesh.shape["stage"]
    n_data = mesh.shape["data"]

    def device_step(x_loc, t_loc, w1_loc, w2_loc, wm_loc, m_loc, v_loc):
        n_micro, n_tok, d_model = x_loc.shape
        n_blk, d_ff = w1_loc.shape[2], w1_loc.shape[4]
        n_tokens = n_micro * n_tok * n_data
        n_blocks = 2 * n_stage * n_blk
        tau_clip = 0.3 * d_model * math.sqrt(n_blocks * (3.0 / n_tokens + 0.008))
        learn_rate = 0.1 / math.sqrt(4.0 * d_model * n_blocks)
        acc_one, acc_two, loss_acc = run_stack(x_loc, t_loc, w1_loc[0], w2_loc[0], n_stage, n_tokens)
        grad_flat = jnp.concatenate([acc_one.reshape(2, n_blk, -1), acc_two.reshape(2, n_blk, -1)], axis=-1)
        grad_shard = lax.psum_scatter(grad_flat, "data", scatter_dimension=2, tiled=True)
        grad_norm = jnp.sqrt(lax.psum(jnp.sum(grad_shard * grad_shard), ("stage", "data")))
        clip_factor = jnp.minimum(1.0, tau_clip / grad_norm)
        w_new, m_new, v_new = adam_update(wm_loc[0], m_loc[0], v_loc[0], grad_shard, clip_factor, learn_rate)
        w_full = lax.all_gather(w_new.astype(jnp.bfloat16), "data", axis=2, tiled=True)
        split_at = d_model * d_ff
        w1_new = w_full[:, :, :split_at].reshape(1, 2, n_blk, d_model, d_ff)
        w2_new = w_full[:, :, split_at:].reshape(1, 2, n_blk, d_ff, d_model)
        mean_loss = lax.psum(loss_acc, ("stage", "data")) / n_tokens
        return w1_new, w2_new, w_new[None], m_new[None], v_new[None], mean_loss

    act_spec = P(None, "data", None)
    flat_spec = P("stage", None, None, "data")
    return jax.shard_map(device_step, mesh=mesh, in_specs=(act_spec, act_spec, P("stage"), P("stage"), flat_spec, flat_spec, flat_spec), out_specs=(P("stage"), P("stage"), flat_spec, flat_spec, flat_spec, P()), check_vma=False)
```

profile of v0, /device:TPU:0, one launch (start us, length us, event | category | flops | bytes accessed | tf_op | source)
XLA Modules:
  0.0 2157.0 jit_solution(11395322389622436179)
XLA Ops:
  7.5 295.6 %while.42 = (s32[]{:T(128)}, bf16[32,768]{1,0:T(8,128)(2,1)S(1)}, bf16[2,17,1,32,768]{4,3,2,1,0:T(8,128)(2,1)S(1)}, bf16[17,32,768]{2,1,0:T(8,128)(2,1)S(1)}, f3...) while((s32[]{:T(128)}, bf16[32,768]{1,0:T(8,128)(2,1)S(1)}, ...), condition=%wide.region_2.3_spmd, body=%wide.region_0.2_spmd.sunk | while | flops 303267904 | bytes 10326387 | solution.py:88
  303.1 8.9 broadcast_in_dim.65
  319.7 901.2 %while.43 = (s32[]{:T(128)}, bf16[32,768]{1,0:T(8,128)(2,1)S(1)}, f32[2,1,768,3072]{3,2,1,0:T(8,128)}, f32[2,1,3072,768]{3,2,1,0:T(8,128)}, s32[]{:T(128)}, /*in...) while((s32[]{:T(128)}, bf16[32,768]{1,0:T(8,128)(2,1)S(1)}, ...), condition=%wide.region_4.5_spmd, body=%wide.region_3.4_spmd.sunk | while | flops 762667072 | bytes 92065504 | solution.py:113
  329.6 8.8 fusion.125
  356.6 8.8 fusion.125
  365.4 8.7 fusion.124
  384.1 8.8 fusion.125
  392.8 8.7 fusion.124
  411.3 8.9 fusion.125
  438.7 8.9 fusion.125
  465.9 8.8 fusion.125
  474.6 8.7 fusion.124
  493.3 8.8 fusion.125
  520.5 8.9 fusion.125
  547.9 8.9 fusion.125
  575.1 8.8 fusion.125
  602.5 8.8 fusion.125
  611.3 8.7 fusion.124
  629.7 8.9 fusion.125
  657.1 8.9 fusion.125
  684.3 8.8 fusion.125
  711.8 8.8 fusion.125
  738.9 8.9 fusion.125
  766.4 8.9 fusion.125
  793.5 8.8 fusion.125
  821.0 8.8 fusion.125
  848.1 8.9 fusion.125
  875.6 8.9 fusion.125
  902.8 8.8 fusion.125
  930.2 8.8 fusion.125
  957.4 8.9 fusion.125
  984.8 8.9 fusion.125
  1012.0 8.8 fusion.125
  1039.4 8.8 fusion.125
  1066.6 8.9 fusion.125
  1094.0 8.9 fusion.125
  1121.2 8.8 fusion.125
  1148.6 8.8 fusion.125
  1175.8 8.9 fusion.125
  1203.2 8.9 fusion.125
  1220.9 40.6 %reshape.70 = f32[2,1,2359296]{2,1,0:T(1,128)} reshape(f32[2,1,768,3072]{3,2,1,0:T(8,128)} %get-tuple-element.591) | data formatting | bytes 37748736 | tf_op jit(solution)/shard_map/reshape | solution.py:129
  1261.5 37.3 %reshape.71 = f32[2,1,2359296]{2,1,0:T(1,128)} reshape(f32[2,1,3072,768]{3,2,1,0:T(8,128)} %get-tuple-element.592) | data formatting | bytes 37748736 | tf_op jit(solution)/shard_map/reshape | solution.py:129
  1298.8 101.8 %pad_maximum_fusion = f32[2,1,4718592]{2,1,0:T(1,128)} fusion(f32[2,1,2359296]{2,1,0:T(1,128)} %reshape.71, f32[2,1,2359296]{2,1,0:T(1,128)} %reshape.70), kind=kLoop, calls=%fused_computation.76 | loop fusion | flops 9437184 | bytes 75497472 | tf_op jit(solution)/shard_map/concatenate | solution.py:129
  1402.5 358.2 %all-reduce.4.cloned.1.call-done = f32[2,1,4718592]{2,1,0:T(1,128)} async-done(((f32[2,1,4718592]{2,1,0:T(1,128)}), f32[2,1,4718592]{2,1,0:T(1,128)}) %all-reduce.4.cloned.1.call-update) | async-done | bytes 37748752
  1763.5 64.7 %all-reduce.1 = (f32[]{:T(128)}, f32[]{:T(128)}) all-reduce(f32[]{:T(128)} %multiply_reduce_fusion.1, f32[]{:T(128)} %get-tuple-element.593), channel_id=1, replica_groups=mesh['stage'=2,'data'=64] {'stage','data'}, use_global_device_ids=true, to_apply=%region_7.8 | all-reduce | flops 2 | bytes 16 | tf_op jit(solution)/shard_map/psum | solution.py:131
  1835.8 170.4 %all-gather.2.cloned.1.call-done = bf16[2,1,4718592]{2,1,0:T(2,128)(2,1)} async-done(((bf16[2,1,73728]{2,1,0:T(2,128)(2,1)}), bf16[2,1,4718592]{2,1,0:T(2,128)(2,1)}) %all-gather.2.cloned.1.call-update) | async-done | bytes 18874384 | tf_op jit(solution)/shard_map/all_gather | solution.py:134
  2006.2 123.5 %slice_reduce_fusion = (bf16[2,2359296]{1,0:T(2,128)(2,1)}, bf16[2,2359296]{1,0:T(2,128)(2,1)}) fusion(bf16[2,1,4718592]{2,1,0:T(2,128)(2,1)} %all-gather.2.cloned.1.call-done), kind=kLoop, calls=%fused_computation.77 | loop fusion | bytes 37748736 | tf_op jit(solution)/shard_map/slice | solution.py:137
  2138.3 10.3 copy.22
  (512 shorter events, 870.7 us)
Async XLA Ops:
  7.2 1753.5 %all-reduce.4.cloned.1.call-start = ((), (), s32[]{:S(2)}) async-start(), calls=%async_computation.1 | async-start | bytes 75497472
  21.9 3.5 collective-permute-start
  39.8 3.5 collective-permute-start
  57.8 3.5 collective-permute-start
  75.7 3.5 collective-permute-start
  93.6 3.5 collective-permute-start
  111.5 3.5 collective-permute-start
  129.5 3.5 collective-permute-start
  147.4 3.5 collective-permute-start
  165.3 3.5 collective-permute-start
  219.1 3.5 collective-permute-start
  237.0 3.5 collective-permute-start
  255.0 3.5 collective-permute-start
  272.9 3.5 collective-permute-start
  329.1 18.0 collective-permute-start.1
  356.5 17.6 collective-permute-start.1
  383.5 18.0 collective-permute-start.1
  411.0 17.9 collective-permute-start.1
  438.3 18.0 collective-permute-start.1
  465.7 17.6 collective-permute-start.1
  492.8 18.0 collective-permute-start.1
  520.2 17.9 collective-permute-start.1
  547.5 18.0 collective-permute-start.1
  575.0 17.6 collective-permute-start.1
  602.0 18.0 collective-permute-start.1
  629.4 17.9 collective-permute-start.1
  656.7 18.0 collective-permute-start.1
  684.2 17.6 collective-permute-start.1
  711.2 18.0 collective-permute-start.1
  738.7 17.9 collective-permute-start.1
  766.0 18.0 collective-permute-start.1
  793.4 17.6 collective-permute-start.1
  820.4 18.0 collective-permute-start.1
  847.9 17.9 collective-permute-start.1
  875.2 18.0 collective-permute-start.1
  902.6 17.6 collective-permute-start.1
  929.6 18.0 collective-permute-start.1
  957.1 17.9 collective-permute-start.1
  984.4 18.0 collective-permute-start.1
  1011.8 17.6 collective-permute-start.1
  1038.9 18.0 collective-permute-start.1
  1066.3 17.9 collective-permute-start.1
  1093.6 18.0 collective-permute-start.1
  1121.1 17.6 collective-permute-start.1
  1148.1 18.0 collective-permute-start.1
  1175.5 17.9 collective-permute-start.1
  1202.8 18.0 collective-permute-start.1
  1400.7 605.5 %all-gather.2.cloned.1.call-start = ((), (), s32[]{:S(2)}) async-start(), calls=%async_computation | async-start | bytes 38338560 | tf_op jit(solution)/shard_map/all_gather | solution.py:134
  (57 other events, 1609.3 us)
Sparse Core Ops, SparseCore 0:
  1400.8 359.8 all-reduce.3
  1835.3 170.8 all-gather.1
where the time goes:
time: 2170 us; the launch traced here: 2160 us
  matrix products  1070 us (49%)
  waiting for transfers between devices  529 us (24%)
  local copies, waits for them, and re-layouts  239 us (11%)
  other arithmetic  188 us (9%)
  blocking collectives  64.7 us (3%)
  loops' own time  26.4 us (1%)
  starting transfers between devices  22.1 us (1%)
    unnamed x3, waiting for transfers between devices  358 us
    dot_general x33, matrix products, block_backward(): jnp.einsum('tf,td->fd', act_val.astype(jnp.bfloat16), grad_out, preferred...  292 us
    dot_general x33, matrix products, block_backward(): jnp.einsum('td,tf->df', h_in, grad_pre, preferred_element_type=jnp.float32)  288 us
    dot_general x33, matrix products, block_forward(): jnp.dot(act_bf, w_two, preferred_element_type=jnp.float32)  183 us
    all_gather x1, waiting for transfers between devices, device_step(): lax.all_gather(w_new.astype(jnp.bfloat16), 'data', axis=2, tiled=True)  170 us
    dot_general x33, matrix products, block_backward(): jnp.einsum('td,fd->tf', grad_out, w_two, preferred_element_type=jnp.float32)  148 us
    slice x1, local copies, waits for them, and re-layouts, device_step(): w2_new = w_full[:, :, split_at:].reshape(1, 2, n_blk, d_ff, d_model)  123 us
    dot_general x33, matrix products, block_backward(): pre_act = jnp.dot(h_in, w_one, preferred_element_type=jnp.float32)  112 us
  transfers between devices with their start and end apart: 68, of which 2 were waited for; matrix products, arithmetic and copies ran while one was open for 30% of the time, Pallas kernels for 0%

commit v1 on v0

v1 whole, which is shorter than its diff:
```python
import math
import jax
import jax.numpy as jnp
from jax import lax
from jax.sharding import PartitionSpec as P

BETA_ONE = 0.9
BETA_TWO = 0.999
ADAM_EPS = 1e-8
WEIGHT_DECAY = 0.1
ADAM_STEP = 1000


def gelu_tanh(pre_act):
    return jax.nn.gelu(pre_act, approximate=True)


def dot32(lhs, rhs, dims):
    return lax.dot_general(lhs, rhs, (dims, ((), ())), preferred_element_type=jnp.float32)


def to_tiles(mat):
    rows, cols = mat.shape
    return mat.reshape(rows // 8, 8, cols // 128, 128).transpose(0, 2, 1, 3).reshape(-1, 8, 128)


def from_tiles(tiles, rows, cols):
    return tiles.reshape(rows // 8, cols // 128, 8, 128).transpose(0, 2, 1, 3).reshape(rows, cols)


def run_stack(x_all, t_all, w1_loc, w2_loc, n_tokens, n_chunk):
    stage_idx = lax.axis_index("stage")
    on_first = stage_idx == 0
    n_rows, d_model = x_all.shape
    n_tok = n_rows // n_chunk
    n_items = 2 * n_chunk
    n_ticks = n_items + 1
    swap = [(0, 1), (1, 0)]

    def weights(half_first, half_second):
        if half_first == half_second:
            return w1_loc[half_first], w2_loc[half_first]
        return (jnp.where(on_first, w1_loc[half_first], w1_loc[half_second]),
                jnp.where(on_first, w2_loc[half_first], w2_loc[half_second]))

    def half_of(item, backward):
        half = min(max(item, 0), n_items - 1) // n_chunk
        return 1 - half if backward else half

    x_in, pre_in, outs = [], [], []
    recv = None
    for tick in range(n_ticks):
        fresh = x_all[tick * n_tok:(tick + 1) * n_tok] if tick < n_chunk else None
        if recv is None:
            h_cur = fresh
        elif fresh is None:
            h_cur = recv
        else:
            h_cur = jnp.where(on_first, fresh, recv)
        w_one, w_two = weights(half_of(tick, False), half_of(tick - 1, False))
        pre = dot32(h_cur, w_one, ((1,), (0,)))
        act = gelu_tanh(pre).astype(jnp.bfloat16)
        h_out = (h_cur.astype(jnp.float32) + dot32(act, w_two, ((1,), (0,)))).astype(jnp.bfloat16)
        x_in.append(h_cur)
        outs.append(h_out)
        recv = lax.ppermute(h_out, "stage", swap)

    loss_acc = jnp.zeros((), jnp.float32)
    seeds = []
    for chunk in range(n_chunk):
        h_last = outs[n_chunk + chunk + 1]
        residual = h_last.astype(jnp.float32) - t_all[chunk * n_tok:(chunk + 1) * n_tok].astype(jnp.float32)
        loss_acc = loss_acc + 0.5 * jnp.sum(residual * residual)
        seeds.append((residual / n_tokens).astype(jnp.bfloat16))
    loss_acc = jnp.where(on_first, 0.0, loss_acc)

    g_in, r_in, a_in = [], [], []
    saved = []
    recv = None
    for tick in range(n_ticks):
        fresh = seeds[tick] if tick < n_chunk else None
        if recv is None:
            grad = fresh
        elif fresh is None:
            grad = recv
        else:
            grad = jnp.where(on_first, recv, fresh)
        first_item = min(max(tick - 1, 0), n_items - 1)
        second_item = min(tick, n_items - 1)
        w_one, w_two = weights(half_of(first_item, True), half_of(second_item, True))
        first_tick = half_of(first_item, True) * n_chunk + first_item % n_chunk
        second_tick = half_of(second_item, True) * n_chunk + second_item % n_chunk + 1
        if first_tick == second_tick:
            x_cur = x_in[first_tick]
        else:
            x_cur = jnp.where(on_first, x_in[first_tick], x_in[second_tick])
        pre = dot32(x_cur, w_one, ((1,), (0,)))
        act, pull = jax.vjp(gelu_tanh, pre)
        r_cur = pull(dot32(grad, w_two, ((1,), (1,))))[0].astype(jnp.bfloat16)
        back = (grad.astype(jnp.float32) + dot32(r_cur, w_one, ((1,), (1,)))).astype(jnp.bfloat16)
        g_in.append(grad)
        r_in.append(r_cur)
        a_in.append(act.astype(jnp.bfloat16))
        saved.append(x_cur)
        if tick < n_ticks - 1:
            recv = lax.ppermute(back, "stage", swap)

    def pick(per_tick, half):
        base = (1 - half) * n_chunk
        return jnp.concatenate([jnp.where(on_first, per_tick[base + c + 1], per_tick[base + c]) for c in range(n_chunk)], axis=0)

    grads = []
    for half in (1, 0):
        x_h, g_h, r_h, a_h = pick(saved, half), pick(g_in, half), pick(r_in, half), pick(a_in, half)
        grads.append((dot32(x_h, r_h, ((0,), (0,))), dot32(a_h, g_h, ((0,), (0,)))))
    return grads[1], grads[0], loss_acc


def solution(mesh):
    n_stage = mesh.shape["stage"]
    n_data = mesh.shape["data"]

    def device_step(x_loc, t_loc, w1_loc, w2_loc, wm_loc, m_loc, v_loc):
        n_micro, n_tok, d_model = x_loc.shape
        d_ff = w1_loc.shape[4]
        n_tokens = n_micro * n_tok * n_data
        n_blocks = 2 * n_stage
        tau_clip = 0.3 * d_model * math.sqrt(n_blocks * (3.0 / n_tokens + 0.008))
        learn_rate = 0.1 / math.sqrt(4.0 * d_model * n_blocks)
        first_kind = lax.axis_index("data") < n_data // 2
        x_all = x_loc.reshape(n_micro * n_tok, d_model)
        t_all = t_loc.reshape(n_micro * n_tok, d_model)
        grad_zero, grad_one, loss_acc = run_stack(x_all, t_all, w1_loc[0, :, 0], w2_loc[0, :, 0], n_tokens, 2)
        tiles = d_model * d_ff * 2 // n_data // 1024
        rows_one, rows_two = 2 * d_model // n_data, 2 * d_ff // n_data

        def scatter(pair):
            full = jnp.concatenate([to_tiles(pair[0]), to_tiles(pair[1])], axis=0).reshape(n_data, tiles, 8, 128)
            piece = lax.psum_scatter(full, "data", scatter_dimension=0, tiled=True)[0]
            return jnp.where(first_kind, from_tiles(piece, rows_one, d_ff).reshape(-1, 128), from_tiles(piece, rows_two, d_model).reshape(-1, 128))

        piece_one = scatter(grad_one)
        piece_zero = scatter(grad_zero)
        grad = jnp.stack([piece_zero, piece_one])
        sums = lax.psum(jnp.stack([jnp.sum(grad * grad), loss_acc]), ("stage", "data"))
        clip = jnp.minimum(1.0, tau_clip / jnp.sqrt(sums[0]))
        grad_clip = clip * grad.reshape(2, 1, -1)
        m_new = BETA_ONE * m_loc[0] + (1.0 - BETA_ONE) * grad_clip
        v_new = BETA_TWO * v_loc[0] + (1.0 - BETA_TWO) * grad_clip * grad_clip
        m_hat = m_new / (1.0 - BETA_ONE ** ADAM_STEP)
        v_hat = v_new / (1.0 - BETA_TWO ** ADAM_STEP)
        w_new = wm_loc[0] - learn_rate * (m_hat / (jnp.sqrt(v_hat) + ADAM_EPS) + WEIGHT_DECAY * wm_loc[0])
        w_bf = w_new.astype(jnp.bfloat16).reshape(2, -1)
        w_tiles = jnp.stack([jnp.where(first_kind, to_tiles(w_bf[h].reshape(rows_one, d_ff)), to_tiles(w_bf[h].reshape(rows_two, d_model))) for h in range(2)])
        w_full = lax.all_gather(w_tiles, "data", axis=1, tiled=False)
        half = n_data // 2
        w1_new = jnp.stack([from_tiles(w_full[h, :half], d_model, d_ff) for h in range(2)])[None, :, None]
        w2_new = jnp.stack([from_tiles(w_full[h, half:], d_ff, d_model) for h in range(2)])[None, :, None]
        return w1_new, w2_new, w_new[None], m_new[None], v_new[None], sums[1] / n_tokens

    act_spec = P(None, "data", None)
    flat_spec = P("stage", None, None, "data")
    return jax.shard_map(device_step, mesh=mesh, in_specs=(act_spec, act_spec, P("stage"), P("stage"), flat_spec, flat_spec, flat_spec), out_specs=(P("stage"), P("stage"), flat_spec, flat_spec, flat_spec, P()), check_vma=False)
```

time: 2170 us -> 865 us (0.40)
  matrix products: 1070 us -> 115 us
  local copies, waits for them, and re-layouts: 239 us -> 30.2 us
  other arithmetic: 188 us -> 67.3 us
  waiting for transfers between devices: 529 us -> 560 us
  loops' own time: 26.4 us -> 0 us
    dot_general x198 -> x23, matrix products: 1070 us -> 115 us  [dot32(): lax.dot_general(lhs, rhs, (dims, ((), ())), preferred_element_type=jnp.fl...]
    reduce_scatter x0 -> x2, waiting for transfers between devices: none -> 455 us  [scatter(): piece = lax.psum_scatter(full, 'data', scatter_dimension=0, tiled=True)[0]]
    unnamed x3, waiting for transfers between devices: 358 us -> 0.05 us
    slice x1 -> x5, local copies, waits for them, and re-layouts: 123 us -> 18.8 us  [the longest x1 15.3 us: device_step(): w_full[h, half:]]
    reshape x2 -> x0, local copies, waits for them, and re-layouts: 77.9 us -> none  [the longest x1 40.6 us: device_step(): acc_one.reshape(2, n_blk, -1)]
    concatenate x1 -> x2, other arithmetic: 102 us -> 30.7 us  [scatter(): jnp.concatenate([to_tiles(pair[0]), to_tiles(pair[1])], axis=0)]
    all_gather x1, waiting for transfers between devices: 170 us -> 101 us  [device_step(): w_full = lax.all_gather(w_tiles, 'data', axis=1, tiled=False)]
    reduce_sum x34 -> x2, other arithmetic: 52.4 us -> 1.59 us  [the longest x1 0.84 us: run_stack(): loss_acc = loss_acc + 0.5 * jnp.sum(residual * residual)]
  transfers between devices with their start and end apart: 68 -> 11, of which waited for: 2 -> 5; matrix products, arithmetic and copies ran while one was open for 30% -> 8% of each run, Pallas kernels for 0% -> 0%
where the time goes in v1:
time: 865 us; the launch traced here: 858 us
  waiting for transfers between devices  560 us (65%)
  matrix products  115 us (13%)
  other arithmetic  67.3 us (8%)
  blocking collectives  63 us (7%)
  local copies, waits for them, and re-layouts  30.2 us (3%)
  between operations  18.7 us (2%)
    reduce_scatter x2, waiting for transfers between devices, scatter(): piece = lax.psum_scatter(full, 'data', scatter_dimension=0, tiled=True)[0]  455 us
    dot_general x23, matrix products, dot32(): lax.dot_general(lhs, rhs, (dims, ((), ())), preferred_element_type=jnp.fl...  115 us
    all_gather x1, waiting for transfers between devices, device_step(): w_full = lax.all_gather(w_tiles, 'data', axis=1, tiled=False)  101 us
    psum x1, blocking collectives, device_step(): lax.psum(jnp.stack([jnp.sum(grad * grad), loss_acc]), ('stage', 'data'))  63 us
    concatenate x2, other arithmetic, scatter(): jnp.concatenate([to_tiles(pair[0]), to_tiles(pair[1])], axis=0)  30.7 us
  transfers between devices with their start and end apart: 11, of which 5 were waited for; matrix products, arithmetic and copies ran while one was open for 8% of the time, Pallas kernels for 0%

profile of v1, /device:TPU:0, one launch (start us, length us, event | category | flops | bytes accessed | tf_op | source)
XLA Modules:
  0.0 857.6 jit_solution(2208200724393513539)
XLA Ops:
  7.2 1.2 fusion.271
  8.4 6.7 fusion.192
  15.2 1.7 collective-permute-done
  17.0 6.7 add_convert_fusion.6
  24.0 6.5 bitcast_select_fusion.1
  30.5 8.4 add_convert_fusion.5
  39.5 5.4 fusion.28
  44.9 8.1 multiply_reduce_fusion.1
  53.2 3.9 fusion.16
  57.1 6.2 fusion.44
  63.4 1.4 fusion.189
  65.5 3.1 fusion.10
  69.3 7.7 broadcast_select_fusion.8
  77.1 6.1 fusion.51
  83.2 1.1 copy-done.22
  84.3 3.8 add_convert_fusion.2
  88.8 1.4 fusion.266
  90.4 1.5 copy-done.12
  91.8 6.6 fusion.58
  98.4 1.2 copy-done.19
  99.7 1.4 add_convert_fusion.1
  101.5 12.2 %broadcast_select_fusion.3 = (bf16[256,3072]{1,0:T(8,128)(2,1)}, bf16[256,3072]{1,0:T(8,128)(2,1)}, bf16[256,3072]{1,0:T(8,128)(2,1)}, bf16[256,3072]{1,0:T(8,128)(2,1)}, f32[256,3072]{1,0:T(8,128)}) fusion(pred[]{:T(512)S(6)} %eq.3, f32[256,3072]{1,0:T(8,128)} %copy-done.12, f32[256,3072]{1,0:T(8,128)} %fusion.28, f32[256,3072]{1,0:T(8,128)} %fusion.10, ...), kind=kOutput, calls=%fused_computation.179 | convolution fusion | flops 1246494720 | bytes 27131904 | tf_op jit(solution)/shard_map/dot_general | solution.py:19
  113.8 6.6 broadcast_select_fusion.4
  120.4 1.5 add_convert_fusion
  122.6 1.3 collective-permute-done.7
  124.0 2.7 fusion.133
  126.7 5.3 fusion.149
  132.0 2.7 fusion.129
  134.7 15.3 %pad_maximum_fusion = f32[4608,8,128]{2,1,0:T(8,128)} fusion(f32[2304,8,128]{2,1,0:T(8,128)S(1)} %bitcast.289, f32[2304,8,128]{2,1,0:T(8,128)S(1)} %bitcast.279), kind=kLoop, calls=%fused_computation | loop fusion | flops 4718592 | bytes 37748736 | tf_op jit(solution)/shard_map/concatenate | solution.py:138
  150.3 4.3 fusion.137
  154.6 2.7 fusion.141
  157.3 15.4 %pad_maximum_fusion.1 = f32[4608,8,128]{2,1,0:T(8,128)} fusion(f32[2304,8,128]{2,1,0:T(8,128)S(1)} %bitcast.290, f32[2304,8,128]{2,1,0:T(8,128)S(1)} %bitcast.278), kind=kLoop, calls=%fused_computation.1 | loop fusion | flops 4718592 | bytes 37748736 | tf_op jit(solution)/shard_map/concatenate | solution.py:138
  172.9 0.9 copy-done.4
  176.0 216.6 %reduce-scatter.3.cloned.1.call-done = f32[1,72,8,128]{3,2,1,0:T(8,128)} async-done(((f32[64,72,8,128]{3,2,1,0:T(8,128)}), f32[1,72,8,128]{3,2,1,0:T(8,128)}) %reduce-scatter.3.cloned.1.call-update) | async-done | bytes 294928 | tf_op jit(solution)/shard_map/reduce_scatter | solution.py:139
  392.6 1.0 copy.16
  393.6 1.0 reshape_reshape.25
  394.7 1.0 copy.15
  395.7 238.9 %reduce-scatter.5.cloned.1.call-done = f32[1,72,8,128]{3,2,1,0:T(8,128)} async-done(((f32[64,72,8,128]{3,2,1,0:T(8,128)}), f32[1,72,8,128]{3,2,1,0:T(8,128)}) %reduce-scatter.5.cloned.1.call-update) | async-done | bytes 294928 | tf_op jit(solution)/shard_map/reduce_scatter | solution.py:139
  634.6 1.0 copy.17
  635.6 1.0 copy.18
  638.6 63.0 %psum.7 = f32[2]{0:T(128)S(1)} all-reduce(f32[2]{0:T(128)S(1)} %pad_maximum_fusion.3), channel_id=1, replica_groups=mesh['stage'=2,'data'=64] {'stage','data'}, use_global_device_ids=true, to_apply=%region_5.6 | all-reduce | flops 2 | bytes 16 | tf_op jit(solution)/shard_map/psum | solution.py:145
  703.8 3.9 fusion.224
  707.7 1.7 slice_reduce_fusion.1
  711.1 5.1 multiply_subtract_fusion
  716.1 101.3 %all-gather.3.cloned.1.call-done = bf16[2,4608,8,128]{3,2,1,0:T(8,128)(2,1)} async-done(((bf16[2,72,8,128]{3,2,1,0:T(8,128)(2,1)}), bf16[2,4608,8,128]{3,2,1,0:T(8,128)(2,1)}) %all-gather.3.cloned.1.call-update) | async-done | bytes 18874384 | tf_op jit(solution)/shard_map/all_gather | solution.py:155
  817.4 15.3 %fusion.269 = (bf16[1,32,72,8,128]{4,3,2,1,0:T(8,128)(2,1)}, bf16[1,32,72,8,128]{4,3,2,1,0:T(8,128)(2,1)}, bf16[1,32,72,8,128]{4,3,2,1,0:T(8,128)(2,1)}, bf16[1,32,72,8,128]{4,3,2,1,0:T(8,128)(2,1)}) fusion(bf16[2,64,72,8,128]{4,3,2,1,0:T(8,128)(2,1)} %bitcast.284), kind=kLoop, calls=%fused_computation.288 | loop fusion | bytes 37748736 | tf_op jit(solution)/shard_map/slice | solution.py:158
  832.7 8.4 maximum_bitcast_fusion.1
  841.1 8.4 maximum_bitcast_fusion
  (114 shorter events, 10.4 us)
Async XLA Ops:
  7.2 385.4 %reduce-scatter.3.cloned.1.call-start = ((), (), s32[]{:S(2)}) async-start(), calls=%async_computation.2 | async-start | bytes 19169280 | tf_op jit(solution)/shard_map/reduce_scatter | solution.py:139
  15.1 1.8 collective-permute-start
  23.8 6.7 copy-start.7
  23.8 6.8 collective-permute-start.1
  30.5 38.8 %copy-start.3 = (bf16[8,32,768]{2,1,0:T(8,128)(2,1)}, bf16[8,32,768]{2,1,0:T(8,128)(2,1)S(1)}, u32[]{:S(2)}) copy-start(bf16[8,32,768]{2,1,0:T(8,128)(2,1)S(1)} %get-tuple-element.30) | copy-start | bytes 1179652
  30.5 59.6 %copy-start.5 = (bf16[256,768]{1,0:T(8,128)(2,1)}, bf16[256,768]{1,0:T(8,128)(2,1)S(1)}, u32[]{:S(2)}) copy-start(bf16[256,768]{1,0:T(8,128)(2,1)S(1)} %collective-permute-done.1) | copy-start | bytes 1179652
  38.9 6.0 collective-permute-start.2
  53.0 4.1 copy-start.23
  53.0 12.5 %collective-permute-start.4 = (bf16[256,768]{1,0:T(8,128)(2,1)S(1)}, bf16[256,768]{1,0:T(8,128)(2,1)S(1)}, u32[]{:S(2)}, u32[]{:S(2)}) collective-permute-start(bf16[256,768]{1,0:T(8,128)(2,1)S(1)} %get-tuple-element.44), channel_id=1, source_target_pairs={{0,64},{64,0},{1,65},{65,1},{2,66},{66,2},{3,67},{67,3},{4,68},{68... | collective-permute-start | bytes 1179656 | tf_op jit(solution)/shard_map/ppermute | solution.py:66
  53.2 10.2 %slice-start = ((s8[9437184]{0:T(1024)(128)(4,1)}), s8[4194304]{0:T(1024)(128)(4,1)S(1)}, s32[]{:S(2)}) async-start(s8[9437184]{0:T(1024)(128)(4,1)} %bitcast.285), calls=%async_computation.5 | async-start | bytes 8388608
  57.0 6.3 copy-start.14
  57.1 6.3 slice-start.1
  57.1 6.3 slice-start.2
  63.4 1.5 copy-start.21
  64.8 3.7 collective-permute-start.3
  68.6 0.7 copy-start.11
  69.3 19.4 %slice-start.6 = ((s8[4718592]{0:T(1024)(128)(4,1)}), s8[524288]{0:T(1024)(128)(4,1)S(1)}, s32[]{:S(2)}) async-start(s8[4718592]{0:T(1024)(128)(4,1)} %bitcast.291), calls=%async_computation.11 | async-start | bytes 1048576
  77.1 6.1 copy-start.9
  77.1 11.7 %slice-start.7 = ((s8[4718592]{0:T(1024)(128)(4,1)}), s8[4194304]{0:T(1024)(128)(4,1)S(1)}, s32[]{:S(2)}) async-start(s8[4718592]{0:T(1024)(128)(4,1)} %bitcast.291), calls=%async_computation.12 | async-start | bytes 8388608
  83.2 1.1 copy-start.22
  88.1 2.3 collective-permute-start.5
  90.2 1.7 copy-start.12
  90.2 11.3 %slice-start.3 = ((s8[9437184]{0:T(1024)(128)(4,1)}), s8[4194304]{0:T(1024)(128)(4,1)S(1)}, s32[]{:S(2)}) async-start(s8[9437184]{0:T(1024)(128)(4,1)} %bitcast.287), calls=%async_computation.8 | async-start | bytes 8388608
  90.3 11.2 %slice-start.4 = ((s8[9437184]{0:T(1024)(128)(4,1)}), s8[4194304]{0:T(1024)(128)(4,1)S(1)}, s32[]{:S(2)}) async-start(s8[9437184]{0:T(1024)(128)(4,1)} %bitcast.287), calls=%async_computation.9 | async-start | bytes 8388608
  90.4 11.2 %slice-start.5 = ((s8[9437184]{0:T(1024)(128)(4,1)}), s8[1048576]{0:T(1024)(128)(4,1)S(1)}, s32[]{:S(2)}) async-start(s8[9437184]{0:T(1024)(128)(4,1)} %bitcast.287), calls=%async_computation.10 | async-start | bytes 2097152
  98.4 1.3 copy-start.19
  99.7 14.1 %slice-start.8 = ((s8[9437184]{0:T(1024)(128)(4,1)}), s8[4194304]{0:T(1024)(128)(4,1)S(1)}, s32[]{:S(2)}) async-start(s8[9437184]{0:T(1024)(128)(4,1)} %bitcast.310), calls=%async_computation.13 | async-start | bytes 8388608
  101.1 12.6 %collective-permute-start.6 = (bf16[256,768]{1,0:T(8,128)(2,1)S(1)}, bf16[256,768]{1,0:T(8,128)(2,1)S(1)}, u32[]{:S(2)}, u32[]{:S(2)}) collective-permute-start(bf16[256,768]{1,0:T(8,128)(2,1)S(1)} %add_convert_fusion.1), channel_id=1, source_target_pairs={{0,64},{64,0},{1,65},{65,1},{2,66},{66,2},{3,67},{67,3},{4,68},{68... | collective-permute-start | bytes 1179656 | tf_op jit(solution)/shard_map/ppermute | solution.py:106
  101.5 12.2 %slice-start.9 = ((s8[9437184]{0:T(1024)(128)(4,1)}), s8[4194304]{0:T(1024)(128)(4,1)S(1)}, s32[]{:S(2)}) async-start(s8[9437184]{0:T(1024)(128)(4,1)} %bitcast.310), calls=%async_computation.14 | async-start | bytes 8388608
  101.5 12.2 %slice-start.10 = ((s8[9437184]{0:T(1024)(128)(4,1)}), s8[1048576]{0:T(1024)(128)(4,1)S(1)}, s32[]{:S(2)}) async-start(s8[9437184]{0:T(1024)(128)(4,1)} %bitcast.310), calls=%async_computation.15 | async-start | bytes 2097152
  120.4 2.1 copy-start.6
  120.4 3.5 copy-start.10
  121.9 2.1 copy-start.17
  121.9 2.1 copy-start.18
  121.9 2.0 collective-permute-start.7
  124.0 2.7 copy-start.13
  150.0 484.6 %reduce-scatter.5.cloned.1.call-start = ((), (), s32[]{:S(2)}) async-start(), calls=%async_computation.3 | async-start | bytes 19169280 | tf_op jit(solution)/shard_map/reduce_scatter | solution.py:139
  150.3 4.3 copy-start.15
  150.3 4.3 copy-start.16
  150.3 4.3 copy-start.20
  172.8 1.0 copy-start.4
  172.8 1.1 copy-start.8
  172.8 644.6 %all-gather.3.cloned.1.call-start = ((), (), s32[]{:S(2)}) async-start(), calls=%async_computation.4 | async-start | bytes 19169280 | tf_op jit(solution)/shard_map/all_gather | solution.py:155
  636.7 67.1 %copy-start = (f32[1,2,1,73728]{3,2,1,0:T(1,128)S(1)}, f32[1,2,1,73728]{3,2,1,0:T(1,128)}, u32[]{:S(2)}) copy-start(f32[1,2,1,73728]{3,2,1,0:T(1,128)} %param.11) | copy-start | bytes 1769476
  636.7 67.1 %copy-start.1 = (f32[1,2,1,73728]{3,2,1,0:T(1,128)S(1)}, f32[1,2,1,73728]{3,2,1,0:T(1,128)}, u32[]{:S(2)}) copy-start(f32[1,2,1,73728]{3,2,1,0:T(1,128)} %param.13) | copy-start | bytes 1769476
  636.7 67.1 %copy-start.2 = (f32[1,2,1,73728]{3,2,1,0:T(1,128)S(1)}, f32[1,2,1,73728]{3,2,1,0:T(1,128)}, u32[]{:S(2)}) copy-start(f32[1,2,1,73728]{3,2,1,0:T(1,128)} %param.12) | copy-start | bytes 1769476
Sparse Core Ops, SparseCore 0:
  150.2 242.4 reduce-scatter.2
  397.4 237.2 reduce-scatter.4
  710.5 106.7 all-gather.2

commit v2 on v1

--- a/solution.py
+++ b/solution.py
@@ -1,7 +1,10 @@
+import functools
 import math
 import jax
 import jax.numpy as jnp
 from jax import lax
+from jax.experimental import pallas as pl
+from jax.experimental.pallas import tpu as pltpu
 from jax.sharding import PartitionSpec as P
 
 BETA_ONE = 0.9
@@ -22,10 +25,6 @@
 def to_tiles(mat):
     rows, cols = mat.shape
     return mat.reshape(rows // 8, 8, cols // 128, 128).transpose(0, 2, 1, 3).reshape(-1, 8, 128)
-
-
-def from_tiles(tiles, rows, cols):
-    return tiles.reshape(rows // 8, cols // 128, 8, 128).transpose(0, 2, 1, 3).reshape(rows, cols)
 
 
 def run_stack(x_all, t_all, w1_loc, w2_loc, n_tokens, n_chunk):
@@ -116,6 +115,283 @@
     return grads[1], grads[0], loss_acc
 
 
+TILES = 72
+PART = 24
+ORDERS = ((2, 1, 0), (1, 0, 2), (0, 2, 1))
+MESH_ID = pl.DeviceIdType.MESH
+
+
+def tail_kernel(tau_clip, learn_rate, g0_ref, g1_ref, w_ref, m_ref, v_ref, loss_ref,
+                w_out, m_out, v_out, stat_out, full_out,
+                recv1, recv2, recv3, local, wbf, nbuf,
+                s1, r1, s2, r2, s3, r3, l_sem, own_sem, ns, nr,
+                t1, q1, t2, q2, t3, q3):
+    stage = lax.axis_index("stage")
+    me = lax.axis_index("data")
+    coords = (me // 16, (me // 4) % 4, me % 4)
+    strides = (16, 4, 1)
+    g_refs = (g0_ref, g1_ref)
+    streams = [(k, d) for k in range(3) for d in range(2)]
+
+    def peer(axis, delta):
+        moved = lax.rem(coords[axis] + delta + 4, 4)
+        return (stage, me + (moved - coords[axis]) * strides[axis])
+
+    def ring(axis, delta):
+        return lax.rem(coords[axis] + delta + 8, 4)
+
+    barrier = pltpu.get_barrier_semaphore()
+    for axis in range(3):
+        for delta in (1, 2, 3):
+            pl.semaphore_signal(barrier, inc=1, device_id=peer(axis, delta), device_id_type=MESH_ID)
+    pl.semaphore_signal(barrier, inc=1, device_id=(1 - stage, me), device_id_type=MESH_ID)
+    pl.semaphore_wait(barrier, 10)
+
+    def sgn(d):
+        return 1 if d == 0 else -1
+
+    def pick(k, on_a, on_b, on_c):
+        index = [None] * 3
+        index[ORDERS[k][0]], index[ORDERS[k][1]], index[ORDERS[k][2]] = on_a, on_b, on_c
+        return tuple(index)
+
+    def remote(src, dst, send_sem, recv_sem, target):
+        return pltpu.make_async_remote_copy(src_ref=src, dst_ref=dst, send_sem=send_sem, recv_sem=recv_sem, device_id=target, device_id_type=MESH_ID)
+
+    def grad_part(st, on_a, on_b):
+        k, d = streams[st]
+        return g_refs[d].at[pick(k, on_a, on_b, slice(None)) + (pl.ds(PART * k, PART),)]
+
+    def sub_of(st, i):
+        k, d = streams[st]
+        return ring(ORDERS[k][1], -sgn(d) * (1 + i))
+
+    def next_of(st, phase):
+        k, d = streams[st]
+        return peer(ORDERS[k][phase], sgn(d))
+
+    def first_send(st, i):
+        k, d = streams[st]
+        return remote(grad_part(st, ring(ORDERS[k][0], -sgn(d)), sub_of(st, i)), recv1.at[st, 0, i], s1.at[st, 0, i], r1.at[st, 0, i], next_of(st, 0))
+
+    def forward1(st, step, i):
+        return remote(recv1.at[st, step, i], recv1.at[st, step + 1, i], s1.at[st, step + 1, i], r1.at[st, step + 1, i], next_of(st, 0))
+
+    def arrived1(st, step, i):
+        return remote(recv1.at[st, step, i], recv1.at[st, step, i], s1.at[st, step, i], r1.at[st, step, i], next_of(st, 0))
+
+    def fetch(st, n):
+        k, d = streams[st]
+        step, i = n // 4, n % 4
+        return pltpu.make_async_copy(grad_part(st, ring(ORDERS[k][0], -sgn(d) * (2 + step)), sub_of(st, i)), local.at[st, n % 2], l_sem.at[st, n % 2])
+
+    def send2(st, step):
+        src = recv1.at[st, 2, 0] if step == 0 else recv2.at[st, step - 1]
+        return remote(src, recv2.at[st, step], s2.at[st, step], r2.at[st, step], next_of(st, 1))
+
+    def send3(st, step):
+        k, d = streams[st]
+        src = recv2.at[st, 2, ring(ORDERS[k][2], -sgn(d))] if step == 0 else recv3.at[st, step - 1]
+        return remote(src, recv3.at[st, step], s3.at[st, step], r3.at[st, step], next_of(st, 2))
+
+    all_st = range(6)
+    for st in all_st:
+        for n in range(2):
+            fetch(st, n).start()
+    for i in range(4):
+        for st in all_st:
+            first_send(st, i).start()
+
+    def accumulate(st, step, i, n, more):
+        arrived1(st, step, i).wait_recv()
+        fetch(st, n).wait()
+        recv1[st, step, i] = recv1[st, step, i] + local[st, n % 2]
+        if more:
+            fetch(st, n + 2).start()
+
+    def phase1(n, carry):
+        step, i = n // 4, n % 4
+        for st in all_st:
+            accumulate(st, step, i, n, True)
+            forward1(st, step, i).start()
+        return carry
+
+    lax.fori_loop(0, 8, phase1, 0)
+    for i in range(4):
+        for st in all_st:
+            accumulate(st, 2, i, 8 + i, i < 2)
+            if i == 0:
+                send2(st, 0).start()
+        if i > 0:
+            for st in all_st:
+                send2(st, i - 1).wait_recv()
+                recv2[st, i - 1] = recv2[st, i - 1] + recv1[st, 2, i]
+                if i < 3:
+                    send2(st, i).start()
+                else:
+                    send3(st, 0).start()
+    for step in range(3):
+        for st in all_st:
+            k, d = streams[st]
+            send3(st, step).wait_recv()
+            recv3[st, step] = recv3[st, step] + recv2[st, 2, ring(ORDERS[k][2], -sgn(d) * (2 + step))]
+            if step < 2:
+                send3(st, step + 1).start()
+
+    total = jnp.zeros((8, 128), jnp.float32)
+    for st in all_st:
+        piece = recv3[st, 2]
+        total = total + jnp.sum(piece * piece, axis=0)
+
+    parts = (total, loss_ref[...])
+    for phase in range(4):
+        size = 2 if phase == 0 else 4
+        mine = stage if phase == 0 else coords[phase - 1]
+        nbuf[phase, mine, 0] = parts[0]
+        nbuf[phase, mine, 1] = parts[1]
+        sends = []
+        for delta in range(1, size):
+            target = (1 - stage, me) if phase == 0 else peer(phase - 1, delta)
+            sends.append(remote(nbuf.at[phase, mine], nbuf.at[phase, mine], ns.at[phase, delta], nr.at[phase, delta], target))
+        for send in sends:
+            send.start()
+        for send in sends:
+            send.wait_recv()
+        parts = tuple(sum((nbuf[phase, slot, j] for slot in range(1, size)), nbuf[phase, 0, j]) for j in range(2))
+        for send in sends:
+            send.wait_send()
+
+    stat_out[...] = jnp.full((8, 128), jnp.sum(parts[1]), jnp.float32)
+    norm = jnp.sqrt(jnp.full((8, 128), jnp.sum(parts[0]), jnp.float32))
+    clip = jnp.minimum(1.0, tau_clip / norm)
+
+    def update(width):
+        def group(k, carry):
+            for h in range(2):
+                for t in range(PART):
+                    rows = pl.ds(k * 192 + (t // width) * (8 * width) + t % width, 8, stride=width)
+                    grad = clip * recv3[2 * k + h, 2, t]
+                    m_new = BETA_ONE * m_ref[h, rows, :] + (1.0 - BETA_ONE) * grad
+                    v_new = BETA_TWO * v_ref[h, rows, :] + (1.0 - BETA_TWO) * grad * grad
+                    m_hat = m_new / (1.0 - BETA_ONE ** ADAM_STEP)
+                    v_hat = v_new / (1.0 - BETA_TWO ** ADAM_STEP)
+                    w_old = w_ref[h, rows, :]
+                    w_new = w_old - learn_rate * (m_hat / (jnp.sqrt(v_hat) + ADAM_EPS) + WEIGHT_DECAY * w_old)
+                    w_out[h, rows, :] = w_new
+                    m_out[h, rows, :] = m_new
+                    v_out[h, rows, :] = v_new
+                    wbf[h, k * PART + t] = w_new.astype(jnp.bfloat16)
+            return carry
+
+        lax.fori_loop(0, 3, group, 0)
+
+    @pl.when(me < 32)
+    def _():
+        update(24)
+
+    @pl.when(me >= 32)
+    def _():
+        update(6)
+
+    def full_part(st, on_a, on_b, on_c):
+        k, d = streams[st]
+        return full_out.at[(d,) + pick(k, on_a, on_b, on_c) + (pl.ds(PART * k, PART),)]
+
+    def coord_of(st, phase, delta):
+        k, d = streams[st]
+        return ring(ORDERS[k][phase], -sgn(d) * delta)
+
+    def gather1(st, step):
+        k, d = streams[st]
+        place = full_part(st, coord_of(st, 0, 0), coord_of(st, 1, 0), coord_of(st, 2, step))
+        src = wbf.at[d, pl.ds(PART * k, PART)] if step == 0 else place
+        return remote(src, place, t1.at[st, step], q1.at[st, step], next_of(st, 2))
+
+    def gather2(st, step):
+        place = full_part(st, coord_of(st, 0, 0), coord_of(st, 1, step), slice(None))
+        return remote(place, place, t2.at[st, step], q2.at[st, step], next_of(st, 1))
+
+    def gather3(st, step, i):
+        place = full_part(st, coord_of(st, 0, step), coord_of(st, 1, i), slice(None))
+        return remote(place, place, t3.at[st, step, i], q3.at[st, step, i], next_of(st, 0))
+
+    def own(st):
+        k, d = streams[st]
+        return pltpu.make_async_copy(wbf.at[d, pl.ds(PART * k, PART)], full_part(st, coord_of(st, 0, 0), coord_of(st, 1, 0), coord_of(st, 2, 0)), own_sem.at[st])
+
+    for st in all_st:
+        gather1(st, 0).start()
+        own(st).start()
+    for step in range(3):
+        for st in all_st:
+            gather1(st, step).wait_recv()
+            if step < 2:
+                gather1(st, step + 1).start()
+    for st in all_st:
+        own(st).wait()
+        gather2(st, 0).start()
+        gather3(st, 0, 0).start()
+    for step in range(3):
+        for st in all_st:
+            gather2(st, step).wait_recv()
+            if step < 2:
+                gather2(st, step + 1).start()
+            gather3(st, 0, step + 1).start()
+
+    def phase3(n, carry):
+        step, i = n // 4, n % 4
+        for st in all_st:
+            gather3(st, step, i).wait_recv()
+            gather3(st, step + 1, i).start()
+        return carry
+
+    lax.fori_loop(0, 8, phase3, 0)
+    for i in range(4):
+        for st in all_st:
+            gather3(st, 2, i).wait_recv()
+
+    def drain(n, carry):
+        step, i = n // 4, n % 4
+        for st in all_st:
+            arrived1(st, step, i).wait_send()
+            gather3(st, step, i).wait_send()
+        return carry
+
+    lax.fori_loop(0, 12, drain, 0)
+    for step in range(3):
+        for st in all_st:
+            send2(st, step).wait_send()
+            send3(st, step).wait_send()
+            gather1(st, step).wait_send()
+            gather2(st, step).wait_send()
+
+
+def tail(g0, g1, w_flat, m_flat, v_flat, loss_tile, tau_clip, learn_rate):
+    flat = jax.ShapeDtypeStruct((2, 576, 128), jnp.float32)
+    in_vmem = pl.BlockSpec(memory_space=pltpu.VMEM)
+    in_any = pl.BlockSpec(memory_space=pl.ANY)
+    dma = pltpu.SemaphoreType.DMA
+    return pl.pallas_call(
+        functools.partial(tail_kernel, tau_clip, learn_rate),
+        out_shape=(flat, flat, flat, jax.ShapeDtypeStruct((8, 128), jnp.float32), jax.ShapeDtypeStruct((2, 4, 4, 4, TILES, 8, 128), jnp.bfloat16)),
+        in_specs=[in_any] * 2 + [in_vmem] * 4,
+        out_specs=(in_vmem, in_vmem, in_vmem, in_vmem, in_any),
+        scratch_shapes=[
+            pltpu.VMEM((6, 3, 4, 4, PART, 8, 128), jnp.float32),
+            pltpu.VMEM((6, 3, 4, PART, 8, 128), jnp.float32),
+            pltpu.VMEM((6, 3, PART, 8, 128), jnp.float32),
+            pltpu.VMEM((6, 2, 4, PART, 8, 128), jnp.float32),
+            pltpu.VMEM((2, TILES, 8, 128), jnp.bfloat16),
+            pltpu.VMEM((4, 4, 2, 8, 128), jnp.float32),
+            dma((6, 3, 4)), dma((6, 3, 4)), dma((6, 3)), dma((6, 3)), dma((6, 3)), dma((6, 3)),
+            dma((6, 2)), dma((6,)), dma((4, 4)), dma((4, 4)),
+            dma((6, 3)), dma((6, 3)), dma((6, 3)), dma((6, 3)), dma((6, 3, 4)), dma((6, 3, 4)),
+        ],
+        compiler_params=pltpu.CompilerParams(collective_id=1, has_side_effects=True, vmem_limit_bytes=60 * 1024 * 1024),
+        name="tail",
+    )(g0, g1, w_flat, m_flat, v_flat, loss_tile)
+
+
 def solution(mesh):
     n_stage = mesh.shape["stage"]
     n_data = mesh.shape["data"]
@@ -127,36 +403,21 @@
         n_blocks = 2 * n_stage
         tau_clip = 0.3 * d_model * math.sqrt(n_blocks * (3.0 / n_tokens + 0.008))
         learn_rate = 0.1 / math.sqrt(4.0 * d_model * n_blocks)
-        first_kind = lax.axis_index("data") < n_data // 2
         x_all = x_loc.reshape(n_micro * n_tok, d_model)
         t_all = t_loc.reshape(n_micro * n_tok, d_model)
         grad_zero, grad_one, loss_acc = run_stack(x_all, t_all, w1_loc[0, :, 0], w2_loc[0, :, 0], n_tokens, 2)
-        tiles = d_model * d_ff * 2 // n_data // 1024
-        rows_one, rows_two = 2 * d_model // n_data, 2 * d_ff // n_data
-
-        def scatter(pair):
-            full = jnp.concatenate([to_tiles(pair[0]), to_tiles(pair[1])], axis=0).reshape(n_data, tiles, 8, 128)
-            piece = lax.psum_scatter(full, "data", scatter_dimension=0, tiled=True)[0]
-            return jnp.where(first_kind, from_tiles(piece, rows_one, d_ff).reshape(-1, 128), from_tiles(piece, rows_two, d_model).reshape(-1, 128))
-
-        piece_one = scatter(grad_one)
-        piece_zero = scatter(grad_zero)
-        grad = jnp.stack([piece_zero, piece_one])
-        sums = lax.psum(jnp.stack([jnp.sum(grad * grad), loss_acc]), ("stage", "data"))
-        clip = jnp.minimum(1.0, tau_clip / jnp.sqrt(sums[0]))
-        grad_clip = clip * grad.reshape(2, 1, -1)
-        m_new = BETA_ONE * m_loc[0] + (1.0 - BETA_ONE) * grad_clip
-        v_new = BETA_TWO * v_loc[0] + (1.0 - BETA_TWO) * grad_clip * grad_clip
-        m_hat = m_new / (1.0 - BETA_ONE ** ADAM_STEP)
-        v_hat = v_new / (1.0 - BETA_TWO ** ADAM_STEP)
-        w_new = wm_loc[0] - learn_rate * (m_hat / (jnp.sqrt(v_hat) + ADAM_EPS) + WEIGHT_DECAY * wm_loc[0])
-        w_bf = w_new.astype(jnp.bfloat16).reshape(2, -1)
-        w_tiles = jnp.stack([jnp.where(first_kind, to_tiles(w_bf[h].reshape(rows_one, d_ff)), to_tiles(w_bf[h].reshape(rows_two, d_model))) for h in range(2)])
-        w_full = lax.all_gather(w_tiles, "data", axis=1, tiled=False)
-        half = n_data // 2
-        w1_new = jnp.stack([from_tiles(w_full[h, :half], d_model, d_ff) for h in range(2)])[None, :, None]
-        w2_new = jnp.stack([from_tiles(w_full[h, half:], d_ff, d_model) for h in range(2)])[None, :, None]
-        return w1_new, w2_new, w_new[None], m_new[None], v_new[None], sums[1] / n_tokens
+
+        def whole(pair):
+            return jnp.concatenate([to_tiles(pair[0]), to_tiles(pair[1])], axis=0).reshape(4, 4, 4, TILES, 8, 128)
+
+        loss_tile = jnp.where(lax.broadcasted_iota(jnp.int32, (8, 128), 0) + lax.broadcasted_iota(jnp.int32, (8, 128), 1) == 0, loss_acc, 0.0)
+        w_new, m_new, v_new, stat, w_full = tail(
+            whole(grad_zero), whole(grad_one), wm_loc.reshape(2, 576, 128), m_loc.reshape(2, 576, 128), v_loc.reshape(2, 576, 128),
+            loss_tile, tau_clip, learn_rate)
+        w1_new = w_full[:, :2].reshape(2, d_model // 8, d_ff // 128, 8, 128).transpose(0, 1, 3, 2, 4).reshape(1, 2, 1, d_model, d_ff)
+        w2_new = w_full[:, 2:].reshape(2, d_ff // 8, d_model // 128, 8, 128).transpose(0, 1, 3, 2, 4).reshape(1, 2, 1, d_ff, d_model)
+        flat_dims = (1, 2, 1, -1)
+        return w1_new, w2_new, w_new.reshape(flat_dims), m_new.reshape(flat_dims), v_new.reshape(flat_dims), stat[0, 0] / n_tokens
 
     act_spec = P(None, "data", None)
     flat_spec = P("stage", None, None, "data")

time: 865 us -> 447 us (0.52)
  waiting for transfers between devices: 560 us -> 4.5 us
  Pallas kernels: 0 us -> 246 us
  blocking collectives: 63 us -> 0 us
  other arithmetic: 67.3 us -> 41.5 us
  between operations: 18.7 us -> 4.77 us
  local copies, waits for them, and re-layouts: 30.2 us -> 20.9 us
    reduce_scatter x2 -> x0, waiting for transfers between devices: 455 us -> none  [scatter(): piece = lax.psum_scatter(full, 'data', scatter_dimension=0, tiled=True)[0]]
    pallas_call x0 -> x1, Pallas kernels: none -> 246 us  [tail(): pl.pallas_call(functools.partial(tail_kernel, tau_clip, learn_rate), out_...]
    all_gather x1 -> x0, waiting for transfers between devices: 101 us -> none  [device_step(): w_full = lax.all_gather(w_tiles, 'data', axis=1, tiled=False)]
    psum x1 -> x0, blocking collectives: 63 us -> none  [device_step(): lax.psum(jnp.stack([jnp.sum(grad * grad), loss_acc]), ('stage', 'data'))]
    broadcast_in_dim x2 -> x0, other arithmetic: 16.8 us -> none  [the longest x1 8.38 us: device_step(): jnp.stack([from_tiles(w_full[h, half:], d_ff, d_model) for h in range(2)])]
    slice x3 -> x2, local copies, waits for them, and re-layouts: 17.6 us -> 15.8 us  [the longest x1 14.6 us: device_step(): w_full[:, 2:].reshape(2, d_ff // 8, d_model // 128, 8, 128)]
  transfers between devices with their start and end apart: 11 -> 8, of which waited for: 5 -> 3; matrix products, arithmetic and copies ran while one was open for 8% -> 5% of each run, Pallas kernels for 0% -> 0%
where the time goes in v2:
time: 447 us; the launch traced here: 439 us
  Pallas kernels  246 us (55%)
  matrix products  118 us (26%)
  other arithmetic  41.5 us (9%)
  local copies, waits for them, and re-layouts  20.9 us (5%)
  between operations  4.77 us (1%)
  waiting for transfers between devices  4.5 us (1%)
    pallas_call x1, Pallas kernels, tail(): pl.pallas_call(functools.partial(tail_kernel, tau_clip, learn_rate), out_...  246 us
    dot_general x23, matrix products, dot32(): lax.dot_general(lhs, rhs, (dims, ((), ())), preferred_element_type=jnp.fl...  118 us
    concatenate x2, other arithmetic, whole(): jnp.concatenate([to_tiles(pair[0]), to_tiles(pair[1])], axis=0)  31.1 us
    slice x1, local copies, waits for them, and re-layouts, device_step(): w_full[:, 2:].reshape(2, d_ff // 8, d_model // 128, 8, 128)  14.6 us
  transfers between devices with their start and end apart: 8, of which 3 were waited for; matrix products, arithmetic and copies ran while one was open for 5% of the time, Pallas kernels for 0%

profile of v2, /device:TPU:0, one launch (start us, length us, event | category | flops | bytes accessed | tf_op | source)
XLA Modules:
  0.0 439.3 jit_solution(3813433551739864336)
XLA Ops:
  0.6 1.2 fusion.260
  1.8 6.7 %fusion.192 = bf16[256,768]{1,0:T(8,128)(2,1)S(1)} fusion(bf16[1,2,1,3072,768]{4,3,2,1,0:T(8,128)(2,1)} %param.10, bf16[256,768]{1,0:T(8,128)(2,1)S(1)} %bitcast.213, bf16[1,2,1,768,3072]{4,3,2,1,0:T(8,128)(2,1)} %param.9), kind=kOutput, calls=%fused_computation.188 | convolution fusion | flops 2423586816 | bytes 10616832 | tf_op jit(solution)/shard_map/dot_general | solution.py:22
  8.6 1.7 collective-permute-done
  10.4 6.7 %add_convert_fusion.6 = bf16[256,768]{1,0:T(8,128)(2,1)S(1)} fusion(bf16[256,768]{1,0:T(8,128)(2,1)S(1)} %bitcast_select_fusion.8, bf16[1,2,1,3072,768]{4,3,2,1,0:T(8,128)(2,1)} %param.10, bf16[1,2,1,768,3072]{4,3,2,1,0:T(8,128)(2,1)} %param.9), kind=kOutput, calls=%fused_computation.213 | convolution fusion | flops 2423586816 | bytes 10616832 | tf_op jit(solution)/shard_map/dot_general | solution.py:22
  17.2 0.2 collective-permute-start.1
  17.4 6.5 %bitcast_select_fusion.1 = bf16[768,3072]{1,0:T(8,128)(2,1)} fusion(pred[]{:T(512)S(6)} %eq.9, bf16[1,2,1,768,3072]{4,3,2,1,0:T(8,128)(2,1)} %param.9), kind=kLoop, calls=%fused_computation.28 | loop fusion | flops 2359296 | bytes 14155777 | tf_op jit(solution)/shard_map/jit(_where)/select_n | solution.py:42
  23.9 8.1 %add_convert_fusion.5 = bf16[256,768]{1,0:T(8,128)(2,1)S(1)} fusion(bf16[256,768]{1,0:T(8,128)(2,1)S(1)} %collective-permute-done.1, pred[]{:T(512)S(6)} %eq.9, bf16[1,2,1,3072,768]{4,3,2,1,0:T(8,128)(2,1)} %param.10, bf16[768,3072]{1,0:T(8,128)(2,1)} %bitcast_select_fusion.1), kind=kOutput, calls=%fused_computation.212 | convolution fusion | flops 2425946112 | bytes 15335425 | tf_op jit(solution)/shard_map/dot_general | solution.py:22
  32.1 0.6 collective-permute-start.2
  32.7 5.4 %fusion.28 = f32[256,3072]{1,0:T(8,128)} fusion(bf16[1,2,1,768,3072]{4,3,2,1,0:T(8,128)(2,1)} %param.9, bf16[256,768]{1,0:T(8,128)(2,1)S(1)} %bitcast_select_fusion.8, bf16[256,768]{1,0:T(8,128)(2,1)S(1)} %collective-permute-done.1, pred[]{:T(512)S(6)} %eq.9), kind=kOutput, calls=%fused_computation.37 | convolution fusion | flops 1208156160 | bytes 8650753 | tf_op jit(solution)/shard_map/dot_general | solution.py:22
  38.1 8.2 %multiply_reduce_fusion.1 = (f32[]{:T(128)}, bf16[256,768]{1,0:T(8,128)(2,1)}, bf16[256,768]{1,0:T(8,128)(2,1)S(1)}) fusion(bf16[8,32,768]{2,1,0:T(8,128)(2,1)S(1)} %get-tuple-element.42, bf16[1,2,1,3072,768]{4,3,2,1,0:T(8,128)(2,1)} %param.10, bf16[256,768]{1,0:T(8,128)(2,1)S(1)} %collective-permute-done.2, bf16[1,2,1,768,3072]{4,3,2,1,0:T(8,128)(2,1)} %param.9), kind=kOutput, calls=%fused_computation.204 | convolution fusion | flops 2424963072 | bytes 11403268 | tf_op jit(solution)/shard_map/dot_general | solution.py:22
  46.5 5.6 %fusion.256 = f32[256,3072]{1,0:T(8,128)} fusion(bf16[768,3072]{1,0:T(8,128)(2,1)} %bitcast_select_fusion.1, bf16[256,768]{1,0:T(8,128)(2,1)S(1)} %collective-permute-done.2, bf16[256,768]{1,0:T(8,128)(2,1)S(1)} %bitcast_select_fusion.8, pred[]{:T(512)S(6)} %eq.9), kind=kOutput, calls=%fused_computation.256 | convolution fusion | flops 1208156160 | bytes 8650753 | tf_op jit(solution)/shard_map/dot_general | solution.py:22
  52.1 1.3 broadcast_select_fusion.8
  53.3 5.4 %fusion.32 = f32[256,3072]{1,0:T(8,128)} fusion(bf16[256,768]{1,0:T(8,128)(2,1)S(1)} %get-tuple-element.38, bf16[1,2,1,768,3072]{4,3,2,1,0:T(8,128)(2,1)} %param.9), kind=kOutput, calls=%fused_computation.41 | convolution fusion | flops 1207959552 | bytes 8257536 | tf_op jit(solution)/shard_map/dot_general | solution.py:22
  58.8 3.1 fusion.10
  61.9 12.0 %fusion.170 = (bf16[256,3072]{1,0:T(8,128)(2,1)}, bf16[256,3072]{1,0:T(8,128)(2,1)}, bf16[256,3072]{1,0:T(8,128)(2,1)}, bf16[256,3072]{1,0:T(8,128)(2,1)}, f32[256,3072]{1,0:T(8,128)}) fusion(pred[]{:T(512)S(6)} %eq.9, f32[256,3072]{1,0:T(8,128)} %fusion.10, f32[256,3072]{1,0:T(8,128)} %fusion.256, f32[256,3072]{1,0:T(8,128)} %fusion.32, ...), kind=kOutput, calls=%fused_computation.168 | convolution fusion | flops 1246691328 | bytes 27526144 | tf_op jit(solution)/shard_map/dot_general | solution.py:22
  74.0 4.3 fusion.44
  78.3 1.4 fusion.189
  79.7 0.8 collective-permute-start.3
  80.5 1.4 collective-permute-done.3
  81.9 0.7 copy-done.12
  82.7 7.9 %broadcast_select_fusion.6 = (bf16[256,768]{1,0:T(8,128)(2,1)}, bf16[256,768]{1,0:T(8,128)(2,1)S(1)}, bf16[256,768]{1,0:T(8,128)(2,1)}) fusion(bf16[256,768]{1,0:T(8,128)(2,1)} %get-tuple-element.40, pred[]{:T(512)S(6)} %eq.9, bf16[256,768]{1,0:T(8,128)(2,1)} %copy-done.12, bf16[8,32,768]{2,1,0:T(8,128)(2,1)S(1)} %get-tuple-element.41, ...), kind=kOutput, calls=%fused_computation.218 | convolution fusion | flops 2424963072 | bytes 12582913 | tf_op jit(solution)/shard_map/dot_general | solution.py:22
  90.5 6.1 %fusion.51 = bf16[256,3072]{1,0:T(8,128)(2,1)S(1)} fusion(f32[256,3072]{1,0:T(8,128)} %fusion.10, bf16[256,768]{1,0:T(8,128)(2,1)S(1)} %get-tuple-element.23, bf16[1,2,1,3072,768]{4,3,2,1,0:T(8,128)(2,1)} %param.10), kind=kOutput, calls=%fused_computation.70 | convolution fusion | flops 1223688192 | bytes 9830400 | tf_op jit(solution)/shard_map/dot_general | solution.py:22
  96.7 4.4 %add_convert_fusion.2 = bf16[256,768]{1,0:T(8,128)(2,1)S(1)} fusion(bf16[256,768]{1,0:T(8,128)(2,1)S(1)} %get-tuple-element.23, bf16[256,3072]{1,0:T(8,128)(2,1)S(1)} %fusion.51, bf16[1,2,1,768,3072]{4,3,2,1,0:T(8,128)(2,1)} %param.9), kind=kOutput, calls=%fused_computation.207 | convolution fusion | flops 1208549376 | bytes 7077888 | tf_op jit(solution)/shard_map/dot_general | solution.py:22
  101.1 0.4 collective-permute-start.5
  101.5 1.4 collective-permute-done.5
  102.9 5.9 %fusion.58 = bf16[256,3072]{1,0:T(8,128)(2,1)S(1)} fusion(f32[256,3072]{1,0:T(8,128)S(1)} %copy-done.13, bf16[256,768]{1,0:T(8,128)(2,1)S(1)} %collective-permute-done.5, pred[]{:T(512)S(6)} %eq.9, bf16[1,2,1,3072,768]{4,3,2,1,0:T(8,128)(2,1)} %param.10), kind=kOutput, calls=%fused_computation.77 | convolution fusion | flops 1226047488 | bytes 14548993 | tf_op jit(solution)/shard_map/dot_general | solution.py:22
  108.9 2.2 add_convert_fusion.1
  111.1 0.5 collective-permute-start.6
  111.6 0.8 multiply_reduce_fusion
  113.8 6.5 %broadcast_select_fusion.2 = (bf16[256,3072]{1,0:T(8,128)(2,1)S(1)}, bf16[256,3072]{1,0:T(8,128)(2,1)S(1)}, bf16[256,3072]{1,0:T(8,128)(2,1)S(1)}, bf16[256,3072]{1,0:T(8,128)(2,1)S(1)}) fusion(bf16[256,3072]{1,0:T(8,128)(2,1)} %copy-done.21, bf16[256,3072]{1,0:T(8,128)(2,1)} %copy-done.20, pred[]{:T(512)S(6)} %eq.9, bf16[256,3072]{1,0:T(8,128)(2,1)} %copy-done.18, ...), kind=kOutput, calls=%fused_computation.176 | convolution fusion | flops 1226047488 | bytes 19267584 | tf_op jit(solution)/shard_map/dot_general | solution.py:22
  120.4 0.5 slice-done.5
  120.9 2.5 add_convert_fusion
  123.4 0.7 collective-permute-start.7
  124.1 0.6 fusion.219.loss_ref
  124.7 2.7 fusion.137
  127.4 1.1 broadcast_select_fusion.5
  128.6 2.7 fusion.141
  131.3 15.5 %pad_maximum_fusion.1 = f32[4608,8,128]{2,1,0:T(8,128)} fusion(f32[2304,8,128]{2,1,0:T(8,128)S(1)} %bitcast.209, f32[2304,8,128]{2,1,0:T(8,128)S(1)} %bitcast.201), kind=kLoop, calls=%fused_computation.1 | loop fusion | flops 4718592 | bytes 37748736 | tf_op jit(solution)/shard_map/concatenate | solution.py:411
  146.8 4.6 %fusion.149 = bf16[256,3072]{1,0:T(8,128)(2,1)S(1)} fusion(bf16[256,3072]{1,0:T(8,128)(2,1)S(1)} %copy-done.23, f32[256,3072]{1,0:T(8,128)} %fusion.28, bf16[256,768]{1,0:T(8,128)(2,1)S(1)} %collective-permute-done.7, bf16[1,2,1,3072,768]{4,3,2,1,0:T(8,128)(2,1)S(1)} %bitcast.223, pred[]{:T(512)S(6)} %eq.9), kind=kOutput, calls=%fused_computation.153 | convolution fusion | flops 1224474624 | bytes 11403265 | tf_op jit(solution)/shard_map/dot_general | solution.py:22
  151.5 2.7 fusion.129
  154.2 2.7 fusion.133
  156.9 15.6 %pad_maximum_fusion = f32[4608,8,128]{2,1,0:T(8,128)} fusion(f32[2304,8,128]{2,1,0:T(8,128)S(1)} %bitcast.210, f32[2304,8,128]{2,1,0:T(8,128)S(1)} %bitcast.202), kind=kLoop, calls=%fused_computation | loop fusion | flops 4718592 | bytes 37748736 | tf_op jit(solution)/shard_map/concatenate | solution.py:411
  172.5 246.3 %tail.1 = (f32[2,576,128]{2,1,0:T(8,128)}, f32[2,576,128]{2,1,0:T(8,128)}, f32[2,576,128]{2,1,0:T(8,128)}, f32[8,128]{1,0:T(8,128)}, bf16[2,4,4,4,72,8,128]{6,5,4,3,2,1,0:T(8,128)(2,1)}) custom-call(f32[4,4,4,72,8,128]{5,4,3,2,1,0:T(8,128)} %bitcast.200, f32[4,4,4,72,8,128]{5,4,3,2,1,0:T(8,128)} %bitcast.199, f32[2,576,128]{2,1,0:T(8,128)} %bitcast.217, ...), custom_call_target="tpu_custom_call" | custom-call | tf_op jit(solution)/shard_map/tail/pallas_call | solution.py:374
  418.8 1.2 slice.77
  420.0 14.6 %fusion.258 = (bf16[2,2,4,4,72,8,128]{6,5,4,3,2,1,0:T(8,128)(2,1)}, bf16[2,2,4,4,72,8,128]{6,5,4,3,2,1,0:T(8,128)(2,1)}) fusion(bf16[2,4,4,4,72,8,128]{6,5,4,3,2,1,0:T(8,128)(2,1)} %get-tuple-element.11), kind=kLoop, calls=%fused_computation.257 | loop fusion | bytes 37748736 | tf_op jit(solution)/shard_map/slice | solution.py:418
  435.3 0.8 copy.19
  436.1 0.8 copy.20
  436.9 0.8 copy.21
  (91 shorter events, 0.6 us)
Async XLA Ops:
  8.6 1.8 collective-permute-start
  17.2 6.7 %copy-start = (bf16[16,32,768]{2,1,0:T(8,128)(2,1)S(1)}, bf16[16,32,768]{2,1,0:T(8,128)(2,1)}, u32[]{:S(2)}) copy-start(bf16[16,32,768]{2,1,0:T(8,128)(2,1)} %param.8) | copy-start | bytes 2359300
  17.2 6.7 %collective-permute-start.1 = (bf16[256,768]{1,0:T(8,128)(2,1)S(1)}, bf16[256,768]{1,0:T(8,128)(2,1)S(1)}, u32[]{:S(2)}, u32[]{:S(2)}) collective-permute-start(bf16[256,768]{1,0:T(8,128)(2,1)S(1)} %add_convert_fusion.6), channel_id=1, source_target_pairs={{0,64},{64,0},{1,65},{65,1},{2,66},{66,2},{3,67},{67,3},{4,68},{68... | collective-permute-start | bytes 1179656 | tf_op jit(solution)/shard_map/ppermute | solution.py:65
  32.1 6.1 %collective-permute-start.2 = (bf16[256,768]{1,0:T(8,128)(2,1)S(1)}, bf16[256,768]{1,0:T(8,128)(2,1)S(1)}, u32[]{:S(2)}, u32[]{:S(2)}) collective-permute-start(bf16[256,768]{1,0:T(8,128)(2,1)S(1)} %add_convert_fusion.5), channel_id=1, source_target_pairs={{0,64},{64,0},{1,65},{65,1},{2,66},{66,2},{3,67},{67,3},{4,68},{68... | collective-permute-start | bytes 1179656 | tf_op jit(solution)/shard_map/ppermute | solution.py:65
  38.1 8.4 %copy-start.10 = (bf16[256,768]{1,0:T(8,128)(2,1)}, bf16[256,768]{1,0:T(8,128)(2,1)S(1)}, u32[]{:S(2)}) copy-start(bf16[256,768]{1,0:T(8,128)(2,1)S(1)} %collective-permute-done.2) | copy-start | bytes 1179652
  46.3 5.7 %collective-permute-start.4 = (bf16[256,768]{1,0:T(8,128)(2,1)S(1)}, bf16[256,768]{1,0:T(8,128)(2,1)S(1)}, u32[]{:S(2)}, u32[]{:S(2)}) collective-permute-start(bf16[256,768]{1,0:T(8,128)(2,1)S(1)} %get-tuple-element.49), channel_id=1, source_target_pairs={{0,64},{64,0},{1,65},{65,1},{2,66},{66,2},{3,67},{67,3},{4,68},{68... | collective-permute-start | bytes 1179656 | tf_op jit(solution)/shard_map/ppermute | solution.py:65
  46.5 12.3 %slice-start = ((s8[9437184]{0:T(1024)(128)(4,1)}), s8[4194304]{0:T(1024)(128)(4,1)S(1)}, s32[]{:S(2)}) async-start(s8[9437184]{0:T(1024)(128)(4,1)} %bitcast.203), calls=%async_computation | async-start | bytes 8388608
  46.5 12.3 %slice-start.1 = ((s8[9437184]{0:T(1024)(128)(4,1)}), s8[4194304]{0:T(1024)(128)(4,1)S(1)}, s32[]{:S(2)}) async-start(s8[9437184]{0:T(1024)(128)(4,1)} %bitcast.203), calls=%async_computation.1 | async-start | bytes 8388608
  52.1 9.8 %copy-start.9 = (bf16[256,768]{1,0:T(8,128)(2,1)}, bf16[256,768]{1,0:T(8,128)(2,1)S(1)}, u32[]{:S(2)}) copy-start(bf16[256,768]{1,0:T(8,128)(2,1)S(1)} %collective-permute-done.4) | copy-start | bytes 1179652
  53.3 5.5 %slice-start.2 = ((s8[9437184]{0:T(1024)(128)(4,1)}), s8[1048576]{0:T(1024)(128)(4,1)S(1)}, s32[]{:S(2)}) async-start(s8[9437184]{0:T(1024)(128)(4,1)} %bitcast.203), calls=%async_computation.2 | async-start | bytes 2097152
  58.8 3.1 copy-start.11
  58.8 15.1 %slice-start.8 = ((s8[9437184]{0:T(1024)(128)(4,1)}), s8[4194304]{0:T(1024)(128)(4,1)S(1)}, s32[]{:S(2)}) async-start(s8[9437184]{0:T(1024)(128)(4,1)} %bitcast.220), calls=%async_computation.8 | async-start | bytes 8388608
  61.9 12.1 %slice-start.9 = ((s8[9437184]{0:T(1024)(128)(4,1)}), s8[4194304]{0:T(1024)(128)(4,1)S(1)}, s32[]{:S(2)}) async-start(s8[9437184]{0:T(1024)(128)(4,1)} %bitcast.220), calls=%async_computation.9 | async-start | bytes 8388608
  61.9 12.1 %slice-start.10 = ((s8[9437184]{0:T(1024)(128)(4,1)}), s8[1048576]{0:T(1024)(128)(4,1)S(1)}, s32[]{:S(2)}) async-start(s8[9437184]{0:T(1024)(128)(4,1)} %bitcast.220), calls=%async_computation.10 | async-start | bytes 2097152
  61.9 12.1 %copy-start.24 = (bf16[256,768]{1,0:T(8,128)(2,1)S(1)}, bf16[256,768]{1,0:T(8,128)(2,1)}, u32[]{:S(2)}) copy-start(bf16[256,768]{1,0:T(8,128)(2,1)} %get-tuple-element.40) | copy-start | bytes 1179652
  78.3 1.4 copy-start.20
  79.7 2.2 collective-permute-start.3
  81.9 0.7 copy-start.12
  90.5 6.1 %copy-start.5 = (bf16[256,768]{1,0:T(8,128)(2,1)}, bf16[256,768]{1,0:T(8,128)(2,1)S(1)}, u32[]{:S(2)}) copy-start(bf16[256,768]{1,0:T(8,128)(2,1)S(1)} %get-tuple-element.23) | copy-start | bytes 1179652
  96.6 4.4 %copy-start.21 = (bf16[256,3072]{1,0:T(8,128)(2,1)}, bf16[256,3072]{1,0:T(8,128)(2,1)S(1)}, u32[]{:S(2)}) copy-start(bf16[256,3072]{1,0:T(8,128)(2,1)S(1)} %fusion.51) | copy-start | bytes 4718596
  96.6 6.3 %copy-start.13 = (f32[256,3072]{1,0:T(8,128)S(1)}, f32[256,3072]{1,0:T(8,128)}, u32[]{:S(2)}) copy-start(f32[256,3072]{1,0:T(8,128)} %fusion.256) | copy-start | bytes 9437188
  96.7 12.2 %slice-start.6 = ((s8[4718592]{0:T(1024)(128)(4,1)}), s8[4194304]{0:T(1024)(128)(4,1)S(1)}, s32[]{:S(2)}) async-start(s8[4718592]{0:T(1024)(128)(4,1)} %bitcast.211), calls=%async_computation.6 | async-start | bytes 8388608
  101.1 7.8 %slice-start.7 = ((s8[4718592]{0:T(1024)(128)(4,1)}), s8[524288]{0:T(1024)(128)(4,1)S(1)}, s32[]{:S(2)}) async-start(s8[4718592]{0:T(1024)(128)(4,1)} %bitcast.211), calls=%async_computation.7 | async-start | bytes 1048576
  101.1 1.8 collective-permute-start.5
  102.9 5.9 %copy-start.7 = (bf16[256,768]{1,0:T(8,128)(2,1)}, bf16[256,768]{1,0:T(8,128)(2,1)S(1)}, u32[]{:S(2)}) copy-start(bf16[256,768]{1,0:T(8,128)(2,1)S(1)} %collective-permute-done.5) | copy-start | bytes 1179652
  108.9 2.2 copy-start.18
  108.9 2.8 copy-start.4
  111.1 2.7 collective-permute-start.6
  113.8 6.6 %slice-start.3 = ((s8[9437184]{0:T(1024)(128)(4,1)}), s8[1048576]{0:T(1024)(128)(4,1)S(1)}, s32[]{:S(2)}) async-start(s8[9437184]{0:T(1024)(128)(4,1)} %bitcast.205), calls=%async_computation.3 | async-start | bytes 2097152
  113.8 6.6 %slice-start.4 = ((s8[9437184]{0:T(1024)(128)(4,1)}), s8[4194304]{0:T(1024)(128)(4,1)S(1)}, s32[]{:S(2)}) async-start(s8[9437184]{0:T(1024)(128)(4,1)} %bitcast.205), calls=%async_computation.4 | async-start | bytes 8388608
  113.8 7.1 %slice-start.5 = ((s8[9437184]{0:T(1024)(128)(4,1)}), s8[4194304]{0:T(1024)(128)(4,1)S(1)}, s32[]{:S(2)}) async-start(s8[9437184]{0:T(1024)(128)(4,1)} %bitcast.205), calls=%async_computation.5 | async-start | bytes 8388608
  120.4 3.0 copy-start.22
  123.4 4.0 collective-permute-start.7
  124.7 2.7 copy-start.6
  124.7 2.7 copy-start.8
  124.7 3.9 copy-start.16
  124.7 3.9 copy-start.17
  124.7 3.9 copy-start.19
  128.6 18.3 %slice-start.11 = ((s8[9437184]{0:T(1024)(128)(4,1)}), s8[4194304]{0:T(1024)(128)(4,1)S(1)}, s32[]{:S(2)}) async-start(s8[9437184]{0:T(1024)(128)(4,1)} %bitcast.222), calls=%async_computation.11 | async-start | bytes 8388608
  131.3 15.5 %slice-start.12 = ((s8[9437184]{0:T(1024)(128)(4,1)}), s8[4194304]{0:T(1024)(128)(4,1)S(1)}, s32[]{:S(2)}) async-start(s8[9437184]{0:T(1024)(128)(4,1)} %bitcast.222), calls=%async_computation.12 | async-start | bytes 8388608
  131.3 15.5 %slice-start.13 = ((s8[9437184]{0:T(1024)(128)(4,1)}), s8[1048576]{0:T(1024)(128)(4,1)S(1)}, s32[]{:S(2)}) async-start(s8[9437184]{0:T(1024)(128)(4,1)} %bitcast.222), calls=%async_computation.13 | async-start | bytes 2097152
  131.3 15.5 %copy-start.23 = (bf16[256,3072]{1,0:T(8,128)(2,1)S(1)}, bf16[256,3072]{1,0:T(8,128)(2,1)}, u32[]{:S(2)}) copy-start(bf16[256,3072]{1,0:T(8,128)(2,1)} %copy-done.22) | copy-start | bytes 4718596
  151.5 2.7 copy-start.14
  151.5 2.7 copy-start.15
  420.0 15.3 %copy-start.3 = (f32[2,576,128]{2,1,0:T(8,128)S(1)}, f32[2,576,128]{2,1,0:T(8,128)}, u32[]{:S(2)}) copy-start(f32[2,576,128]{2,1,0:T(8,128)} %get-tuple-element.12) | copy-start | bytes 1769476
  420.0 16.1 %copy-start.2 = (f32[2,576,128]{2,1,0:T(8,128)S(1)}, f32[2,576,128]{2,1,0:T(8,128)}, u32[]{:S(2)}) copy-start(f32[2,576,128]{2,1,0:T(8,128)} %get-tuple-element.13) | copy-start | bytes 1769476
  420.0 16.9 %copy-start.1 = (f32[2,576,128]{2,1,0:T(8,128)S(1)}, f32[2,576,128]{2,1,0:T(8,128)}, u32[]{:S(2)}) copy-start(f32[2,576,128]{2,1,0:T(8,128)} %get-tuple-element.14) | copy-start | bytes 1769476

commit v3 on v2

--- a/solution.py
+++ b/solution.py
@@ -14,114 +14,15 @@
 ADAM_STEP = 1000
 
 
-def gelu_tanh(pre_act):
-    return jax.nn.gelu(pre_act, approximate=True)
-
-
-def dot32(lhs, rhs, dims):
-    return lax.dot_general(lhs, rhs, (dims, ((), ())), preferred_element_type=jnp.float32)
-
-
-def to_tiles(mat):
-    rows, cols = mat.shape
-    return mat.reshape(rows // 8, 8, cols // 128, 128).transpose(0, 2, 1, 3).reshape(-1, 8, 128)
-
-
-def run_stack(x_all, t_all, w1_loc, w2_loc, n_tokens, n_chunk):
-    stage_idx = lax.axis_index("stage")
-    on_first = stage_idx == 0
-    n_rows, d_model = x_all.shape
-    n_tok = n_rows // n_chunk
-    n_items = 2 * n_chunk
-    n_ticks = n_items + 1
-    swap = [(0, 1), (1, 0)]
-
-    def weights(half_first, half_second):
-        if half_first == half_second:
-            return w1_loc[half_first], w2_loc[half_first]
-        return (jnp.where(on_first, w1_loc[half_first], w1_loc[half_second]),
-                jnp.where(on_first, w2_loc[half_first], w2_loc[half_second]))
-
-    def half_of(item, backward):
-        half = min(max(item, 0), n_items - 1) // n_chunk
-        return 1 - half if backward else half
-
-    x_in, pre_in, outs = [], [], []
-    recv = None
-    for tick in range(n_ticks):
-        fresh = x_all[tick * n_tok:(tick + 1) * n_tok] if tick < n_chunk else None
-        if recv is None:
-            h_cur = fresh
-        elif fresh is None:
-            h_cur = recv
-        else:
-            h_cur = jnp.where(on_first, fresh, recv)
-        w_one, w_two = weights(half_of(tick, False), half_of(tick - 1, False))
-        pre = dot32(h_cur, w_one, ((1,), (0,)))
-        act = gelu_tanh(pre).astype(jnp.bfloat16)
-        h_out = (h_cur.astype(jnp.float32) + dot32(act, w_two, ((1,), (0,)))).astype(jnp.bfloat16)
-        x_in.append(h_cur)
-        outs.append(h_out)
-        recv = lax.ppermute(h_out, "stage", swap)
-
-    loss_acc = jnp.zeros((), jnp.float32)
-    seeds = []
-    for chunk in range(n_chunk):
-        h_last = outs[n_chunk + chunk + 1]
-        residual = h_last.astype(jnp.float32) - t_all[chunk * n_tok:(chunk + 1) * n_tok].astype(jnp.float32)
-        loss_acc = loss_acc + 0.5 * jnp.sum(residual * residual)
-        seeds.append((residual / n_tokens).astype(jnp.bfloat16))
-    loss_acc = jnp.where(on_first, 0.0, loss_acc)
-
-    g_in, r_in, a_in = [], [], []
-    saved = []
-    recv = None
-    for tick in range(n_ticks):
-        fresh = seeds[tick] if tick < n_chunk else None
-        if recv is None:
-            grad = fresh
-        elif fresh is None:
-            grad = recv
-        else:
-            grad = jnp.where(on_first, recv, fresh)
-        first_item = min(max(tick - 1, 0), n_items - 1)
-        second_item = min(tick, n_items - 1)
-        w_one, w_two = weights(half_of(first_item, True), half_of(second_item, True))
-        first_tick = half_of(first_item, True) * n_chunk + first_item % n_chunk
-        second_tick = half_of(second_item, True) * n_chunk + second_item % n_chunk + 1
-        if first_tick == second_tick:
-            x_cur = x_in[first_tick]
-        else:
-            x_cur = jnp.where(on_first, x_in[first_tick], x_in[second_tick])
-        pre = dot32(x_cur, w_one, ((1,), (0,)))
-        act, pull = jax.vjp(gelu_tanh, pre)
-        r_cur = pull(dot32(grad, w_two, ((1,), (1,))))[0].astype(jnp.bfloat16)
-        back = (grad.astype(jnp.float32) + dot32(r_cur, w_one, ((1,), (1,)))).astype(jnp.bfloat16)
-        g_in.append(grad)
-        r_in.append(r_cur)
-        a_in.append(act.astype(jnp.bfloat16))
-        saved.append(x_cur)
-        if tick < n_ticks - 1:
-            recv = lax.ppermute(back, "stage", swap)
-
-    def pick(per_tick, half):
-        base = (1 - half) * n_chunk
-        return jnp.concatenate([jnp.where(on_first, per_tick[base + c + 1], per_tick[base + c]) for c in range(n_chunk)], axis=0)
-
-    grads = []
-    for half in (1, 0):
-        x_h, g_h, r_h, a_h = pick(saved, half), pick(g_in, half), pick(r_in, half), pick(a_in, half)
-        grads.append((dot32(x_h, r_h, ((0,), (0,))), dot32(a_h, g_h, ((0,), (0,)))))
-    return grads[1], grads[0], loss_acc
-
-
+TILE = (8, 128)
 TILES = 72
+VMEM_LIMIT = 60 * 1024 * 1024
 PART = 24
 ORDERS = ((2, 1, 0), (1, 0, 2), (0, 2, 1))
 MESH_ID = pl.DeviceIdType.MESH
 
 
-def tail_kernel(tau_clip, learn_rate, g0_ref, g1_ref, w_ref, m_ref, v_ref, loss_ref,
+def tail_kernel(tau_clip, learn_rate, g_ref, w_ref, m_ref, v_ref, loss_ref,
                 w_out, m_out, v_out, stat_out, full_out,
                 recv1, recv2, recv3, local, wbf, nbuf,
                 s1, r1, s2, r2, s3, r3, l_sem, own_sem, ns, nr,
@@ -130,7 +31,7 @@
     me = lax.axis_index("data")
     coords = (me // 16, (me // 4) % 4, me % 4)
     strides = (16, 4, 1)
-    g_refs = (g0_ref, g1_ref)
+    g_refs = (g_ref.at[0], g_ref.at[1])
     streams = [(k, d) for k in range(3) for d in range(2)]
 
     def peer(axis, delta):
@@ -366,30 +267,270 @@
             gather2(st, step).wait_send()
 
 
-def tail(g0, g1, w_flat, m_flat, v_flat, loss_tile, tau_clip, learn_rate):
-    flat = jax.ShapeDtypeStruct((2, 576, 128), jnp.float32)
+def tail(grads, w_flat, m_flat, v_flat, loss_tile, tau_clip, learn_rate):
+    f32, bf16 = jnp.float32, jnp.bfloat16
+    flat = jax.ShapeDtypeStruct(w_flat.shape, f32)
     in_vmem = pl.BlockSpec(memory_space=pltpu.VMEM)
     in_any = pl.BlockSpec(memory_space=pl.ANY)
     dma = pltpu.SemaphoreType.DMA
+    per_step = (6, 3)
+    per_sub = per_step + (4,)
+    part = (PART,) + TILE
     return pl.pallas_call(
         functools.partial(tail_kernel, tau_clip, learn_rate),
-        out_shape=(flat, flat, flat, jax.ShapeDtypeStruct((8, 128), jnp.float32), jax.ShapeDtypeStruct((2, 4, 4, 4, TILES, 8, 128), jnp.bfloat16)),
-        in_specs=[in_any] * 2 + [in_vmem] * 4,
+        out_shape=(flat, flat, flat, jax.ShapeDtypeStruct(TILE, f32), jax.ShapeDtypeStruct(grads.shape, bf16)),
+        in_specs=[in_any] + [in_vmem] * 4,
         out_specs=(in_vmem, in_vmem, in_vmem, in_vmem, in_any),
         scratch_shapes=[
-            pltpu.VMEM((6, 3, 4, 4, PART, 8, 128), jnp.float32),
-            pltpu.VMEM((6, 3, 4, PART, 8, 128), jnp.float32),
-            pltpu.VMEM((6, 3, PART, 8, 128), jnp.float32),
-            pltpu.VMEM((6, 2, 4, PART, 8, 128), jnp.float32),
-            pltpu.VMEM((2, TILES, 8, 128), jnp.bfloat16),
-            pltpu.VMEM((4, 4, 2, 8, 128), jnp.float32),
-            dma((6, 3, 4)), dma((6, 3, 4)), dma((6, 3)), dma((6, 3)), dma((6, 3)), dma((6, 3)),
-            dma((6, 2)), dma((6,)), dma((4, 4)), dma((4, 4)),
-            dma((6, 3)), dma((6, 3)), dma((6, 3)), dma((6, 3)), dma((6, 3, 4)), dma((6, 3, 4)),
+            pltpu.VMEM(per_sub + (4,) + part, f32),
+            pltpu.VMEM(per_sub + part, f32),
+            pltpu.VMEM(per_step + part, f32),
+            pltpu.VMEM((6, 2, 4) + part, f32),
+            pltpu.VMEM((2, TILES) + TILE, bf16),
+            pltpu.VMEM((4, 4, 2) + TILE, f32),
+            *[dma(per_sub)] * 2, *[dma(per_step)] * 4,
+            dma((6, 2)), dma((6,)), *[dma((4, 4))] * 2,
+            *[dma(per_step)] * 4, *[dma(per_sub)] * 2,
         ],
-        compiler_params=pltpu.CompilerParams(collective_id=1, has_side_effects=True, vmem_limit_bytes=60 * 1024 * 1024),
+        compiler_params=pltpu.CompilerParams(collective_id=1, has_side_effects=True, vmem_limit_bytes=VMEM_LIMIT),
         name="tail",
-    )(g0, g1, w_flat, m_flat, v_flat, loss_tile)
+    )(grads, w_flat, m_flat, v_flat, loss_tile)
+
+
+ROWS = 256
+GELU_K = math.sqrt(2.0 / math.pi)
+GELU_C = 0.044715
+
+
+def stack_kernel(n_tokens, x_hbm, t_hbm, w1_hbm, w2_hbm, g_out, loss_out,
+                 w1, w2, xs, gs, us, acts, rs, outf, outb, tgt, stage1, stage2,
+                 w1_sem, w2_sem, x_sem, t_sem, xsend, xrecv, gsend, grecv, o1_sem, o2_sem):
+    stage = lax.axis_index("stage")
+    me = lax.axis_index("data")
+    partner = (1 - stage, me)
+    n_half, d_model, d_ff = w1.shape
+
+    def load_w1(h):
+        return pltpu.make_async_copy(w1_hbm.at[h], w1.at[h], w1_sem.at[h])
+
+    def load_w2(h):
+        return pltpu.make_async_copy(w2_hbm.at[h], w2.at[h], w2_sem.at[h])
+
+    load_x = pltpu.make_async_copy(x_hbm, xs.at[0], x_sem)
+    load_t = pltpu.make_async_copy(t_hbm, tgt, t_sem)
+
+    @pl.when(stage == 0)
+    def _():
+        load_x.start()
+
+    load_w1(0).start()
+    load_w2(0).start()
+    load_w1(1).start()
+    load_w2(1).start()
+    load_t.start()
+
+    barrier = pltpu.get_barrier_semaphore()
+    pl.semaphore_signal(barrier, inc=1, device_id=partner, device_id_type=MESH_ID)
+    pl.semaphore_wait(barrier, 1)
+
+    @pl.when(stage == 0)
+    def _():
+        load_x.wait()
+
+    loss_out[...] = jnp.zeros((8, 128), jnp.float32)
+
+    def dot(lhs, rhs, on_left, on_right):
+        return lax.dot_general(lhs, rhs, (((on_left,), (on_right,)), ((), ())), preferred_element_type=jnp.float32)
+
+    def rows_of(c):
+        return pl.ds(pl.multiple_of(c * ROWS, ROWS), ROWS)
+
+    def block(i, size):
+        return pl.ds(pl.multiple_of(i * size, size), size)
+
+    def send_x(h, c):
+        return pltpu.make_async_remote_copy(src_ref=outf.at[h, c], dst_ref=xs.at[h + stage, rows_of(c)], send_sem=xsend.at[h, c], recv_sem=xrecv.at[h + stage, c], device_id=partner, device_id_type=MESH_ID)
+
+    def wait_x(h, c):
+        pltpu.make_async_remote_copy(src_ref=outf.at[h, c], dst_ref=xs.at[h, rows_of(c)], send_sem=xsend.at[h, c], recv_sem=xrecv.at[h, c], device_id=partner, device_id_type=MESH_ID).wait_recv()
+
+    def send_g(h, c):
+        to = h - 1 + stage
+        return pltpu.make_async_remote_copy(src_ref=outb.at[h, c], dst_ref=gs.at[to, rows_of(c)], send_sem=gsend.at[h, c], recv_sem=grecv.at[to, c], device_id=partner, device_id_type=MESH_ID)
+
+    def wait_g(h, c):
+        pltpu.make_async_remote_copy(src_ref=outb.at[h, c], dst_ref=gs.at[h, rows_of(c)], send_sem=gsend.at[h, c], recv_sem=grecv.at[h, c], device_id=partner, device_id_type=MESH_ID).wait_recv()
+
+    def forward(item, carry):
+        h, c = item // 2, item % 2
+        rows = rows_of(c)
+
+        @pl.when(c == 0)
+        def _():
+            load_w1(h).wait()
+            load_w2(h).wait()
+
+        @pl.when(h + stage > 0)
+        def _():
+            wait_x(h, c)
+
+        def up(f, inner):
+            cols = block(f, 512)
+            pre = dot(xs[h, rows, :], w1[h, :, cols], 1, 0)
+            us[h, rows, cols] = pre
+            cdf = 0.5 * (1.0 + jnp.tanh(GELU_K * (pre + GELU_C * (pre * pre * pre))))
+            acts[h, rows, cols] = (pre * cdf).astype(jnp.bfloat16)
+            return inner
+
+        lax.fori_loop(0, d_ff // 512, up, 0)
+
+        def down(n, inner):
+            cols = block(n, 256)
+            val = dot(acts[h, rows, :], w2[h, :, cols], 1, 0)
+            outf[h, c, :, cols] = (xs[h, rows, cols].astype(jnp.float32) + val).astype(jnp.bfloat16)
+            return inner
+
+        lax.fori_loop(0, d_model // 256, down, 0)
+
+        @pl.when(h + stage < 2)
+        def _():
+            send_x(h, c).start()
+
+        @pl.when(h + stage == 2)
+        def _():
+            @pl.when(c == 0)
+            def _():
+                load_t.wait()
+
+            residual = outf[h, c].astype(jnp.float32) - tgt[rows, :].astype(jnp.float32)
+            gs[h, rows, :] = (residual / n_tokens).astype(jnp.bfloat16)
+            square = residual * residual
+            part = sum(square[:, 128 * j:128 * (j + 1)] for j in range(d_model // 128))
+            loss_out[...] += 0.5 * jnp.sum(part.reshape(ROWS // 8, 8, 128), axis=0)
+
+        return carry
+
+    lax.fori_loop(0, 2 * n_half, forward, 0)
+
+    @pl.when(stage == 0)
+    def _():
+        load_t.wait()
+
+    def out_one(h, n, i):
+        return pltpu.make_async_copy(stage1.at[n % 2, i], g_out.at[h, pl.ds(0, 32), pl.ds(i * 24 + 2 * n, 2)], o1_sem.at[n % 2, i])
+
+    def out_two(h, m):
+        return pltpu.make_async_copy(stage2.at[m % 2], g_out.at[h, pl.ds(32 + 4 * m, 4)], o2_sem.at[m % 2])
+
+    def backward(b, carry):
+        h = 1 - b
+
+        def chain(c, inner):
+            rows = rows_of(c)
+
+            @pl.when(h + stage < 2)
+            def _():
+                wait_g(h, c)
+
+            def up(f, deep):
+                cols = block(f, 512)
+                q = dot(gs[h, rows, :], w2[h, cols, :], 1, 1)
+                pre = us[h, rows, cols]
+                square = pre * pre
+                th = jnp.tanh(GELU_K * (pre + GELU_C * (square * pre)))
+                slope = 0.5 * (1.0 + th) + 0.5 * pre * (1.0 - th * th) * (GELU_K * (1.0 + 3.0 * GELU_C * square))
+                rs[rows, cols] = (q * slope).astype(jnp.bfloat16)
+                return deep
+
+            lax.fori_loop(0, d_ff // 512, up, 0)
+
+            @pl.when(h + stage > 0)
+            def _():
+                def down(n, deep):
+                    cols = block(n, 256)
+                    val = dot(rs[rows, :], w1[h, cols, :], 1, 1)
+                    outb[h, c, :, cols] = (gs[h, rows, cols].astype(jnp.float32) + val).astype(jnp.bfloat16)
+                    return deep
+
+                lax.fori_loop(0, d_model // 256, down, 0)
+                send_g(h, c).start()
+
+            return inner
+
+        lax.fori_loop(0, 2, chain, 0)
+
+        def grad_one(n, inner):
+            @pl.when(b * 12 + n >= 2)
+            def _():
+                for i in range(3):
+                    out_one(h, n, i).wait()
+
+            val = dot(xs[h], rs[:, block(n, 256)], 0, 0)
+            for p in range(32):
+                for i in range(3):
+                    for j in range(2):
+                        stage1[n % 2, i, p, j] = val[p * 24 + i * 8:p * 24 + i * 8 + 8, 128 * j:128 * (j + 1)]
+            for i in range(3):
+                out_one(h, n, i).start()
+            return inner
+
+        lax.fori_loop(0, d_ff // 256, grad_one, 0)
+
+        def grad_two(m, inner):
+            @pl.when(b * 8 + m >= 2)
+            def _():
+                out_two(h, m).wait()
+
+            val = dot(acts[h, :, block(m, 384)], gs[h], 0, 0)
+            for p in range(4):
+                for i in range(12):
+                    for j in range(6):
+                        stage2[m % 2, p, i * 6 + j] = val[p * 96 + i * 8:p * 96 + i * 8 + 8, 128 * j:128 * (j + 1)]
+            out_two(h, m).start()
+            return inner
+
+        lax.fori_loop(0, d_ff // 384, grad_two, 0)
+        return carry
+
+    lax.fori_loop(0, n_half, backward, 0)
+    for n in range(2):
+        for i in range(3):
+            out_one(0, n, i).wait()
+        out_two(0, n).wait()
+
+    for h in range(2):
+        for c in range(2):
+            @pl.when(h + stage < 2)
+            def _():
+                send_x(h, c).wait_send()
+
+            @pl.when(h + stage > 0)
+            def _():
+                send_g(h, c).wait_send()
+
+
+def stack(x_all, t_all, w1, w2, n_tokens):
+    rows, d_model = x_all.shape
+    d_ff = w1.shape[2]
+    bf16, f32 = jnp.bfloat16, jnp.float32
+    dma = pltpu.SemaphoreType.DMA
+    in_any = pl.BlockSpec(memory_space=pl.ANY)
+    return pl.pallas_call(
+        functools.partial(stack_kernel, n_tokens),
+        out_shape=(jax.ShapeDtypeStruct((2, 64, TILES, 8, 128), f32), jax.ShapeDtypeStruct((8, 128), f32)),
+        in_specs=[in_any] * 4,
+        out_specs=(in_any, pl.BlockSpec(memory_space=pltpu.VMEM)),
+        scratch_shapes=[
+            pltpu.VMEM((2, d_model, d_ff), bf16), pltpu.VMEM((2, d_ff, d_model), bf16),
+            pltpu.VMEM((2, rows, d_model), bf16), pltpu.VMEM((2, rows, d_model), bf16),
+            pltpu.VMEM((2, rows, d_ff), f32), pltpu.VMEM((2, rows, d_ff), bf16), pltpu.VMEM((rows, d_ff), bf16),
+            pltpu.VMEM((2, 2, ROWS, d_model), bf16), pltpu.VMEM((2, 2, ROWS, d_model), bf16), pltpu.VMEM((rows, d_model), bf16),
+            pltpu.VMEM((2, 3, 32, 2, 8, 128), f32), pltpu.VMEM((2, 4, TILES, 8, 128), f32),
+            dma((2,)), dma((2,)), dma, dma, *[dma((2, 2))] * 4, dma((2, 3)), dma((2,)),
+        ],
+        compiler_params=pltpu.CompilerParams(collective_id=0, has_side_effects=True, vmem_limit_bytes=VMEM_LIMIT),
+        name="stack",
+    )(x_all, t_all, w1, w2)
 
 
 def solution(mesh):
@@ -405,14 +546,9 @@
         learn_rate = 0.1 / math.sqrt(4.0 * d_model * n_blocks)
         x_all = x_loc.reshape(n_micro * n_tok, d_model)
         t_all = t_loc.reshape(n_micro * n_tok, d_model)
-        grad_zero, grad_one, loss_acc = run_stack(x_all, t_all, w1_loc[0, :, 0], w2_loc[0, :, 0], n_tokens, 2)
-
-        def whole(pair):
-            return jnp.concatenate([to_tiles(pair[0]), to_tiles(pair[1])], axis=0).reshape(4, 4, 4, TILES, 8, 128)
-
-        loss_tile = jnp.where(lax.broadcasted_iota(jnp.int32, (8, 128), 0) + lax.broadcasted_iota(jnp.int32, (8, 128), 1) == 0, loss_acc, 0.0)
+        grads, loss_tile = stack(x_all, t_all, w1_loc[0, :, 0], w2_loc[0, :, 0], n_tokens)
         w_new, m_new, v_new, stat, w_full = tail(
-            whole(grad_zero), whole(grad_one), wm_loc.reshape(2, 576, 128), m_loc.reshape(2, 576, 128), v_loc.reshape(2, 576, 128),
+            grads.reshape(2, 4, 4, 4, TILES, 8, 128), wm_loc.reshape(2, 576, 128), m_loc.reshape(2, 576, 128), v_loc.reshape(2, 576, 128),
             loss_tile, tau_clip, learn_rate)
         w1_new = w_full[:, :2].reshape(2, d_model // 8, d_ff // 128, 8, 128).transpose(0, 1, 3, 2, 4).reshape(1, 2, 1, d_model, d_ff)
         w2_new = w_full[:, 2:].reshape(2, d_ff // 8, d_model // 128, 8, 128).transpose(0, 1, 3, 2, 4).reshape(1, 2, 1, d_ff, d_model)

time: 447 us -> 354 us (0.79); the launches traced: 439 us -> 354 us
  matrix products: 118 us -> 0 us
  Pallas kernels: 246 us -> 334 us
  other arithmetic: 41.5 us -> 0 us
  waiting for transfers between devices: 4.5 us -> 0 us
    dot_general x23 -> x0, matrix products: 118 us -> none  [dot32(): lax.dot_general(lhs, rhs, (dims, ((), ())), preferred_element_type=jnp.fl...]
    pallas_call x0 -> x1, Pallas kernels: none -> 89.9 us  [stack(): pl.pallas_call(functools.partial(stack_kernel, n_tokens), out_shape=(jax....]
    concatenate x2 -> x0, other arithmetic: 31.1 us -> none  [whole(): jnp.concatenate([to_tiles(pair[0]), to_tiles(pair[1])], axis=0)]
    select_n x6 -> x0, other arithmetic: 9.57 us -> none  [the longest x1 6.47 us: weights(): jnp.where(on_first, w1_loc[half_first], w1_loc[half_second])]
    ppermute x8 -> x0, waiting for transfers between devices: 4.5 us -> none  [the longest x4 2.79 us: run_stack(): recv = lax.ppermute(back, 'stage', swap)]
  transfers between devices with their start and end apart: 8 -> 0, of which waited for: 3 -> 0; matrix products, arithmetic and copies ran while one was open for 5% -> 0% of each run, Pallas kernels for 0% -> 0%
where the time goes in v3:
time: 354 us
  Pallas kernels  334 us (94%)
  local copies, waits for them, and re-layouts  18.2 us (5%)
    pallas_call x1, Pallas kernels, tail(): pl.pallas_call(functools.partial(tail_kernel, tau_clip, learn_rate), out_...  244 us
    pallas_call x1, Pallas kernels, stack(): pl.pallas_call(functools.partial(stack_kernel, n_tokens), out_shape=(jax....  89.9 us
    slice x1, local copies, waits for them, and re-layouts, device_step(): w_full[:, 2:].reshape(2, d_ff // 8, d_model // 128, 8, 128)  14.6 us

profile of v3, /device:TPU:0, one launch (start us, length us, event | category | flops | bytes accessed | tf_op | source)
XLA Modules:
  0.0 354.2 jit_solution(2345218395451889437)
XLA Ops:
  0.6 89.9 %stack.1 = (f32[2,64,72,8,128]{4,3,2,1,0:T(8,128)}, f32[8,128]{1,0:T(8,128)}) custom-call(bf16[512,768]{1,0:T(8,128)(2,1)} %bitcast.27, bf16[512,768]{1,0:T(8,128)(2,1)} %bitcast.28, bf16[2,768,3072]{2,1,0:T(8,128)(2,1)} %bitcast.23, bf16[2,3072,768]{2,1,0:T(8,128)(2,1)} %bitcast.24), custom_call_target="tpu_custom_call" | custom-call | tf_op jit(solution)/shard_map/stack/pallas_call | solution.py:518
  90.5 243.7 %tail.1 = (f32[2,576,128]{2,1,0:T(8,128)}, f32[2,576,128]{2,1,0:T(8,128)}, f32[2,576,128]{2,1,0:T(8,128)}, f32[8,128]{1,0:T(8,128)}, bf16[2,4,4,4,72,8,128]{6,5,4,3,2,1,0:T(8,128)(2,1)}) custom-call(f32[2,4,4,4,72,8,128]{6,5,4,3,2,1,0:T(8,128)} %bitcast.22, f32[2,576,128]{2,1,0:T(8,128)} %bitcast.32, f32[2,576,128]{2,1,0:T(8,128)} %bitcast.33, ...), custom_call_target="tpu_custom_call" | custom-call | tf_op jit(solution)/shard_map/tail/pallas_call | solution.py:279
  334.2 1.2 slice.11
  336.0 0.0 copy-start.2
  336.1 0.0 copy-start.1
  336.1 0.0 copy-start
  336.1 14.6 %fusion = (bf16[2,2,4,4,72,8,128]{6,5,4,3,2,1,0:T(8,128)(2,1)}, bf16[2,2,4,4,72,8,128]{6,5,4,3,2,1,0:T(8,128)(2,1)}) fusion(bf16[2,4,4,4,72,8,128]{6,5,4,3,2,1,0:T(8,128)(2,1)} %get-tuple-element.15), kind=kLoop, calls=%fused_computation | loop fusion | bytes 37748736 | tf_op jit(solution)/shard_map/slice | solution.py:554
  350.7 0.0 copy-done.2
  350.7 0.8 copy.19
  351.5 0.0 copy-done.1
  351.5 0.8 copy.20
  352.3 0.0 copy-done
  352.3 0.8 copy.21
Async XLA Ops:
  336.0 14.6 %copy-start.2 = (f32[2,576,128]{2,1,0:T(8,128)S(1)}, f32[2,576,128]{2,1,0:T(8,128)}, u32[]{:S(2)}) copy-start(f32[2,576,128]{2,1,0:T(8,128)} %get-tuple-element.16) | copy-start | bytes 1769476
  336.1 15.4 %copy-start.1 = (f32[2,576,128]{2,1,0:T(8,128)S(1)}, f32[2,576,128]{2,1,0:T(8,128)}, u32[]{:S(2)}) copy-start(f32[2,576,128]{2,1,0:T(8,128)} %get-tuple-element.17) | copy-start | bytes 1769476
  336.1 16.2 %copy-start = (f32[2,576,128]{2,1,0:T(8,128)S(1)}, f32[2,576,128]{2,1,0:T(8,128)}, u32[]{:S(2)}) copy-start(f32[2,576,128]{2,1,0:T(8,128)} %get-tuple-element.18) | copy-start | bytes 1769476

commit v4 on v3

--- a/solution.py
+++ b/solution.py
@@ -19,27 +19,54 @@
 VMEM_LIMIT = 60 * 1024 * 1024
 PART = 24
 ORDERS = ((2, 1, 0), (1, 0, 2), (0, 2, 1))
+HALF_PART = PART // 2
+STREAMS = tuple((h, k, d) for h in (1, 0) for k in range(3) for d in range(2))
+EARLY = len(STREAMS) // 2
 MESH_ID = pl.DeviceIdType.MESH
 
 
-def tail_kernel(tau_clip, learn_rate, g_ref, w_ref, m_ref, v_ref, loss_ref,
-                w_out, m_out, v_out, stat_out, full_out,
-                recv1, recv2, recv3, local, wbf, nbuf,
-                s1, r1, s2, r2, s3, r3, l_sem, own_sem, ns, nr,
-                t1, q1, t2, q2, t3, q3):
+def torus():
     stage = lax.axis_index("stage")
     me = lax.axis_index("data")
     coords = (me // 16, (me // 4) % 4, me % 4)
     strides = (16, 4, 1)
-    g_refs = (g_ref.at[0], g_ref.at[1])
-    streams = [(k, d) for k in range(3) for d in range(2)]
-
-    def peer(axis, delta):
-        moved = lax.rem(coords[axis] + delta + 4, 4)
-        return (stage, me + (moved - coords[axis]) * strides[axis])
 
     def ring(axis, delta):
         return lax.rem(coords[axis] + delta + 8, 4)
+
+    def peer(axis, delta):
+        return (stage, me + (ring(axis, delta) - coords[axis]) * strides[axis])
+
+    return stage, me, coords, ring, peer
+
+
+def sgn(d):
+    return 1 - 2 * d
+
+
+def pick(k, on_a, on_b, on_c):
+    index = [on_a] * 3
+    index[ORDERS[k][1]], index[ORDERS[k][2]] = on_b, on_c
+    return tuple(index)
+
+
+def remote(src, dst, send_sem, recv_sem, target):
+    return pltpu.make_async_remote_copy(src_ref=src, dst_ref=dst, send_sem=send_sem, recv_sem=recv_sem, device_id=target, device_id_type=MESH_ID)
+
+
+def grad_view(g_ref, stream, ring, turns, i):
+    h, k, d = stream
+    on_a, on_b = ring(ORDERS[k][0], -sgn(d) * turns), ring(ORDERS[k][1], -sgn(d) * (1 + i))
+    return g_ref.at[(h,) + pick(k, on_a, on_b, slice(None)) + (pl.ds(PART * k + HALF_PART * d, HALF_PART),)]
+
+
+def tail_kernel(tau_clip, learn_rate, g_ref, early_ref, w_ref, m_ref, v_ref, loss_ref,
+                w_out, m_out, v_out, stat_out, full_out,
+                recv1, recv2, recv3, local, wbf, nbuf,
+                s1, r1, s2, r2, s3, r3, l_sem, e_sem, own_sem, ns, nr,
+                t1, q1, t2, q2, t3, q3):
+    stage, me, coords, ring, peer = torus()
+    streams = [(k, d) for k in range(3) for d in range(2)]
 
     barrier = pltpu.get_barrier_semaphore()
     for axis in range(3):
@@ -48,32 +75,19 @@
     pl.semaphore_signal(barrier, inc=1, device_id=(1 - stage, me), device_id_type=MESH_ID)
     pl.semaphore_wait(barrier, 10)
 
-    def sgn(d):
-        return 1 if d == 0 else -1
-
-    def pick(k, on_a, on_b, on_c):
-        index = [None] * 3
-        index[ORDERS[k][0]], index[ORDERS[k][1]], index[ORDERS[k][2]] = on_a, on_b, on_c
-        return tuple(index)
-
-    def remote(src, dst, send_sem, recv_sem, target):
-        return pltpu.make_async_remote_copy(src_ref=src, dst_ref=dst, send_sem=send_sem, recv_sem=recv_sem, device_id=target, device_id_type=MESH_ID)
-
-    def grad_part(st, on_a, on_b):
-        k, d = streams[st]
-        return g_refs[d].at[pick(k, on_a, on_b, slice(None)) + (pl.ds(PART * k, PART),)]
-
-    def sub_of(st, i):
-        k, d = streams[st]
-        return ring(ORDERS[k][1], -sgn(d) * (1 + i))
-
     def next_of(st, phase):
-        k, d = streams[st]
+        h, k, d = STREAMS[st]
         return peer(ORDERS[k][phase], sgn(d))
 
+    def back_of(st, phase, turns):
+        h, k, d = STREAMS[st]
+        return ring(ORDERS[k][phase], -sgn(d) * turns)
+
     def first_send(st, i):
-        k, d = streams[st]
-        return remote(grad_part(st, ring(ORDERS[k][0], -sgn(d)), sub_of(st, i)), recv1.at[st, 0, i], s1.at[st, 0, i], r1.at[st, 0, i], next_of(st, 0))
+        return remote(grad_view(g_ref, STREAMS[st], ring, 1, i), recv1.at[st, 0, i], s1.at[st, 0, i], r1.at[st, 0, i], next_of(st, 0))
+
+    def first_load(st, i):
+        return pltpu.make_async_copy(early_ref.at[st, i], recv1.at[st, 0, i], e_sem.at[st, i])
 
     def forward1(st, step, i):
         return remote(recv1.at[st, step, i], recv1.at[st, step + 1, i], s1.at[st, step + 1, i], r1.at[st, step + 1, i], next_of(st, 0))
@@ -82,45 +96,50 @@
         return remote(recv1.at[st, step, i], recv1.at[st, step, i], s1.at[st, step, i], r1.at[st, step, i], next_of(st, 0))
 
     def fetch(st, n):
-        k, d = streams[st]
-        step, i = n // 4, n % 4
-        return pltpu.make_async_copy(grad_part(st, ring(ORDERS[k][0], -sgn(d) * (2 + step)), sub_of(st, i)), local.at[st, n % 2], l_sem.at[st, n % 2])
+        return pltpu.make_async_copy(grad_view(g_ref, STREAMS[st], ring, 2 + n // 4, n % 4), local.at[st, n % 2], l_sem.at[st, n % 2])
 
     def send2(st, step):
         src = recv1.at[st, 2, 0] if step == 0 else recv2.at[st, step - 1]
         return remote(src, recv2.at[st, step], s2.at[st, step], r2.at[st, step], next_of(st, 1))
 
     def send3(st, step):
-        k, d = streams[st]
-        src = recv2.at[st, 2, ring(ORDERS[k][2], -sgn(d))] if step == 0 else recv3.at[st, step - 1]
+        src = recv2.at[st, 2, back_of(st, 2, 1)] if step == 0 else recv3.at[st, step - 1]
         return remote(src, recv3.at[st, step], s3.at[st, step], r3.at[st, step], next_of(st, 2))
 
-    all_st = range(6)
-    for st in all_st:
-        for n in range(2):
-            fetch(st, n).start()
+    all_st = range(len(STREAMS))
+    early, late = all_st[:EARLY], all_st[EARLY:]
     for i in range(4):
-        for st in all_st:
+        for st in early:
+            first_load(st, i).start()
+        for st in late:
             first_send(st, i).start()
-
-    def accumulate(st, step, i, n, more):
-        arrived1(st, step, i).wait_recv()
+        if i == 0:
+            for st in all_st:
+                for n in range(2):
+                    fetch(st, n).start()
+
+    def accumulate(st, step, i, more):
+        n = step * 4 + i
+        if step == 0 and st < EARLY:
+            first_load(st, i).wait()
+        else:
+            arrived1(st, step, i).wait_recv()
         fetch(st, n).wait()
         recv1[st, step, i] = recv1[st, step, i] + local[st, n % 2]
         if more:
             fetch(st, n + 2).start()
 
-    def phase1(n, carry):
-        step, i = n // 4, n % 4
-        for st in all_st:
-            accumulate(st, step, i, n, True)
-            forward1(st, step, i).start()
-        return carry
-
-    lax.fori_loop(0, 8, phase1, 0)
+    for step in range(2):
+        def phase1(i, carry):
+            for st in all_st:
+                accumulate(st, step, i, True)
+                forward1(st, step, i).start()
+            return carry
+
+        lax.fori_loop(0, 4, phase1, 0)
     for i in range(4):
         for st in all_st:
-            accumulate(st, 2, i, 8 + i, i < 2)
+            accumulate(st, 2, i, i < 2)
             if i == 0:
                 send2(st, 0).start()
         if i > 0:
@@ -133,9 +152,8 @@
                     send3(st, 0).start()
     for step in range(3):
         for st in all_st:
-            k, d = streams[st]
             send3(st, step).wait_recv()
-            recv3[st, step] = recv3[st, step] + recv2[st, 2, ring(ORDERS[k][2], -sgn(d) * (2 + step))]
+            recv3[st, step] = recv3[st, step] + recv2[st, 2, back_of(st, 2, 2 + step)]
             if step < 2:
                 send3(st, step + 1).start()
 
@@ -171,7 +189,7 @@
             for h in range(2):
                 for t in range(PART):
                     rows = pl.ds(k * 192 + (t // width) * (8 * width) + t % width, 8, stride=width)
-                    grad = clip * recv3[2 * k + h, 2, t]
+                    grad = clip * recv3[(1 - h) * EARLY + 2 * k + t // HALF_PART, 2, t % HALF_PART]
                     m_new = BETA_ONE * m_ref[h, rows, :] + (1.0 - BETA_ONE) * grad
                     v_new = BETA_TWO * v_ref[h, rows, :] + (1.0 - BETA_TWO) * grad * grad
                     m_hat = m_new / (1.0 - BETA_ONE ** ADAM_STEP)
@@ -198,6 +216,10 @@
         k, d = streams[st]
         return full_out.at[(d,) + pick(k, on_a, on_b, on_c) + (pl.ds(PART * k, PART),)]
 
+    def along(st, phase):
+        k, d = streams[st]
+        return peer(ORDERS[k][phase], sgn(d))
+
     def coord_of(st, phase, delta):
         k, d = streams[st]
         return ring(ORDERS[k][phase], -sgn(d) * delta)
@@ -206,34 +228,34 @@
         k, d = streams[st]
         place = full_part(st, coord_of(st, 0, 0), coord_of(st, 1, 0), coord_of(st, 2, step))
         src = wbf.at[d, pl.ds(PART * k, PART)] if step == 0 else place
-        return remote(src, place, t1.at[st, step], q1.at[st, step], next_of(st, 2))
+        return remote(src, place, t1.at[st, step], q1.at[st, step], along(st, 2))
 
     def gather2(st, step):
         place = full_part(st, coord_of(st, 0, 0), coord_of(st, 1, step), slice(None))
-        return remote(place, place, t2.at[st, step], q2.at[st, step], next_of(st, 1))
+        return remote(place, place, t2.at[st, step], q2.at[st, step], along(st, 1))
 
     def gather3(st, step, i):
         place = full_part(st, coord_of(st, 0, step), coord_of(st, 1, i), slice(None))
-        return remote(place, place, t3.at[st, step, i], q3.at[st, step, i], next_of(st, 0))
+        return remote(place, place, t3.at[st, step, i], q3.at[st, step, i], along(st, 0))
 
     def own(st):
         k, d = streams[st]
         return pltpu.make_async_copy(wbf.at[d, pl.ds(PART * k, PART)], full_part(st, coord_of(st, 0, 0), coord_of(st, 1, 0), coord_of(st, 2, 0)), own_sem.at[st])
 
-    for st in all_st:
+    for st in range(6):
         gather1(st, 0).start()
         own(st).start()
     for step in range(3):
-        for st in all_st:
+        for st in range(6):
             gather1(st, step).wait_recv()
             if step < 2:
                 gather1(st, step + 1).start()
-    for st in all_st:
+    for st in range(6):
         own(st).wait()
         gather2(st, 0).start()
         gather3(st, 0, 0).start()
     for step in range(3):
-        for st in all_st:
+        for st in range(6):
             gather2(st, step).wait_recv()
             if step < 2:
                 gather2(st, step + 1).start()
@@ -241,60 +263,65 @@
 
     def phase3(n, carry):
         step, i = n // 4, n % 4
-        for st in all_st:
+        for st in range(6):
             gather3(st, step, i).wait_recv()
             gather3(st, step + 1, i).start()
         return carry
 
     lax.fori_loop(0, 8, phase3, 0)
     for i in range(4):
-        for st in all_st:
+        for st in range(6):
             gather3(st, 2, i).wait_recv()
 
-    def drain(n, carry):
-        step, i = n // 4, n % 4
-        for st in all_st:
-            arrived1(st, step, i).wait_send()
-            gather3(st, step, i).wait_send()
+    def drain(i, carry):
+        for step in range(3):
+            for st in all_st:
+                if step > 0 or st >= EARLY:
+                    arrived1(st, step, i).wait_send()
+            for st in range(6):
+                gather3(st, step, i).wait_send()
         return carry
 
-    lax.fori_loop(0, 12, drain, 0)
+    lax.fori_loop(0, 4, drain, 0)
     for step in range(3):
         for st in all_st:
             send2(st, step).wait_send()
             send3(st, step).wait_send()
+        for st in range(6):
             gather1(st, step).wait_send()
             gather2(st, step).wait_send()
 
 
-def tail(grads, w_flat, m_flat, v_flat, loss_tile, tau_clip, learn_rate):
+def tail(grads, early, w_flat, m_flat, v_flat, loss_tile, tau_clip, learn_rate):
     f32, bf16 = jnp.float32, jnp.bfloat16
     flat = jax.ShapeDtypeStruct(w_flat.shape, f32)
     in_vmem = pl.BlockSpec(memory_space=pltpu.VMEM)
     in_any = pl.BlockSpec(memory_space=pl.ANY)
     dma = pltpu.SemaphoreType.DMA
-    per_step = (6, 3)
+    n_stream = len(STREAMS)
+    per_step = (n_stream, 3)
     per_sub = per_step + (4,)
-    part = (PART,) + TILE
+    part = (HALF_PART,) + TILE
+    per_place = (6, 3)
     return pl.pallas_call(
         functools.partial(tail_kernel, tau_clip, learn_rate),
         out_shape=(flat, flat, flat, jax.ShapeDtypeStruct(TILE, f32), jax.ShapeDtypeStruct(grads.shape, bf16)),
-        in_specs=[in_any] + [in_vmem] * 4,
+        in_specs=[in_any] * 2 + [in_vmem] * 4,
         out_specs=(in_vmem, in_vmem, in_vmem, in_vmem, in_any),
         scratch_shapes=[
             pltpu.VMEM(per_sub + (4,) + part, f32),
             pltpu.VMEM(per_sub + part, f32),
             pltpu.VMEM(per_step + part, f32),
-            pltpu.VMEM((6, 2, 4) + part, f32),
+            pltpu.VMEM((n_stream, 2, 4) + part, f32),
             pltpu.VMEM((2, TILES) + TILE, bf16),
             pltpu.VMEM((4, 4, 2) + TILE, f32),
             *[dma(per_sub)] * 2, *[dma(per_step)] * 4,
-            dma((6, 2)), dma((6,)), *[dma((4, 4))] * 2,
-            *[dma(per_step)] * 4, *[dma(per_sub)] * 2,
+            dma((n_stream, 2)), dma((EARLY, 4)), dma((6,)), *[dma((4, 4))] * 2,
+            *[dma(per_place)] * 4, *[dma(per_place + (4,))] * 2,
         ],
         compiler_params=pltpu.CompilerParams(collective_id=1, has_side_effects=True, vmem_limit_bytes=VMEM_LIMIT),
         name="tail",
-    )(grads, w_flat, m_flat, v_flat, loss_tile)
+    )(grads, early, w_flat, m_flat, v_flat, loss_tile)
 
 
 ROWS = 256
@@ -302,11 +329,14 @@
 GELU_C = 0.044715
 
 
-def stack_kernel(n_tokens, x_hbm, t_hbm, w1_hbm, w2_hbm, g_out, loss_out,
-                 w1, w2, xs, gs, us, acts, rs, outf, outb, tgt, stage1, stage2,
-                 w1_sem, w2_sem, x_sem, t_sem, xsend, xrecv, gsend, grecv, o1_sem, o2_sem):
-    stage = lax.axis_index("stage")
-    me = lax.axis_index("data")
+def gelu_tanh(pre, square):
+    return jnp.tanh(pre * (GELU_K + (GELU_K * GELU_C) * square))
+
+
+def stack_kernel(n_tokens, x_hbm, t_hbm, w1_hbm, w2_hbm, g_out, early_out, loss_out,
+                 w1, w2, xs, gs, us, acts, rs, outf, outb, tgt, xt, stage1, stage2,
+                 w1_sem, w2_sem, x_sem, t_sem, xsend, xrecv, gsend, grecv, o1_sem, o2_sem, es, er):
+    stage, me, coords, ring, peer = torus()
     partner = (1 - stage, me)
     n_half, d_model, d_ff = w1.shape
 
@@ -331,7 +361,10 @@
 
     barrier = pltpu.get_barrier_semaphore()
     pl.semaphore_signal(barrier, inc=1, device_id=partner, device_id_type=MESH_ID)
-    pl.semaphore_wait(barrier, 1)
+    for axis in range(3):
+        for d in range(2):
+            pl.semaphore_signal(barrier, inc=1, device_id=peer(axis, sgn(d)), device_id_type=MESH_ID)
+    pl.semaphore_wait(barrier, 7)
 
     @pl.when(stage == 0)
     def _():
@@ -368,7 +401,6 @@
         @pl.when(c == 0)
         def _():
             load_w1(h).wait()
-            load_w2(h).wait()
 
         @pl.when(h + stage > 0)
         def _():
@@ -378,11 +410,15 @@
             cols = block(f, 512)
             pre = dot(xs[h, rows, :], w1[h, :, cols], 1, 0)
             us[h, rows, cols] = pre
-            cdf = 0.5 * (1.0 + jnp.tanh(GELU_K * (pre + GELU_C * (pre * pre * pre))))
-            acts[h, rows, cols] = (pre * cdf).astype(jnp.bfloat16)
+            half = 0.5 * pre
+            acts[h, rows, cols] = (half + half * gelu_tanh(pre, pre * pre)).astype(jnp.bfloat16)
             return inner
 
-        lax.fori_loop(0, d_ff // 512, up, 0)
+        lax.fori_loop(0, d_ff // 512, up, 0, unroll=True)
+
+        @pl.when(c == 0)
+        def _():
+            load_w2(h).wait()
 
         def down(n, inner):
             cols = block(n, 256)
@@ -417,10 +453,14 @@
         load_t.wait()
 
     def out_one(h, n, i):
-        return pltpu.make_async_copy(stage1.at[n % 2, i], g_out.at[h, pl.ds(0, 32), pl.ds(i * 24 + 2 * n, 2)], o1_sem.at[n % 2, i])
+        return pltpu.make_async_copy(stage1.at[n % 2, i], g_out.at[h, pl.ds(0, 2), :, :, pl.ds(i * 24 + 2 * n, 2)], o1_sem.at[n % 2, i])
 
     def out_two(h, m):
-        return pltpu.make_async_copy(stage2.at[m % 2], g_out.at[h, pl.ds(32 + 4 * m, 4)], o2_sem.at[m % 2])
+        return pltpu.make_async_copy(stage2.at[m % 2], g_out.at[h, 2 + m // 4, m % 4], o2_sem.at[m % 2])
+
+    def early_send(st, i):
+        h, k, d = STREAMS[st]
+        return remote(grad_view(g_out, STREAMS[st], ring, 1, i), early_out.at[st, i], es.at[st, i], er.at[st, i], peer(ORDERS[k][0], sgn(d)))
 
     def backward(b, carry):
         h = 1 - b
@@ -437,12 +477,12 @@
                 q = dot(gs[h, rows, :], w2[h, cols, :], 1, 1)
                 pre = us[h, rows, cols]
                 square = pre * pre
-                th = jnp.tanh(GELU_K * (pre + GELU_C * (square * pre)))
-                slope = 0.5 * (1.0 + th) + 0.5 * pre * (1.0 - th * th) * (GELU_K * (1.0 + 3.0 * GELU_C * square))
+                th = gelu_tanh(pre, square)
+                slope = (0.5 + 0.5 * th) + (1.0 - th * th) * (pre * (0.5 * GELU_K + (1.5 * GELU_K * GELU_C) * square))
                 rs[rows, cols] = (q * slope).astype(jnp.bfloat16)
                 return deep
 
-            lax.fori_loop(0, d_ff // 512, up, 0)
+            lax.fori_loop(0, d_ff // 512, up, 0, unroll=True)
 
             @pl.when(h + stage > 0)
             def _():
@@ -459,17 +499,19 @@
 
         lax.fori_loop(0, 2, chain, 0)
 
+        xt[...] = xs[h].T
+
         def grad_one(n, inner):
-            @pl.when(b * 12 + n >= 2)
+            @pl.when(n >= 2)
             def _():
                 for i in range(3):
                     out_one(h, n, i).wait()
 
-            val = dot(xs[h], rs[:, block(n, 256)], 0, 0)
+            val = dot(xt[...], rs[:, block(n, 256)], 1, 0)
             for p in range(32):
                 for i in range(3):
                     for j in range(2):
-                        stage1[n % 2, i, p, j] = val[p * 24 + i * 8:p * 24 + i * 8 + 8, 128 * j:128 * (j + 1)]
+                        stage1[n % 2, i, p // 16, (p // 4) % 4, p % 4, j] = val[p * 24 + i * 8:p * 24 + i * 8 + 8, 128 * j:128 * (j + 1)]
             for i in range(3):
                 out_one(h, n, i).start()
             return inner
@@ -477,7 +519,7 @@
         lax.fori_loop(0, d_ff // 256, grad_one, 0)
 
         def grad_two(m, inner):
-            @pl.when(b * 8 + m >= 2)
+            @pl.when(m >= 2)
             def _():
                 out_two(h, m).wait()
 
@@ -490,13 +532,23 @@
             return inner
 
         lax.fori_loop(0, d_ff // 384, grad_two, 0)
+        for n in range(2):
+            for i in range(3):
+                out_one(h, n, i).wait()
+            out_two(h, n).wait()
+
+        @pl.when(b == 0)
+        def _():
+            for i in range(4):
+                for st in range(EARLY):
+                    early_send(st, i).start()
+
         return carry
 
     lax.fori_loop(0, n_half, backward, 0)
-    for n in range(2):
-        for i in range(3):
-            out_one(0, n, i).wait()
-        out_two(0, n).wait()
+    for i in range(4):
+        for st in range(EARLY):
+            early_send(st, i).wait()
 
     for h in range(2):
         for c in range(2):
@@ -517,16 +569,16 @@
     in_any = pl.BlockSpec(memory_space=pl.ANY)
     return pl.pallas_call(
         functools.partial(stack_kernel, n_tokens),
-        out_shape=(jax.ShapeDtypeStruct((2, 64, TILES, 8, 128), f32), jax.ShapeDtypeStruct((8, 128), f32)),
+        out_shape=(jax.ShapeDtypeStruct((2, 4, 4, 4, TILES) + TILE, f32), jax.ShapeDtypeStruct((EARLY, 4, 4, HALF_PART) + TILE, f32), jax.ShapeDtypeStruct(TILE, f32)),
         in_specs=[in_any] * 4,
-        out_specs=(in_any, pl.BlockSpec(memory_space=pltpu.VMEM)),
+        out_specs=(in_any, in_any, pl.BlockSpec(memory_space=pltpu.VMEM)),
         scratch_shapes=[
             pltpu.VMEM((2, d_model, d_ff), bf16), pltpu.VMEM((2, d_ff, d_model), bf16),
             pltpu.VMEM((2, rows, d_model), bf16), pltpu.VMEM((2, rows, d_model), bf16),
             pltpu.VMEM((2, rows, d_ff), f32), pltpu.VMEM((2, rows, d_ff), bf16), pltpu.VMEM((rows, d_ff), bf16),
-            pltpu.VMEM((2, 2, ROWS, d_model), bf16), pltpu.VMEM((2, 2, ROWS, d_model), bf16), pltpu.VMEM((rows, d_model), bf16),
-            pltpu.VMEM((2, 3, 32, 2, 8, 128), f32), pltpu.VMEM((2, 4, TILES, 8, 128), f32),
-            dma((2,)), dma((2,)), dma, dma, *[dma((2, 2))] * 4, dma((2, 3)), dma((2,)),
+            pltpu.VMEM((2, 2, ROWS, d_model), bf16), pltpu.VMEM((2, 2, ROWS, d_model), bf16), pltpu.VMEM((rows, d_model), bf16), pltpu.VMEM((d_model, rows), bf16),
+            pltpu.VMEM((2, 3, 2, 4, 4, 2) + TILE, f32), pltpu.VMEM((2, 4, TILES) + TILE, f32),
+            dma((2,)), dma((2,)), dma, dma, *[dma((2, 2))] * 4, dma((2, 3)), dma((2,)), *[dma((EARLY, 4))] * 2,
         ],
         compiler_params=pltpu.CompilerParams(collective_id=0, has_side_effects=True, vmem_limit_bytes=VMEM_LIMIT),
         name="stack",
@@ -546,9 +598,9 @@
         learn_rate = 0.1 / math.sqrt(4.0 * d_model * n_blocks)
         x_all = x_loc.reshape(n_micro * n_tok, d_model)
         t_all = t_loc.reshape(n_micro * n_tok, d_model)
-        grads, loss_tile = stack(x_all, t_all, w1_loc[0, :, 0], w2_loc[0, :, 0], n_tokens)
+        grads, early, loss_tile = stack(x_all, t_all, w1_loc[0, :, 0], w2_loc[0, :, 0], n_tokens)
         w_new, m_new, v_new, stat, w_full = tail(
-            grads.reshape(2, 4, 4, 4, TILES, 8, 128), wm_loc.reshape(2, 576, 128), m_loc.reshape(2, 576, 128), v_loc.reshape(2, 576, 128),
+            grads, early, wm_loc.reshape(2, 576, 128), m_loc.reshape(2, 576, 128), v_loc.reshape(2, 576, 128),
             loss_tile, tau_clip, learn_rate)
         w1_new = w_full[:, :2].reshape(2, d_model // 8, d_ff // 128, 8, 128).transpose(0, 1, 3, 2, 4).reshape(1, 2, 1, d_model, d_ff)
         w2_new = w_full[:, 2:].reshape(2, d_ff // 8, d_model // 128, 8, 128).transpose(0, 1, 3, 2, 4).reshape(1, 2, 1, d_ff, d_model)

time: 354 us -> 326 us (0.921)
  Pallas kernels: 334 us -> 305 us
    pallas_call x1, Pallas kernels: 244 us -> 226 us  [tail(): pl.pallas_call(functools.partial(tail_kernel, tau_clip, learn_rate), out_...]
    pallas_call x1, Pallas kernels: 89.9 us -> 78.3 us  [stack(): pl.pallas_call(functools.partial(stack_kernel, n_tokens), out_shape=(jax....]
where the time goes in v4:
time: 326 us; the launch traced here: 325 us
  Pallas kernels  305 us (94%)
  local copies, waits for them, and re-layouts  18.2 us (6%)
    pallas_call x1, Pallas kernels, tail(): pl.pallas_call(functools.partial(tail_kernel, tau_clip, learn_rate), out_...  226 us
    pallas_call x1, Pallas kernels, stack(): pl.pallas_call(functools.partial(stack_kernel, n_tokens), out_shape=(jax....  78.3 us
    slice x1, local copies, waits for them, and re-layouts, device_step(): w_full[:, 2:].reshape(2, d_ff // 8, d_model // 128, 8, 128)  14.6 us

profile of v4, /device:TPU:0, one launch (start us, length us, event | category | flops | bytes accessed | tf_op | source)
XLA Modules:
  0.0 325.4 jit_solution(14633200295889061977)
XLA Ops:
  0.6 78.3 %stack.1 = (f32[2,4,4,4,72,8,128]{6,5,4,3,2,1,0:T(8,128)}, f32[6,4,4,12,8,128]{5,4,3,2,1,0:T(8,128)}, f32[8,128]{1,0:T(8,128)}) custom-call(bf16[512,768]{1,0:T(8,128)(2,1)} %bitcast.25, bf16[512,768]{1,0:T(8,128)(2,1)} %bitcast.26, bf16[2,768,3072]{2,1,0:T(8,128)(2,1)} %bitcast.21, bf16[2,3072,768]{2,1,0:T(8,128)(2,1)} %bitcast.22), custom_call_target="tpu_custom_call" | custom-call | tf_op jit(solution)/shard_map/stack/pallas_call | solution.py:570
  78.9 226.4 %tail.1 = (f32[2,576,128]{2,1,0:T(8,128)}, f32[2,576,128]{2,1,0:T(8,128)}, f32[2,576,128]{2,1,0:T(8,128)}, f32[8,128]{1,0:T(8,128)}, bf16[2,4,4,4,72,8,128]{6,5,4,3,2,1,0:T(8,128)(2,1)}) custom-call(f32[2,4,4,4,72,8,128]{6,5,4,3,2,1,0:T(8,128)} %get-tuple-element.14.g_ref, f32[6,4,4,12,8,128]{5,4,3,2,1,0:T(8,128)} %get-tuple-element.15.early_ref, ...), custom_call_target="tpu_custom_call" | custom-call | tf_op jit(solution)/shard_map/tail/pallas_call | solution.py:306
  305.4 1.2 slice.11
  307.2 0.0 copy-start.2
  307.2 0.0 copy-start.1
  307.2 0.0 copy-start
  307.2 14.6 %fusion = (bf16[2,2,4,4,72,8,128]{6,5,4,3,2,1,0:T(8,128)(2,1)}, bf16[2,2,4,4,72,8,128]{6,5,4,3,2,1,0:T(8,128)(2,1)}) fusion(bf16[2,4,4,4,72,8,128]{6,5,4,3,2,1,0:T(8,128)(2,1)} %get-tuple-element.17), kind=kLoop, calls=%fused_computation | loop fusion | bytes 37748736 | tf_op jit(solution)/shard_map/slice | solution.py:606
  321.8 0.0 copy-done.2
  321.8 0.8 copy.19
  322.6 0.0 copy-done.1
  322.6 0.8 copy.20
  323.4 0.0 copy-done
  323.5 0.8 copy.21
Async XLA Ops:
  307.2 14.6 %copy-start.2 = (f32[2,576,128]{2,1,0:T(8,128)S(1)}, f32[2,576,128]{2,1,0:T(8,128)}, u32[]{:S(2)}) copy-start(f32[2,576,128]{2,1,0:T(8,128)} %get-tuple-element.18) | copy-start | bytes 1769476
  307.2 15.4 %copy-start.1 = (f32[2,576,128]{2,1,0:T(8,128)S(1)}, f32[2,576,128]{2,1,0:T(8,128)}, u32[]{:S(2)}) copy-start(f32[2,576,128]{2,1,0:T(8,128)} %get-tuple-element.19) | copy-start | bytes 1769476
  307.2 16.2 %copy-start = (f32[2,576,128]{2,1,0:T(8,128)S(1)}, f32[2,576,128]{2,1,0:T(8,128)}, u32[]{:S(2)}) copy-start(f32[2,576,128]{2,1,0:T(8,128)} %get-tuple-element.20) | copy-start | bytes 1769476

commit v5 on v4

--- a/solution.py
+++ b/solution.py
@@ -62,8 +62,8 @@
 
 def tail_kernel(tau_clip, learn_rate, g_ref, early_ref, w_ref, m_ref, v_ref, loss_ref,
                 w_out, m_out, v_out, stat_out, full_out,
-                recv1, recv2, recv3, local, wbf, nbuf,
-                s1, r1, s2, r2, s3, r3, l_sem, e_sem, own_sem, ns, nr,
+                recv1, recv2, recv3, local, wbf, nbuf, state,
+                s1, r1, s2, r2, s3, r3, l_sem, e_sem, own_sem, ns, nr, in_sem, out_sem,
                 t1, q1, t2, q2, t3, q3):
     stage, me, coords, ring, peer = torus()
     streams = [(k, d) for k in range(3) for d in range(2)]
@@ -106,6 +106,8 @@
         src = recv2.at[st, 2, back_of(st, 2, 1)] if step == 0 else recv3.at[st, step - 1]
         return remote(src, recv3.at[st, step], s3.at[st, step], r3.at[st, step], next_of(st, 2))
 
+    state_in = [pltpu.make_async_copy(ref, state.at[j], in_sem.at[j]) for j, ref in enumerate((w_ref, m_ref, v_ref))]
+    state_out = [pltpu.make_async_copy(state.at[j], ref, out_sem.at[j]) for j, ref in enumerate((w_out, m_out, v_out))]
     all_st = range(len(STREAMS))
     early, late = all_st[:EARLY], all_st[EARLY:]
     for i in range(4):
@@ -117,6 +119,9 @@
             for st in all_st:
                 for n in range(2):
                     fetch(st, n).start()
+
+    for copy in state_in:
+        copy.start()
 
     def accumulate(st, step, i, more):
         n = step * 4 + i
@@ -157,7 +162,9 @@
             if step < 2:
                 send3(st, step + 1).start()
 
-    total = jnp.zeros((8, 128), jnp.float32)
+    for copy in state_in:
+        copy.wait()
+    total = jnp.zeros(TILE, jnp.float32)
     for st in all_st:
         piece = recv3[st, 2]
         total = total + jnp.sum(piece * piece, axis=0)
@@ -190,15 +197,15 @@
                 for t in range(PART):
                     rows = pl.ds(k * 192 + (t // width) * (8 * width) + t % width, 8, stride=width)
                     grad = clip * recv3[(1 - h) * EARLY + 2 * k + t // HALF_PART, 2, t % HALF_PART]
-                    m_new = BETA_ONE * m_ref[h, rows, :] + (1.0 - BETA_ONE) * grad
-                    v_new = BETA_TWO * v_ref[h, rows, :] + (1.0 - BETA_TWO) * grad * grad
-                    m_hat = m_new / (1.0 - BETA_ONE ** ADAM_STEP)
-                    v_hat = v_new / (1.0 - BETA_TWO ** ADAM_STEP)
-                    w_old = w_ref[h, rows, :]
+                    m_new = BETA_ONE * state[1, h, rows, :] + (1.0 - BETA_ONE) * grad
+                    v_new = BETA_TWO * state[2, h, rows, :] + (1.0 - BETA_TWO) * grad * grad
+                    m_hat = m_new * (1.0 / (1.0 - BETA_ONE ** ADAM_STEP))
+                    v_hat = v_new * (1.0 / (1.0 - BETA_TWO ** ADAM_STEP))
+                    w_old = state[0, h, rows, :]
                     w_new = w_old - learn_rate * (m_hat / (jnp.sqrt(v_hat) + ADAM_EPS) + WEIGHT_DECAY * w_old)
-                    w_out[h, rows, :] = w_new
-                    m_out[h, rows, :] = m_new
-                    v_out[h, rows, :] = v_new
+                    state[0, h, rows, :] = w_new
+                    state[1, h, rows, :] = m_new
+                    state[2, h, rows, :] = v_new
                     wbf[h, k * PART + t] = w_new.astype(jnp.bfloat16)
             return carry
 
@@ -211,6 +218,9 @@
     @pl.when(me >= 32)
     def _():
         update(6)
+
+    for copy in state_out:
+        copy.start()
 
     def full_part(st, on_a, on_b, on_c):
         k, d = streams[st]
@@ -283,6 +293,8 @@
         return carry
 
     lax.fori_loop(0, 4, drain, 0)
+    for copy in state_out:
+        copy.wait()
     for step in range(3):
         for st in all_st:
             send2(st, step).wait_send()
@@ -306,8 +318,8 @@
     return pl.pallas_call(
         functools.partial(tail_kernel, tau_clip, learn_rate),
         out_shape=(flat, flat, flat, jax.ShapeDtypeStruct(TILE, f32), jax.ShapeDtypeStruct(grads.shape, bf16)),
-        in_specs=[in_any] * 2 + [in_vmem] * 4,
-        out_specs=(in_vmem, in_vmem, in_vmem, in_vmem, in_any),
+        in_specs=[in_any] * 5 + [in_vmem],
+        out_specs=(in_any, in_any, in_any, in_vmem, in_any),
         scratch_shapes=[
             pltpu.VMEM(per_sub + (4,) + part, f32),
             pltpu.VMEM(per_sub + part, f32),
@@ -315,8 +327,9 @@
             pltpu.VMEM((n_stream, 2, 4) + part, f32),
             pltpu.VMEM((2, TILES) + TILE, bf16),
             pltpu.VMEM((4, 4, 2) + TILE, f32),
+            pltpu.VMEM((3,) + w_flat.shape, f32),
             *[dma(per_sub)] * 2, *[dma(per_step)] * 4,
-            dma((n_stream, 2)), dma((EARLY, 4)), dma((6,)), *[dma((4, 4))] * 2,
+            dma((n_stream, 2)), dma((EARLY, 4)), dma((6,)), *[dma((4, 4))] * 2, *[dma((3,))] * 2,
             *[dma(per_place)] * 4, *[dma(per_place + (4,))] * 2,
         ],
         compiler_params=pltpu.CompilerParams(collective_id=1, has_side_effects=True, vmem_limit_bytes=VMEM_LIMIT),
@@ -325,6 +338,8 @@
 
 
 ROWS = 256
+SLOTS = 4
+BAND = 256
 GELU_K = math.sqrt(2.0 / math.pi)
 GELU_C = 0.044715
 
@@ -354,10 +369,6 @@
         load_x.start()
 
     load_w1(0).start()
-    load_w2(0).start()
-    load_w1(1).start()
-    load_w2(1).start()
-    load_t.start()
 
     barrier = pltpu.get_barrier_semaphore()
     pl.semaphore_signal(barrier, inc=1, device_id=partner, device_id_type=MESH_ID)
@@ -366,6 +377,8 @@
             pl.semaphore_signal(barrier, inc=1, device_id=peer(axis, sgn(d)), device_id_type=MESH_ID)
     pl.semaphore_wait(barrier, 7)
 
+    load_w2(0).start()
+
     @pl.when(stage == 0)
     def _():
         load_x.wait()
@@ -381,18 +394,21 @@
     def block(i, size):
         return pl.ds(pl.multiple_of(i * size, size), size)
 
-    def send_x(h, c):
-        return pltpu.make_async_remote_copy(src_ref=outf.at[h, c], dst_ref=xs.at[h + stage, rows_of(c)], send_sem=xsend.at[h, c], recv_sem=xrecv.at[h + stage, c], device_id=partner, device_id_type=MESH_ID)
-
-    def wait_x(h, c):
-        pltpu.make_async_remote_copy(src_ref=outf.at[h, c], dst_ref=xs.at[h, rows_of(c)], send_sem=xsend.at[h, c], recv_sem=xrecv.at[h, c], device_id=partner, device_id_type=MESH_ID).wait_recv()
-
-    def send_g(h, c):
-        to = h - 1 + stage
-        return pltpu.make_async_remote_copy(src_ref=outb.at[h, c], dst_ref=gs.at[to, rows_of(c)], send_sem=gsend.at[h, c], recv_sem=grecv.at[to, c], device_id=partner, device_id_type=MESH_ID)
-
-    def wait_g(h, c):
-        pltpu.make_async_remote_copy(src_ref=outb.at[h, c], dst_ref=gs.at[h, rows_of(c)], send_sem=gsend.at[h, c], recv_sem=grecv.at[h, c], device_id=partner, device_id_type=MESH_ID).wait_recv()
+    def send_x(h, c, n):
+        cols = block(n, BAND)
+        return remote(outf.at[h, c, :, cols], xs.at[h + stage, rows_of(c), cols], xsend.at[h, c, n], xrecv.at[h + stage, c, n], partner)
+
+    def wait_x(h, c, n):
+        cols = block(n, BAND)
+        remote(outf.at[h, c, :, cols], xs.at[h, rows_of(c), cols], xsend.at[h, c, n], xrecv.at[h, c, n], partner).wait_recv()
+
+    def send_g(h, c, n):
+        to, cols = h - 1 + stage, block(n, BAND)
+        return remote(outb.at[h, c, :, cols], gs.at[to, rows_of(c), cols], gsend.at[h, c, n], grecv.at[to, c, n], partner)
+
+    def wait_g(h, c, n):
+        cols = block(n, BAND)
+        remote(outb.at[h, c, :, cols], gs.at[h, rows_of(c), cols], gsend.at[h, c, n], grecv.at[h, c, n], partner).wait_recv()
 
     def forward(item, carry):
         h, c = item // 2, item % 2
@@ -404,7 +420,8 @@
 
         @pl.when(h + stage > 0)
         def _():
-            wait_x(h, c)
+            for n in range(3):
+                wait_x(h, c, n)
 
         def up(f, inner):
             cols = block(f, 512)
@@ -420,17 +437,24 @@
         def _():
             load_w2(h).wait()
 
+        @pl.when(item == 0)
+        def _():
+            load_w1(1).start()
+            load_w2(1).start()
+            load_t.start()
+
         def down(n, inner):
-            cols = block(n, 256)
+            cols = block(n, BAND)
             val = dot(acts[h, rows, :], w2[h, :, cols], 1, 0)
             outf[h, c, :, cols] = (xs[h, rows, cols].astype(jnp.float32) + val).astype(jnp.bfloat16)
+
+            @pl.when(h + stage < 2)
+            def _():
+                send_x(h, c, n).start()
+
             return inner
 
-        lax.fori_loop(0, d_model // 256, down, 0)
-
-        @pl.when(h + stage < 2)
-        def _():
-            send_x(h, c).start()
+        lax.fori_loop(0, d_model // BAND, down, 0)
 
         @pl.when(h + stage == 2)
         def _():
@@ -453,10 +477,10 @@
         load_t.wait()
 
     def out_one(h, n, i):
-        return pltpu.make_async_copy(stage1.at[n % 2, i], g_out.at[h, pl.ds(0, 2), :, :, pl.ds(i * 24 + 2 * n, 2)], o1_sem.at[n % 2, i])
+        return pltpu.make_async_copy(stage1.at[n % SLOTS, i], g_out.at[h, pl.ds(0, 2), :, :, pl.ds(i * 24 + 2 * n, 2)], o1_sem.at[n % SLOTS, i])
 
     def out_two(h, m):
-        return pltpu.make_async_copy(stage2.at[m % 2], g_out.at[h, 2 + m // 4, m % 4], o2_sem.at[m % 2])
+        return pltpu.make_async_copy(stage2.at[m % SLOTS], g_out.at[h, 2 + m // 4, m % 4], o2_sem.at[m % SLOTS])
 
     def early_send(st, i):
         h, k, d = STREAMS[st]
@@ -470,7 +494,8 @@
 
             @pl.when(h + stage < 2)
             def _():
-                wait_g(h, c)
+                for n in range(3):
+                    wait_g(h, c, n)
 
             def up(f, deep):
                 cols = block(f, 512)
@@ -487,13 +512,13 @@
             @pl.when(h + stage > 0)
             def _():
                 def down(n, deep):
-                    cols = block(n, 256)
+                    cols = block(n, BAND)
                     val = dot(rs[rows, :], w1[h, cols, :], 1, 1)
                     outb[h, c, :, cols] = (gs[h, rows, cols].astype(jnp.float32) + val).astype(jnp.bfloat16)
+                    send_g(h, c, n).start()
                     return deep
 
-                lax.fori_loop(0, d_model // 256, down, 0)
-                send_g(h, c).start()
+                lax.fori_loop(0, d_model // BAND, down, 0)
 
             return inner
 
@@ -502,24 +527,24 @@
         xt[...] = xs[h].T
 
         def grad_one(n, inner):
-            @pl.when(n >= 2)
+            @pl.when(n >= SLOTS)
             def _():
                 for i in range(3):
                     out_one(h, n, i).wait()
 
-            val = dot(xt[...], rs[:, block(n, 256)], 1, 0)
+            val = dot(xt[...], rs[:, block(n, BAND)], 1, 0)
             for p in range(32):
                 for i in range(3):
                     for j in range(2):
-                        stage1[n % 2, i, p // 16, (p // 4) % 4, p % 4, j] = val[p * 24 + i * 8:p * 24 + i * 8 + 8, 128 * j:128 * (j + 1)]
+                        stage1[n % SLOTS, i, p // 16, (p // 4) % 4, p % 4, j] = val[p * 24 + i * 8:p * 24 + i * 8 + 8, 128 * j:128 * (j + 1)]
             for i in range(3):
                 out_one(h, n, i).start()
             return inner
 
-        lax.fori_loop(0, d_ff // 256, grad_one, 0)
+        lax.fori_loop(0, d_ff // BAND, grad_one, 0)
 
         def grad_two(m, inner):
-            @pl.when(m >= 2)
+            @pl.when(m >= SLOTS)
             def _():
                 out_two(h, m).wait()
 
@@ -527,12 +552,12 @@
             for p in range(4):
                 for i in range(12):
                     for j in range(6):
-                        stage2[m % 2, p, i * 6 + j] = val[p * 96 + i * 8:p * 96 + i * 8 + 8, 128 * j:128 * (j + 1)]
+                        stage2[m % SLOTS, p, i * 6 + j] = val[p * 96 + i * 8:p * 96 + i * 8 + 8, 128 * j:128 * (j + 1)]
             out_two(h, m).start()
             return inner
 
         lax.fori_loop(0, d_ff // 384, grad_two, 0)
-        for n in range(2):
+        for n in range(SLOTS):
             for i in range(3):
                 out_one(h, n, i).wait()
             out_two(h, n).wait()
@@ -554,11 +579,13 @@
         for c in range(2):
             @pl.when(h + stage < 2)
             def _():
-                send_x(h, c).wait_send()
+                for n in range(3):
+                    send_x(h, c, n).wait_send()
 
             @pl.when(h + stage > 0)
             def _():
-                send_g(h, c).wait_send()
+                for n in range(3):
+                    send_g(h, c, n).wait_send()
 
 
 def stack(x_all, t_all, w1, w2, n_tokens):
@@ -577,12 +604,48 @@
             pltpu.VMEM((2, rows, d_model), bf16), pltpu.VMEM((2, rows, d_model), bf16),
             pltpu.VMEM((2, rows, d_ff), f32), pltpu.VMEM((2, rows, d_ff), bf16), pltpu.VMEM((rows, d_ff), bf16),
             pltpu.VMEM((2, 2, ROWS, d_model), bf16), pltpu.VMEM((2, 2, ROWS, d_model), bf16), pltpu.VMEM((rows, d_model), bf16), pltpu.VMEM((d_model, rows), bf16),
-            pltpu.VMEM((2, 3, 2, 4, 4, 2) + TILE, f32), pltpu.VMEM((2, 4, TILES) + TILE, f32),
-            dma((2,)), dma((2,)), dma, dma, *[dma((2, 2))] * 4, dma((2, 3)), dma((2,)), *[dma((EARLY, 4))] * 2,
+            pltpu.VMEM((SLOTS, 3, 2, 4, 4, 2) + TILE, f32), pltpu.VMEM((SLOTS, 4, TILES) + TILE, f32),
+            dma((2,)), dma((2,)), dma, dma, *[dma((2, 2, 3))] * 4, dma((SLOTS, 3)), dma((SLOTS,)), *[dma((EARLY, 4))] * 2,
         ],
         compiler_params=pltpu.CompilerParams(collective_id=0, has_side_effects=True, vmem_limit_bytes=VMEM_LIMIT),
         name="stack",
     )(x_all, t_all, w1, w2)
+
+
+def finish_kernel(full_ref, w_ref, m_ref, v_ref, stat_ref, w1_out, w2_out, w_out, m_out, v_out, loss_out, full, state, in_sem, out_sem, sin_sem, sout_sem):
+    places = [(h, z, y) for h in range(2) for z in range(4) for y in range(4)]
+    loads, stores = [], []
+    for n, (h, z, y) in enumerate(places):
+        target = w1_out if z < 2 else w2_out
+        loads.append(pltpu.make_async_copy(full_ref.at[h, z, y], full.at[n], in_sem.at[n]))
+        stores.append(pltpu.make_async_copy(full.at[n], target.at[h, z % 2, y], out_sem.at[n]))
+    for j, (src, dst) in enumerate(((w_ref, w_out), (m_ref, m_out), (v_ref, v_out))):
+        loads.append(pltpu.make_async_copy(src, state.at[j], sin_sem.at[j]))
+        stores.append(pltpu.make_async_copy(state.at[j], dst, sout_sem.at[j]))
+    for load in loads:
+        load.start()
+    for load, store in zip(loads, stores):
+        load.wait()
+        store.start()
+    loss_out[0] = jnp.max(stat_ref[...])
+    for store in stores:
+        store.wait()
+
+
+def finish(w_full, w_flat, m_flat, v_flat, stat):
+    flat = jax.ShapeDtypeStruct(w_flat.shape, jnp.float32)
+    half = jax.ShapeDtypeStruct((2, 2) + w_full.shape[2:], jnp.bfloat16)
+    in_any = pl.BlockSpec(memory_space=pl.ANY)
+    dma = pltpu.SemaphoreType.DMA
+    return pl.pallas_call(
+        finish_kernel,
+        out_shape=(half, half, flat, flat, flat, jax.ShapeDtypeStruct((1,), jnp.float32)),
+        in_specs=[in_any] * 4 + [pl.BlockSpec(memory_space=pltpu.VMEM)],
+        out_specs=(in_any,) * 5 + (pl.BlockSpec(memory_space=pltpu.SMEM),),
+        scratch_shapes=[pltpu.VMEM((32,) + w_full.shape[3:], jnp.bfloat16), pltpu.VMEM((3,) + w_flat.shape, jnp.float32), dma((32,)), dma((32,)), dma((3,)), dma((3,))],
+        compiler_params=pltpu.CompilerParams(vmem_limit_bytes=VMEM_LIMIT),
+        name="finish",
+    )(w_full, w_flat, m_flat, v_flat, stat)
 
 
 def solution(mesh):
@@ -602,10 +665,11 @@
         w_new, m_new, v_new, stat, w_full = tail(
             grads, early, wm_loc.reshape(2, 576, 128), m_loc.reshape(2, 576, 128), v_loc.reshape(2, 576, 128),
             loss_tile, tau_clip, learn_rate)
-        w1_new = w_full[:, :2].reshape(2, d_model // 8, d_ff // 128, 8, 128).transpose(0, 1, 3, 2, 4).reshape(1, 2, 1, d_model, d_ff)
-        w2_new = w_full[:, 2:].reshape(2, d_ff // 8, d_model // 128, 8, 128).transpose(0, 1, 3, 2, 4).reshape(1, 2, 1, d_ff, d_model)
+        w1_new, w2_new, w_new, m_new, v_new, loss = finish(w_full, w_new, m_new, v_new, stat)
+        w1_new = w1_new.reshape(2, d_model // 8, d_ff // 128, 8, 128).transpose(0, 1, 3, 2, 4).reshape(1, 2, 1, d_model, d_ff)
+        w2_new = w2_new.reshape(2, d_ff // 8, d_model // 128, 8, 128).transpose(0, 1, 3, 2, 4).reshape(1, 2, 1, d_ff, d_model)
         flat_dims = (1, 2, 1, -1)
-        return w1_new, w2_new, w_new.reshape(flat_dims), m_new.reshape(flat_dims), v_new.reshape(flat_dims), stat[0, 0] / n_tokens
+        return w1_new, w2_new, w_new.reshape(flat_dims), m_new.reshape(flat_dims), v_new.reshape(flat_dims), loss.reshape(()) / n_tokens
 
     act_spec = P(None, "data", None)
     flat_spec = P("stage", None, None, "data")

time: 326 us -> 310 us (0.951)
  local copies, waits for them, and re-layouts: 18.2 us -> 0 us
    pallas_call x0 -> x1, Pallas kernels: none -> 15.9 us  [finish(): pl.pallas_call(finish_kernel, out_shape=(half, half, flat, flat, flat, ja...]
    slice x2 -> x0, local copies, waits for them, and re-layouts: 15.8 us -> none  [the longest x1 14.6 us: device_step(): w_full[:, 2:].reshape(2, d_ff // 8, d_model // 128, 8, 128)]
    pallas_call x1, Pallas kernels: 78.3 us -> 68 us  [stack(): pl.pallas_call(functools.partial(stack_kernel, n_tokens), out_shape=(jax....]
    pallas_call x1, Pallas kernels: 226 us -> 223 us  [tail(): pl.pallas_call(functools.partial(tail_kernel, tau_clip, learn_rate), out_...]
where the time goes in v5:
time: 310 us; the launch traced here: 309 us
  Pallas kernels  307 us (99%)
    pallas_call x1, Pallas kernels, tail(): pl.pallas_call(functools.partial(tail_kernel, tau_clip, learn_rate), out_...  223 us
    pallas_call x1, Pallas kernels, stack(): pl.pallas_call(functools.partial(stack_kernel, n_tokens), out_shape=(jax....  68 us
    pallas_call x1, Pallas kernels, finish(): pl.pallas_call(finish_kernel, out_shape=(half, half, flat, flat, flat, ja...  15.9 us

profile of v5, /device:TPU:0, one launch (start us, length us, event | category | flops | bytes accessed | tf_op | source)
XLA Modules:
  0.0 309.4 jit_solution(3928183221636284890)
XLA Ops:
  0.6 68.0 %stack.1 = (f32[2,4,4,4,72,8,128]{6,5,4,3,2,1,0:T(8,128)}, f32[6,4,4,12,8,128]{5,4,3,2,1,0:T(8,128)}, f32[8,128]{1,0:T(8,128)}) custom-call(bf16[512,768]{1,0:T(8,128)(2,1)} %bitcast.23, bf16[512,768]{1,0:T(8,128)(2,1)} %bitcast.24, bf16[2,768,3072]{2,1,0:T(8,128)(2,1)} %bitcast.21, bf16[2,3072,768]{2,1,0:T(8,128)(2,1)} %bitcast.22), custom_call_target="tpu_custom_call" | custom-call | tf_op jit(solution)/shard_map/stack/pallas_call | solution.py:597
  68.7 223.0 %tail.1 = (f32[2,576,128]{2,1,0:T(8,128)}, f32[2,576,128]{2,1,0:T(8,128)}, f32[2,576,128]{2,1,0:T(8,128)}, f32[8,128]{1,0:T(8,128)}, bf16[2,4,4,4,72,8,128]{6,5,4,3,2,1,0:T(8,128)(2,1)}) custom-call(f32[2,4,4,4,72,8,128]{6,5,4,3,2,1,0:T(8,128)} %get-tuple-element.20.g_ref, f32[6,4,4,12,8,128]{5,4,3,2,1,0:T(8,128)} %get-tuple-element.21.early_ref, ...), custom_call_target="tpu_custom_call" | custom-call | tf_op jit(solution)/shard_map/tail/pallas_call | solution.py:318
  291.7 15.9 %finish.1 = (bf16[2,2,4,4,72,8,128]{6,5,4,3,2,1,0:T(8,128)(2,1)}, bf16[2,2,4,4,72,8,128]{6,5,4,3,2,1,0:T(8,128)(2,1)}, f32[2,576,128]{2,1,0:T(8,128)}, f32[2,576...) custom-call(bf16[2,4,4,4,72,8,128]{6,5,4,3,2,1,0:T(8,128)(2,1)} %get-tuple-element.23.full_ref, ...), custom_call_target="tpu_custom_call" | custom-call | tf_op jit(solution)/shard_map/finish/pallas_call | solution.py:640

commit v6 on v5

--- a/solution.py
+++ b/solution.py
@@ -62,18 +62,24 @@
 
 def tail_kernel(tau_clip, learn_rate, g_ref, early_ref, w_ref, m_ref, v_ref, loss_ref,
                 w_out, m_out, v_out, stat_out, full_out,
-                recv1, recv2, recv3, local, wbf, nbuf, state,
-                s1, r1, s2, r2, s3, r3, l_sem, e_sem, own_sem, ns, nr, in_sem, out_sem,
+                recv1, recv2, recv3, local, nbuf,
+                s1, r1, s2, r2, s3, r3, l_sem, e_sem, ns, nr, in_sem,
                 t1, q1, t2, q2, t3, q3):
     stage, me, coords, ring, peer = torus()
     streams = [(k, d) for k in range(3) for d in range(2)]
 
+    def friend(phase, delta):
+        far, near = divmod(delta, 4)
+        if phase == 0:
+            return (lax.rem(stage + far, 2), peer(2, near)[1])
+        return (stage, peer(0, far)[1] + peer(1, near)[1] - me)
+
+    sizes = (8, 16)
     barrier = pltpu.get_barrier_semaphore()
-    for axis in range(3):
-        for delta in (1, 2, 3):
-            pl.semaphore_signal(barrier, inc=1, device_id=peer(axis, delta), device_id_type=MESH_ID)
-    pl.semaphore_signal(barrier, inc=1, device_id=(1 - stage, me), device_id_type=MESH_ID)
-    pl.semaphore_wait(barrier, 10)
+    for phase, size in enumerate(sizes):
+        for delta in range(1, size):
+            pl.semaphore_signal(barrier, inc=1, device_id=friend(phase, delta), device_id_type=MESH_ID)
+    pl.semaphore_wait(barrier, sum(sizes) - len(sizes))
 
     def next_of(st, phase):
         h, k, d = STREAMS[st]
@@ -106,8 +112,7 @@
         src = recv2.at[st, 2, back_of(st, 2, 1)] if step == 0 else recv3.at[st, step - 1]
         return remote(src, recv3.at[st, step], s3.at[st, step], r3.at[st, step], next_of(st, 2))
 
-    state_in = [pltpu.make_async_copy(ref, state.at[j], in_sem.at[j]) for j, ref in enumerate((w_ref, m_ref, v_ref))]
-    state_out = [pltpu.make_async_copy(state.at[j], ref, out_sem.at[j]) for j, ref in enumerate((w_out, m_out, v_out))]
+    state_in = [pltpu.make_async_copy(src, dst, in_sem.at[j]) for j, (src, dst) in enumerate(((w_ref, w_out), (m_ref, m_out), (v_ref, v_out)))]
     all_st = range(len(STREAMS))
     early, late = all_st[:EARLY], all_st[EARLY:]
     for i in range(4):
@@ -170,15 +175,10 @@
         total = total + jnp.sum(piece * piece, axis=0)
 
     parts = (total, loss_ref[...])
-    for phase in range(4):
-        size = 2 if phase == 0 else 4
-        mine = stage if phase == 0 else coords[phase - 1]
-        nbuf[phase, mine, 0] = parts[0]
-        nbuf[phase, mine, 1] = parts[1]
-        sends = []
-        for delta in range(1, size):
-            target = (1 - stage, me) if phase == 0 else peer(phase - 1, delta)
-            sends.append(remote(nbuf.at[phase, mine], nbuf.at[phase, mine], ns.at[phase, delta], nr.at[phase, delta], target))
+    for phase, size in enumerate(sizes):
+        mine = (stage * 4 + coords[2], coords[0] * 4 + coords[1])[phase]
+        nbuf[phase, mine, 0], nbuf[phase, mine, 1] = parts
+        sends = [remote(nbuf.at[phase, mine], nbuf.at[phase, mine], ns.at[phase, delta], nr.at[phase, delta], friend(phase, delta)) for delta in range(1, size)]
         for send in sends:
             send.start()
         for send in sends:
@@ -187,7 +187,7 @@
         for send in sends:
             send.wait_send()
 
-    stat_out[...] = jnp.full((8, 128), jnp.sum(parts[1]), jnp.float32)
+    stat_out[0] = jnp.sum(parts[1])
     norm = jnp.sqrt(jnp.full((8, 128), jnp.sum(parts[0]), jnp.float32))
     clip = jnp.minimum(1.0, tau_clip / norm)
 
@@ -197,16 +197,16 @@
                 for t in range(PART):
                     rows = pl.ds(k * 192 + (t // width) * (8 * width) + t % width, 8, stride=width)
                     grad = clip * recv3[(1 - h) * EARLY + 2 * k + t // HALF_PART, 2, t % HALF_PART]
-                    m_new = BETA_ONE * state[1, h, rows, :] + (1.0 - BETA_ONE) * grad
-                    v_new = BETA_TWO * state[2, h, rows, :] + (1.0 - BETA_TWO) * grad * grad
+                    m_new = BETA_ONE * m_out[h, rows, :] + (1.0 - BETA_ONE) * grad
+                    v_new = BETA_TWO * v_out[h, rows, :] + (1.0 - BETA_TWO) * grad * grad
                     m_hat = m_new * (1.0 / (1.0 - BETA_ONE ** ADAM_STEP))
                     v_hat = v_new * (1.0 / (1.0 - BETA_TWO ** ADAM_STEP))
-                    w_old = state[0, h, rows, :]
+                    w_old = w_out[h, rows, :]
                     w_new = w_old - learn_rate * (m_hat / (jnp.sqrt(v_hat) + ADAM_EPS) + WEIGHT_DECAY * w_old)
-                    state[0, h, rows, :] = w_new
-                    state[1, h, rows, :] = m_new
-                    state[2, h, rows, :] = v_new
-                    wbf[h, k * PART + t] = w_new.astype(jnp.bfloat16)
+                    w_out[h, rows, :] = w_new
+                    m_out[h, rows, :] = m_new
+                    v_out[h, rows, :] = v_new
+                    full_out[(h,) + coords + (k * PART + t,)] = w_new.astype(jnp.bfloat16)
             return carry
 
         lax.fori_loop(0, 3, group, 0)
@@ -219,9 +219,6 @@
     def _():
         update(6)
 
-    for copy in state_out:
-        copy.start()
-
     def full_part(st, on_a, on_b, on_c):
         k, d = streams[st]
         return full_out.at[(d,) + pick(k, on_a, on_b, on_c) + (pl.ds(PART * k, PART),)]
@@ -237,8 +234,7 @@
     def gather1(st, step):
         k, d = streams[st]
         place = full_part(st, coord_of(st, 0, 0), coord_of(st, 1, 0), coord_of(st, 2, step))
-        src = wbf.at[d, pl.ds(PART * k, PART)] if step == 0 else place
-        return remote(src, place, t1.at[st, step], q1.at[st, step], along(st, 2))
+        return remote(place, place, t1.at[st, step], q1.at[st, step], along(st, 2))
 
     def gather2(st, step):
         place = full_part(st, coord_of(st, 0, 0), coord_of(st, 1, step), slice(None))
@@ -248,20 +244,14 @@
         place = full_part(st, coord_of(st, 0, step), coord_of(st, 1, i), slice(None))
         return remote(place, place, t3.at[st, step, i], q3.at[st, step, i], along(st, 0))
 
-    def own(st):
-        k, d = streams[st]
-        return pltpu.make_async_copy(wbf.at[d, pl.ds(PART * k, PART)], full_part(st, coord_of(st, 0, 0), coord_of(st, 1, 0), coord_of(st, 2, 0)), own_sem.at[st])
-
     for st in range(6):
         gather1(st, 0).start()
-        own(st).start()
     for step in range(3):
         for st in range(6):
             gather1(st, step).wait_recv()
             if step < 2:
                 gather1(st, step + 1).start()
     for st in range(6):
-        own(st).wait()
         gather2(st, 0).start()
         gather3(st, 0, 0).start()
     for step in range(3):
@@ -293,8 +283,6 @@
         return carry
 
     lax.fori_loop(0, 4, drain, 0)
-    for copy in state_out:
-        copy.wait()
     for step in range(3):
         for st in all_st:
             send2(st, step).wait_send()
@@ -306,7 +294,7 @@
 
 def tail(grads, early, w_flat, m_flat, v_flat, loss_tile, tau_clip, learn_rate):
     f32, bf16 = jnp.float32, jnp.bfloat16
-    flat = jax.ShapeDtypeStruct(w_flat.shape, f32)
+    flat = pltpu.VMEM(w_flat.shape, f32)
     in_vmem = pl.BlockSpec(memory_space=pltpu.VMEM)
     in_any = pl.BlockSpec(memory_space=pl.ANY)
     dma = pltpu.SemaphoreType.DMA
@@ -317,22 +305,20 @@
     per_place = (6, 3)
     return pl.pallas_call(
         functools.partial(tail_kernel, tau_clip, learn_rate),
-        out_shape=(flat, flat, flat, jax.ShapeDtypeStruct(TILE, f32), jax.ShapeDtypeStruct(grads.shape, bf16)),
+        out_shape=(flat, flat, flat, jax.ShapeDtypeStruct((1,), f32), pltpu.VMEM(grads.shape, bf16)),
         in_specs=[in_any] * 5 + [in_vmem],
-        out_specs=(in_any, in_any, in_any, in_vmem, in_any),
+        out_specs=(in_vmem, in_vmem, in_vmem, pl.BlockSpec(memory_space=pltpu.SMEM), in_vmem),
         scratch_shapes=[
             pltpu.VMEM(per_sub + (4,) + part, f32),
             pltpu.VMEM(per_sub + part, f32),
             pltpu.VMEM(per_step + part, f32),
             pltpu.VMEM((n_stream, 2, 4) + part, f32),
-            pltpu.VMEM((2, TILES) + TILE, bf16),
-            pltpu.VMEM((4, 4, 2) + TILE, f32),
-            pltpu.VMEM((3,) + w_flat.shape, f32),
+            pltpu.VMEM((2, 16, 2) + TILE, f32),
             *[dma(per_sub)] * 2, *[dma(per_step)] * 4,
-            dma((n_stream, 2)), dma((EARLY, 4)), dma((6,)), *[dma((4, 4))] * 2, *[dma((3,))] * 2,
+            dma((n_stream, 2)), dma((EARLY, 4)), *[dma((2, 16))] * 2, dma((3,)),
             *[dma(per_place)] * 4, *[dma(per_place + (4,))] * 2,
         ],
-        compiler_params=pltpu.CompilerParams(collective_id=1, has_side_effects=True, vmem_limit_bytes=VMEM_LIMIT),
+        compiler_params=pltpu.CompilerParams(collective_id=1, has_side_effects=True, vmem_limit_bytes=VMEM_LIMIT * 7 // 10),
         name="tail",
     )(grads, early, w_flat, m_flat, v_flat, loss_tile)
 
@@ -612,42 +598,6 @@
     )(x_all, t_all, w1, w2)
 
 
-def finish_kernel(full_ref, w_ref, m_ref, v_ref, stat_ref, w1_out, w2_out, w_out, m_out, v_out, loss_out, full, state, in_sem, out_sem, sin_sem, sout_sem):
-    places = [(h, z, y) for h in range(2) for z in range(4) for y in range(4)]
-    loads, stores = [], []
-    for n, (h, z, y) in enumerate(places):
-        target = w1_out if z < 2 else w2_out
-        loads.append(pltpu.make_async_copy(full_ref.at[h, z, y], full.at[n], in_sem.at[n]))
-        stores.append(pltpu.make_async_copy(full.at[n], target.at[h, z % 2, y], out_sem.at[n]))
-    for j, (src, dst) in enumerate(((w_ref, w_out), (m_ref, m_out), (v_ref, v_out))):
-        loads.append(pltpu.make_async_copy(src, state.at[j], sin_sem.at[j]))
-        stores.append(pltpu.make_async_copy(state.at[j], dst, sout_sem.at[j]))
-    for load in loads:
-        load.start()
-    for load, store in zip(loads, stores):
-        load.wait()
-        store.start()
-    loss_out[0] = jnp.max(stat_ref[...])
-    for store in stores:
-        store.wait()
-
-
-def finish(w_full, w_flat, m_flat, v_flat, stat):
-    flat = jax.ShapeDtypeStruct(w_flat.shape, jnp.float32)
-    half = jax.ShapeDtypeStruct((2, 2) + w_full.shape[2:], jnp.bfloat16)
-    in_any = pl.BlockSpec(memory_space=pl.ANY)
-    dma = pltpu.SemaphoreType.DMA
-    return pl.pallas_call(
-        finish_kernel,
-        out_shape=(half, half, flat, flat, flat, jax.ShapeDtypeStruct((1,), jnp.float32)),
-        in_specs=[in_any] * 4 + [pl.BlockSpec(memory_space=pltpu.VMEM)],
-        out_specs=(in_any,) * 5 + (pl.BlockSpec(memory_space=pltpu.SMEM),),
-        scratch_shapes=[pltpu.VMEM((32,) + w_full.shape[3:], jnp.bfloat16), pltpu.VMEM((3,) + w_flat.shape, jnp.float32), dma((32,)), dma((32,)), dma((3,)), dma((3,))],
-        compiler_params=pltpu.CompilerParams(vmem_limit_bytes=VMEM_LIMIT),
-        name="finish",
-    )(w_full, w_flat, m_flat, v_flat, stat)
-
-
 def solution(mesh):
     n_stage = mesh.shape["stage"]
     n_data = mesh.shape["data"]
@@ -665,11 +615,10 @@
         w_new, m_new, v_new, stat, w_full = tail(
             grads, early, wm_loc.reshape(2, 576, 128), m_loc.reshape(2, 576, 128), v_loc.reshape(2, 576, 128),
             loss_tile, tau_clip, learn_rate)
-        w1_new, w2_new, w_new, m_new, v_new, loss = finish(w_full, w_new, m_new, v_new, stat)
-        w1_new = w1_new.reshape(2, d_model // 8, d_ff // 128, 8, 128).transpose(0, 1, 3, 2, 4).reshape(1, 2, 1, d_model, d_ff)
-        w2_new = w2_new.reshape(2, d_ff // 8, d_model // 128, 8, 128).transpose(0, 1, 3, 2, 4).reshape(1, 2, 1, d_ff, d_model)
+        w1_new = w_full[:, :2].reshape(2, d_model // 8, d_ff // 128, 8, 128).transpose(0, 1, 3, 2, 4).reshape(1, 2, 1, d_model, d_ff)
+        w2_new = w_full[:, 2:].reshape(2, d_ff // 8, d_model // 128, 8, 128).transpose(0, 1, 3, 2, 4).reshape(1, 2, 1, d_ff, d_model)
         flat_dims = (1, 2, 1, -1)
-        return w1_new, w2_new, w_new.reshape(flat_dims), m_new.reshape(flat_dims), v_new.reshape(flat_dims), loss.reshape(()) / n_tokens
+        return w1_new, w2_new, w_new.reshape(flat_dims), m_new.reshape(flat_dims), v_new.reshape(flat_dims), stat.reshape(()) / n_tokens
 
     act_spec = P(None, "data", None)
     flat_spec = P("stage", None, None, "data")

time: 310 us -> 302 us (0.974)
  Pallas kernels: 307 us -> 290 us
  local copies, waits for them, and re-layouts: 0 us -> 9.56 us
    pallas_call x1 -> x0, Pallas kernels: 15.9 us -> none  [finish(): pl.pallas_call(finish_kernel, out_shape=(half, half, flat, flat, flat, ja...]
    slice x0 -> x1, local copies, waits for them, and re-layouts: none -> 7.12 us  [device_step(): w_full[:, 2:].reshape(2, d_ff // 8, d_model // 128, 8, 128)]
where the time goes in v6:
time: 302 us
  Pallas kernels  290 us (96%)
  local copies, waits for them, and re-layouts  9.56 us (3%)
    pallas_call x1, Pallas kernels, tail(): pl.pallas_call(functools.partial(tail_kernel, tau_clip, learn_rate), out_...  222 us
    pallas_call x1, Pallas kernels, stack(): pl.pallas_call(functools.partial(stack_kernel, n_tokens), out_shape=(jax....  68 us
    slice x1, local copies, waits for them, and re-layouts, device_step(): w_full[:, 2:].reshape(2, d_ff // 8, d_model // 128, 8, 128)  7.12 us

profile of v6, /device:TPU:0, one launch (start us, length us, event | category | flops | bytes accessed | tf_op | source)
XLA Modules:
  0.0 302.1 jit_solution(11981965349379595387)
XLA Ops:
  0.6 68.0 %stack.1 = (f32[2,4,4,4,72,8,128]{6,5,4,3,2,1,0:T(8,128)}, f32[6,4,4,12,8,128]{5,4,3,2,1,0:T(8,128)}, f32[8,128]{1,0:T(8,128)}) custom-call(bf16[512,768]{1,0:T(8,128)(2,1)} %bitcast.28, bf16[512,768]{1,0:T(8,128)(2,1)} %bitcast.29, bf16[2,768,3072]{2,1,0:T(8,128)(2,1)} %bitcast.24, bf16[2,3072,768]{2,1,0:T(8,128)(2,1)} %bitcast.25), custom_call_target="tpu_custom_call" | custom-call | tf_op jit(solution)/shard_map/stack/pallas_call | solution.py:583
  68.7 222.0 %tail.1 = (f32[2,576,128]{2,1,0:T(8,128)S(1)}, f32[2,576,128]{2,1,0:T(8,128)S(1)}, f32[2,576,128]{2,1,0:T(8,128)S(1)}, f32[1]{0:T(128)}, bf16[2,4,4,4,72,8,128]{6,5,4,3,2,1,0:T(8,128)(2,1)S(1)}) custom-call(f32[2,4,4,4,72,8,128]{6,5,4,3,2,1,0:T(8,128)} %get-tuple-element.14.g_ref, f32[6,4,4,12,8,128]{5,4,3,2,1,0:T(8,128)} %get-tuple-element.15.early_ref, ...), custom_call_target="tpu_custom_call" | custom-call | tf_op jit(solution)/shard_map/tail/pallas_call | solution.py:306
  291.4 0.8 copy.19
  292.2 7.1 %fusion = (bf16[2,2,4,4,72,8,128]{6,5,4,3,2,1,0:T(8,128)(2,1)}, bf16[2,2,4,4,72,8,128]{6,5,4,3,2,1,0:T(8,128)(2,1)}) fusion(bf16[2,4,4,4,72,8,128]{6,5,4,3,2,1,0:T(8,128)(2,1)S(1)} %get-tuple-element.17), kind=kLoop, calls=%fused_computation | loop fusion | bytes 37748736 | tf_op jit(solution)/shard_map/slice | solution.py:619
  299.3 0.8 copy.20
  300.2 0.8 copy.21

commit v7 on v6

--- a/solution.py
+++ b/solution.py
@@ -115,16 +115,17 @@
     state_in = [pltpu.make_async_copy(src, dst, in_sem.at[j]) for j, (src, dst) in enumerate(((w_ref, w_out), (m_ref, m_out), (v_ref, v_out)))]
     all_st = range(len(STREAMS))
     early, late = all_st[:EARLY], all_st[EARLY:]
-    for i in range(4):
+    for st in early:
+        first_load(st, 0).start()
+    for i in range(2):
+        for st in late:
+            first_send(st, i).start()
+    for st in all_st:
+        for n in range(2):
+            fetch(st, n).start()
+    for i in range(1, 4):
         for st in early:
             first_load(st, i).start()
-        for st in late:
-            first_send(st, i).start()
-        if i == 0:
-            for st in all_st:
-                for n in range(2):
-                    fetch(st, n).start()
-
     for copy in state_in:
         copy.start()
 
@@ -139,33 +140,55 @@
         if more:
             fetch(st, n + 2).start()
 
-    for step in range(2):
-        def phase1(i, carry):
-            for st in all_st:
-                accumulate(st, step, i, True)
-                forward1(st, step, i).start()
-            return carry
-
-        lax.fori_loop(0, 4, phase1, 0)
-    for i in range(4):
-        for st in all_st:
+    def pass_on(group, step, i):
+        for st in group:
+            accumulate(st, step, i, True)
+            forward1(st, step, i).start()
+
+    def last_step(group, i):
+        for st in group:
             accumulate(st, 2, i, i < 2)
             if i == 0:
                 send2(st, 0).start()
         if i > 0:
-            for st in all_st:
+            for st in group:
                 send2(st, i - 1).wait_recv()
                 recv2[st, i - 1] = recv2[st, i - 1] + recv1[st, 2, i]
                 if i < 3:
                     send2(st, i).start()
                 else:
                     send3(st, 0).start()
-    for step in range(3):
-        for st in all_st:
+
+    def last_ring(group, step):
+        for st in group:
             send3(st, step).wait_recv()
             recv3[st, step] = recv3[st, step] + recv2[st, 2, back_of(st, 2, 2 + step)]
             if step < 2:
                 send3(st, step + 1).start()
+
+    def lead(i, carry):
+        pass_on(early, 0, i)
+        return carry
+
+    def both(i, carry):
+        pass_on(early, 1, i)
+        pass_on(late, 0, i)
+        return carry
+
+    lax.fori_loop(0, 4, lead, 0)
+    for i in range(2, 4):
+        for st in late:
+            first_send(st, i).start()
+    lax.fori_loop(0, 4, both, 0)
+    for i in range(4):
+        last_step(early, i)
+        pass_on(late, 1, i)
+    for i in range(4):
+        if i < 3:
+            last_ring(early, i)
+        last_step(late, i)
+    for step in range(3):
+        last_ring(late, step)
 
     for copy in state_in:
         copy.wait()

time: 302 us -> 308 us (1.020)
  Pallas kernels: 290 us -> 296 us
    pallas_call x1, Pallas kernels: 222 us -> 228 us  [tail(): pl.pallas_call(functools.partial(tail_kernel, tau_clip, learn_rate), out_...]
where the time goes in v7:
time: 308 us
  Pallas kernels  296 us (96%)
  local copies, waits for them, and re-layouts  9.56 us (3%)
    pallas_call x1, Pallas kernels, tail(): pl.pallas_call(functools.partial(tail_kernel, tau_clip, learn_rate), out_...  228 us
    pallas_call x1, Pallas kernels, stack(): pl.pallas_call(functools.partial(stack_kernel, n_tokens), out_shape=(jax....  68 us
    slice x1, local copies, waits for them, and re-layouts, device_step(): w_full[:, 2:].reshape(2, d_ff // 8, d_model // 128, 8, 128)  7.12 us

profile of v7, /device:TPU:0, one launch (start us, length us, event | category | flops | bytes accessed | tf_op | source)
XLA Modules:
  0.0 308.0 jit_solution(6457887670080896024)
XLA Ops:
  0.6 68.0 %stack.1 = (f32[2,4,4,4,72,8,128]{6,5,4,3,2,1,0:T(8,128)}, f32[6,4,4,12,8,128]{5,4,3,2,1,0:T(8,128)}, f32[8,128]{1,0:T(8,128)}) custom-call(bf16[512,768]{1,0:T(8,128)(2,1)} %bitcast.28, bf16[512,768]{1,0:T(8,128)(2,1)} %bitcast.29, bf16[2,768,3072]{2,1,0:T(8,128)(2,1)} %bitcast.24, bf16[2,3072,768]{2,1,0:T(8,128)(2,1)} %bitcast.25), custom_call_target="tpu_custom_call" | custom-call | tf_op jit(solution)/shard_map/stack/pallas_call | solution.py:606
  68.7 227.9 %tail.1 = (f32[2,576,128]{2,1,0:T(8,128)S(1)}, f32[2,576,128]{2,1,0:T(8,128)S(1)}, f32[2,576,128]{2,1,0:T(8,128)S(1)}, f32[1]{0:T(128)}, bf16[2,4,4,4,72,8,128]{6,5,4,3,2,1,0:T(8,128)(2,1)S(1)}) custom-call(f32[2,4,4,4,72,8,128]{6,5,4,3,2,1,0:T(8,128)} %get-tuple-element.14.g_ref, f32[6,4,4,12,8,128]{5,4,3,2,1,0:T(8,128)} %get-tuple-element.15.early_ref, ...), custom_call_target="tpu_custom_call" | custom-call | tf_op jit(solution)/shard_map/tail/pallas_call | solution.py:329
  297.3 0.8 copy.19
  298.1 7.1 %fusion = (bf16[2,2,4,4,72,8,128]{6,5,4,3,2,1,0:T(8,128)(2,1)}, bf16[2,2,4,4,72,8,128]{6,5,4,3,2,1,0:T(8,128)(2,1)}) fusion(bf16[2,4,4,4,72,8,128]{6,5,4,3,2,1,0:T(8,128)(2,1)S(1)} %get-tuple-element.17), kind=kLoop, calls=%fused_computation | loop fusion | bytes 37748736 | tf_op jit(solution)/shard_map/slice | solution.py:642
  305.2 0.8 copy.20
  306.0 0.8 copy.21

commit v8 on v6

--- a/solution.py
+++ b/solution.py
@@ -61,7 +61,7 @@
 
 
 def tail_kernel(tau_clip, learn_rate, g_ref, early_ref, w_ref, m_ref, v_ref, loss_ref,
-                w_out, m_out, v_out, stat_out, full_out,
+                state, stat_out, full_out,
                 recv1, recv2, recv3, local, nbuf,
                 s1, r1, s2, r2, s3, r3, l_sem, e_sem, ns, nr, in_sem,
                 t1, q1, t2, q2, t3, q3):
@@ -79,7 +79,6 @@
     for phase, size in enumerate(sizes):
         for delta in range(1, size):
             pl.semaphore_signal(barrier, inc=1, device_id=friend(phase, delta), device_id_type=MESH_ID)
-    pl.semaphore_wait(barrier, sum(sizes) - len(sizes))
 
     def next_of(st, phase):
         h, k, d = STREAMS[st]
@@ -112,19 +111,20 @@
         src = recv2.at[st, 2, back_of(st, 2, 1)] if step == 0 else recv3.at[st, step - 1]
         return remote(src, recv3.at[st, step], s3.at[st, step], r3.at[st, step], next_of(st, 2))
 
-    state_in = [pltpu.make_async_copy(src, dst, in_sem.at[j]) for j, (src, dst) in enumerate(((w_ref, w_out), (m_ref, m_out), (v_ref, v_out)))]
+    state_in = [pltpu.make_async_copy(src, state.at[j], in_sem.at[j]) for j, src in enumerate((w_ref, m_ref, v_ref))]
     all_st = range(len(STREAMS))
     early, late = all_st[:EARLY], all_st[EARLY:]
     for i in range(4):
         for st in early:
             first_load(st, i).start()
-        for st in late:
-            first_send(st, i).start()
         if i == 0:
             for st in all_st:
                 for n in range(2):
                     fetch(st, n).start()
-
+    pl.semaphore_wait(barrier, sum(sizes) - len(sizes))
+    for i in range(4):
+        for st in late:
+            first_send(st, i).start()
     for copy in state_in:
         copy.start()
 
@@ -175,6 +175,7 @@
         total = total + jnp.sum(piece * piece, axis=0)
 
     parts = (total, loss_ref[...])
+    pending = []
     for phase, size in enumerate(sizes):
         mine = (stage * 4 + coords[2], coords[0] * 4 + coords[1])[phase]
         nbuf[phase, mine, 0], nbuf[phase, mine, 1] = parts
@@ -184,8 +185,7 @@
         for send in sends:
             send.wait_recv()
         parts = tuple(sum((nbuf[phase, slot, j] for slot in range(1, size)), nbuf[phase, 0, j]) for j in range(2))
-        for send in sends:
-            send.wait_send()
+        pending += sends
 
     stat_out[0] = jnp.sum(parts[1])
     norm = jnp.sqrt(jnp.full((8, 128), jnp.sum(parts[0]), jnp.float32))
@@ -197,15 +197,15 @@
                 for t in range(PART):
                     rows = pl.ds(k * 192 + (t // width) * (8 * width) + t % width, 8, stride=width)
                     grad = clip * recv3[(1 - h) * EARLY + 2 * k + t // HALF_PART, 2, t % HALF_PART]
-                    m_new = BETA_ONE * m_out[h, rows, :] + (1.0 - BETA_ONE) * grad
-                    v_new = BETA_TWO * v_out[h, rows, :] + (1.0 - BETA_TWO) * grad * grad
+                    m_new = BETA_ONE * state[1, h, rows, :] + (1.0 - BETA_ONE) * grad
+                    v_new = BETA_TWO * state[2, h, rows, :] + (1.0 - BETA_TWO) * grad * grad
                     m_hat = m_new * (1.0 / (1.0 - BETA_ONE ** ADAM_STEP))
                     v_hat = v_new * (1.0 / (1.0 - BETA_TWO ** ADAM_STEP))
-                    w_old = w_out[h, rows, :]
+                    w_old = state[0, h, rows, :]
                     w_new = w_old - learn_rate * (m_hat / (jnp.sqrt(v_hat) + ADAM_EPS) + WEIGHT_DECAY * w_old)
-                    w_out[h, rows, :] = w_new
-                    m_out[h, rows, :] = m_new
-                    v_out[h, rows, :] = v_new
+                    state[0, h, rows, :] = w_new
+                    state[1, h, rows, :] = m_new
+                    state[2, h, rows, :] = v_new
                     full_out[(h,) + coords + (k * PART + t,)] = w_new.astype(jnp.bfloat16)
             return carry
 
@@ -283,6 +283,8 @@
         return carry
 
     lax.fori_loop(0, 4, drain, 0)
+    for send in pending:
+        send.wait_send()
     for step in range(3):
         for st in all_st:
             send2(st, step).wait_send()
@@ -294,7 +296,7 @@
 
 def tail(grads, early, w_flat, m_flat, v_flat, loss_tile, tau_clip, learn_rate):
     f32, bf16 = jnp.float32, jnp.bfloat16
-    flat = pltpu.VMEM(w_flat.shape, f32)
+    flat = pltpu.VMEM((3,) + w_flat.shape, f32)
     in_vmem = pl.BlockSpec(memory_space=pltpu.VMEM)
     in_any = pl.BlockSpec(memory_space=pl.ANY)
     dma = pltpu.SemaphoreType.DMA
@@ -305,9 +307,9 @@
     per_place = (6, 3)
     return pl.pallas_call(
         functools.partial(tail_kernel, tau_clip, learn_rate),
-        out_shape=(flat, flat, flat, jax.ShapeDtypeStruct((1,), f32), pltpu.VMEM(grads.shape, bf16)),
+        out_shape=(flat, jax.ShapeDtypeStruct((1,), f32), pltpu.VMEM(grads.shape, bf16)),
         in_specs=[in_any] * 5 + [in_vmem],
-        out_specs=(in_vmem, in_vmem, in_vmem, pl.BlockSpec(memory_space=pltpu.SMEM), in_vmem),
+        out_specs=(in_vmem, pl.BlockSpec(memory_space=pltpu.SMEM), in_vmem),
         scratch_shapes=[
             pltpu.VMEM(per_sub + (4,) + part, f32),
             pltpu.VMEM(per_sub + part, f32),
@@ -612,13 +614,13 @@
         x_all = x_loc.reshape(n_micro * n_tok, d_model)
         t_all = t_loc.reshape(n_micro * n_tok, d_model)
         grads, early, loss_tile = stack(x_all, t_all, w1_loc[0, :, 0], w2_loc[0, :, 0], n_tokens)
-        w_new, m_new, v_new, stat, w_full = tail(
+        state, stat, w_full = tail(
             grads, early, wm_loc.reshape(2, 576, 128), m_loc.reshape(2, 576, 128), v_loc.reshape(2, 576, 128),
             loss_tile, tau_clip, learn_rate)
         w1_new = w_full[:, :2].reshape(2, d_model // 8, d_ff // 128, 8, 128).transpose(0, 1, 3, 2, 4).reshape(1, 2, 1, d_model, d_ff)
         w2_new = w_full[:, 2:].reshape(2, d_ff // 8, d_model // 128, 8, 128).transpose(0, 1, 3, 2, 4).reshape(1, 2, 1, d_ff, d_model)
         flat_dims = (1, 2, 1, -1)
-        return w1_new, w2_new, w_new.reshape(flat_dims), m_new.reshape(flat_dims), v_new.reshape(flat_dims), stat.reshape(()) / n_tokens
+        return w1_new, w2_new, *(state[j].reshape(flat_dims) for j in range(3)), stat.reshape(()) / n_tokens
 
     act_spec = P(None, "data", None)
     flat_spec = P("stage", None, None, "data")

time: 302 us -> 301 us (level)
  no operation moved by 1% of the time
where the time goes in v8:
time: 301 us
  Pallas kernels  290 us (96%)
  local copies, waits for them, and re-layouts  8.38 us (3%)
    pallas_call x1, Pallas kernels, tail(): pl.pallas_call(functools.partial(tail_kernel, tau_clip, learn_rate), out_...  222 us
    pallas_call x1, Pallas kernels, stack(): pl.pallas_call(functools.partial(stack_kernel, n_tokens), out_shape=(jax....  68 us
    slice x1, local copies, waits for them, and re-layouts, device_step(): w_full[:, 2:].reshape(2, d_ff // 8, d_model // 128, 8, 128)  7.14 us

profile of v8, /device:TPU:0, one launch (start us, length us, event | category | flops | bytes accessed | tf_op | source)
XLA Modules:
  0.0 300.8 jit_solution(4648867105669458512)
XLA Ops:
  0.6 68.0 %stack.1 = (f32[2,4,4,4,72,8,128]{6,5,4,3,2,1,0:T(8,128)}, f32[6,4,4,12,8,128]{5,4,3,2,1,0:T(8,128)}, f32[8,128]{1,0:T(8,128)}) custom-call(bf16[512,768]{1,0:T(8,128)(2,1)} %bitcast.25, bf16[512,768]{1,0:T(8,128)(2,1)} %bitcast.26, bf16[2,768,3072]{2,1,0:T(8,128)(2,1)} %bitcast.21, bf16[2,3072,768]{2,1,0:T(8,128)(2,1)} %bitcast.22), custom_call_target="tpu_custom_call" | custom-call | tf_op jit(solution)/shard_map/stack/pallas_call | solution.py:585
  68.7 222.0 %tail.1 = (f32[3,2,576,128]{3,2,1,0:T(8,128)S(1)}, f32[1]{0:T(128)}, bf16[2,4,4,4,72,8,128]{6,5,4,3,2,1,0:T(8,128)(2,1)S(1)}) custom-call(f32[2,4,4,4,72,8,128]{6,5,4,3,2,1,0:T(8,128)} %get-tuple-element.12.g_ref, f32[6,4,4,12,8,128]{5,4,3,2,1,0:T(8,128)} %get-tuple-element.13.early_ref, f32[2,576,128]{2,1,0:T(8,128)} %bitcast.30, f32[2,576,128]{2,1,0:T(8,128)} %bitcast.31, ...), custom_call_target="tpu_custom_call" | custom-call | tf_op jit(solution)/shard_map/tail/pallas_call | solution.py:308
  291.3 7.1 %fusion = (bf16[2,2,4,4,72,8,128]{6,5,4,3,2,1,0:T(8,128)(2,1)}, bf16[2,2,4,4,72,8,128]{6,5,4,3,2,1,0:T(8,128)(2,1)}) fusion(bf16[2,4,4,4,72,8,128]{6,5,4,3,2,1,0:T(8,128)(2,1)S(1)} %get-tuple-element.15), kind=kLoop, calls=%fused_computation | loop fusion | bytes 37748736 | tf_op jit(solution)/shard_map/slice | solution.py:621
  298.4 1.2 fusion.1
